TPU v7x, 32 devices: a whole 2x2x4 slice. The times are simulated.
32 devices in a mesh: dp: 8 (over z, core), expert: 4 (over y, x).
Axes of the slice: x: 2, y: 2, z: 4, core: 2. Of those that a mesh axis runs over, the one named last changes fastest.
Arguments:
- mamba_in: bfloat16 [8, 256, 4096], P('dp'), may hold values from -6 to 6
- conv_state: bfloat16 [8, 3, 8192], P('dp', None, 'expert'), may hold values from -6 to 6
- in_weight: bfloat16 [4096, 8192], P('dp', 'expert'), may hold values from -0.09375 to 0.09375
- conv_kernel: float32 [4, 8192], P(None, 'expert'), may hold values from -3 to 3
- conv_bias: float32 [8192], P('expert'), may hold values from -1 to 1
- moe_in: bfloat16 [512, 4096], P('expert'), may hold values from -6 to 6
- router: bfloat16 [4096, 4], replicated, may hold values from -0.09375 to 0.09375
- expert_ids: int32 [512, 2], P('expert'), may hold values from 0 to 3, all different within a row; in each aligned block of 128 rows (0 to 127, 128 to 255, ...) at most 128 rows name the same one
- w_gate: bfloat16 [4, 4096, 12288], P('expert', None, 'dp'), may hold values from -0.09375 to 0.09375
- w_up: bfloat16 [4, 4096, 12288], P('expert', None, 'dp'), may hold values from -0.09375 to 0.09375
- w_down: bfloat16 [4, 12288, 4096], P('expert', 'dp'), may hold values from -0.078125 to 0.078125
Outputs:
- conv_out: bfloat16 [8, 256, 8192], P('dp', None, 'expert')
- moe_out: bfloat16 [512, 4096], P('expert', 'dp')
Inputs may be any that keep to these rules, and one draw needn't show every extreme that they name: `expert_ids`: each row names two different experts; among the 128 rows of one index of expert no expert is named more than 128 times, a bound that some block reaches.
All inputs are finite; a program needn't handle non-finite values.
Results may differ from a plain program's by a relative error of at most 0.0049.
Values may be sent and summed in bfloat16 or wider, within the bound.
No kernel may reach another device: no remote copies, remote signals or barrier semaphores. Data moves between devices by JAX's collectives and lax.ppermute only.
A program may use at most 192 MiB of HBM per device.

v0:
```python
import jax
import jax.numpy as jnp
from jax import lax
from jax.sharding import PartitionSpec as P


def expert_ffn(inputs, gate_mat, up_mat, down_mat):
    gate_val = jnp.dot(inputs, gate_mat, preferred_element_type=jnp.float32)
    up_val = jnp.dot(inputs, up_mat, preferred_element_type=jnp.float32)
    hidden = (jax.nn.silu(gate_val) * up_val).astype(jnp.bfloat16)
    return jnp.dot(hidden, down_mat, preferred_element_type=jnp.float32)


def body(
    mamba_in,
    conv_state,
    in_weight,
    conv_kernel,
    conv_bias,
    moe_in,
    router,
    expert_ids,
    w_gate,
    w_up,
    w_down,
):
    token_count = mamba_in.shape[1]
    width = mamba_in.shape[2]
    window = mamba_in.reshape(token_count, width)
    channels = in_weight.shape[1]
    taps = conv_kernel.shape[0]
    summed_proj = jnp.dot(
        window,
        lax.all_gather(in_weight, "dp", axis=0, tiled=True),
        preferred_element_type=jnp.float32,
    )
    projected = summed_proj.astype(jnp.bfloat16)
    extended = jnp.concatenate([conv_state[0], projected], axis=0)
    summed = jnp.zeros((token_count, channels), jnp.float32) + conv_bias[None, :]
    for offset in range(taps):
        summed = (
            summed
            + extended[offset : offset + token_count].astype(jnp.float32)
            * conv_kernel[offset][None, :]
        )
    conv_out = jax.nn.silu(summed).astype(jnp.bfloat16).reshape(1, token_count, channels)
    moe_rows = moe_in.shape[0]
    experts = lax.axis_size("expert") * w_gate.shape[0]
    capacity = min(moe_rows, 4 * moe_rows // experts)
    expert_range = jnp.arange(experts, dtype=jnp.int32)
    onehot_ids = (expert_ids.reshape(-1)[:, None] == expert_range[None, :]).astype(jnp.int32)
    earlier = jnp.cumsum(onehot_ids, axis=0) - onehot_ids
    slots = jnp.sum(earlier * onehot_ids, axis=1).reshape(moe_rows, 2)
    targets = expert_ids * capacity + slots
    slot_range = jnp.arange(experts * capacity, dtype=jnp.int32)
    first_hit = targets[:, 0][None, :] == slot_range[:, None]
    second_hit = targets[:, 1][None, :] == slot_range[:, None]
    dispatch_table = jnp.logical_or(first_hit, second_hit).astype(jnp.bfloat16)
    send_buffer = jnp.dot(dispatch_table, moe_in, preferred_element_type=jnp.float32).astype(
        jnp.bfloat16
    )
    send_buffer = send_buffer.reshape(experts, capacity, width)
    logits = jnp.dot(moe_in, router, preferred_element_type=jnp.float32)
    chosen_mask = (expert_ids[:, :, None] == expert_range[None, None, :]).astype(jnp.float32)
    chosen = jnp.sum(logits[:, None, :] * chosen_mask, axis=2)
    first_weight = jax.nn.sigmoid(chosen[:, 0] - chosen[:, 1])
    combine_table = first_weight[:, None] * first_hit.T.astype(jnp.float32) + (1.0 - first_weight)[
        :, None
    ] * second_hit.T.astype(jnp.float32)
    received = lax.all_to_all(send_buffer, "expert", split_axis=0, concat_axis=0, tiled=True)
    flat_rows = received.reshape(-1, width)
    result = expert_ffn(flat_rows, w_gate[0], w_up[0], w_down[0])
    partials = result.reshape(received.shape[0], received.shape[1], width)
    shares = lax.psum_scatter(partials, "dp", scatter_dimension=2, tiled=True)
    returned = lax.all_to_all(shares, "expert", split_axis=0, concat_axis=0, tiled=True)
    flat_back = returned.reshape(experts * capacity, returned.shape[2])
    mixed = jnp.dot(
        combine_table,
        flat_back,
        precision=lax.Precision.HIGHEST,
        preferred_element_type=jnp.float32,
    )
    return (conv_out, mixed.astype(jnp.bfloat16))


def solution(mesh):
    in_specs = (
        P("dp", None, None),
        P("dp", None, "expert"),
        P("dp", "expert"),
        P(None, "expert"),
        P("expert"),
        P("expert", None),
        P(),
        P("expert", None),
        P("expert", None, "dp"),
        P("expert", None, "dp"),
        P("expert", "dp", None),
    )
    out_specs = (P("dp", None, "expert"), P("expert", "dp"))
    return jax.shard_map(body, mesh=mesh, in_specs=in_specs, out_specs=out_specs, check_vma=False)
```

profile of v0, /device:TPU:0, one launch (start us, length us, event | category | flops | bytes accessed | tf_op | source)
XLA Modules:
  0.0 353.5 jit_solution(8871153900584539604)
XLA Ops:
  7.2 0.0 copy-start
  7.2 0.0 reduce-scatter.2.cloned.1.call-start
  7.2 0.9 copy.39
  8.2 0.1 eq.86
  8.3 0.1 eq.82
  8.4 1.2 reduce-window.6
  9.7 0.1 slice.56
  9.7 0.1 copy.41
  9.9 0.1 copy.42
  10.0 0.1 add_bitcast_fusion
  10.1 0.1 reshape.49
  10.2 0.1 copy.43
  10.3 0.7 multiply_add_fusion
  11.0 0.0 copy-start.6
  11.0 2.6 convolution_convert_fusion
  13.6 0.0 slice-start
  13.6 53.1 %all_to_all.10 = bf16[4,128,4096]{2,1,0:T(8,128)(2,1)S(1)} all-to-all(bf16[4,128,4096]{2,1,0:T(8,128)(2,1)S(1)} %bitcast.62), channel_id=1, replica_groups=mesh['dp'=8,'expert'=4] {'expert'}, dimensions={0} | all-to-all | bytes 8388608 | tf_op jit(solution)/shard_map/all_to_all | solution.py:70
  66.7 0.0 copy-done.6
  66.7 0.0 slice-start.1
  66.7 0.0 slice-start.2
  66.7 8.3 %fusion.4 = f32[512,1536]{1,0:T(8,128)} fusion(bf16[512,4096]{1,0:T(8,128)(2,1)S(1)} %bitcast.63, bf16[1,4096,1536]{2,1,0:T(8,128)(2,1)S(1)} %copy-done.6), kind=kOutput, calls=%fused_computation.4 | convolution fusion | flops 6442450944 | bytes 19922944 | tf_op jit(solution)/shard_map/dot_general | solution.py:8
  75.0 0.0 slice-done
  75.0 0.0 slice-done.1
  75.0 0.0 slice-done.2
  75.0 8.5 %fusion.9 = bf16[512,1536]{1,0:T(8,128)(2,1)S(1)} fusion(bf16[512,4096]{1,0:T(8,128)(2,1)S(1)} %bitcast.64, bf16[1,4096,1536]{2,1,0:T(8,128)(2,1)S(1)} %bitcast.74, f32[512,1536]{1,0:T(8,128)} %fusion.4), kind=kOutput, calls=%fused_computation.8 | convolution fusion | flops 6447169536 | bytes 21495808 | tf_op jit(solution)/shard_map/dot_general | solution.py:9
  83.5 11.8 %fusion = f32[4,128,4096]{2,1,0:T(8,128)} fusion(bf16[4,128,1536]{2,1,0:T(8,128)(2,1)S(1)} %bitcast.75, bf16[1,1536,4096]{2,1,0:T(8,128)(2,1)} %param.21), kind=kOutput, calls=%fused_computation | convolution fusion | flops 6442450944 | bytes 22544384 | tf_op jit(solution)/shard_map/dot_general | solution.py:11
  95.3 0.0 reduce-scatter.2.cloned.1.call-update
  95.4 0.0 copy-start.1
  95.4 0.0 all-gather.2.cloned.1.call-start
  95.4 0.7 all-gather.2.cloned.1.call-update
  96.1 0.0 copy-start.4
  96.1 0.0 copy-start.2
  96.2 88.7 %reduce-scatter.2.cloned.1.call-done = f32[4,128,512]{2,1,0:T(8,128)} async-done(((f32[4,128,4096]{2,1,0:T(8,128)}), f32[4,128,512]{2,1,0:T(8,128)}) %reduce-scatter.2.cloned.1.call-update) | async-done | bytes 1048592 | tf_op jit(solution)/shard_map/reduce_scatter | solution.py:74
  184.8 3.7 %all-to-all-start.1 = ((f32[4,128,512]{2,1,0:T(8,128)}), f32[4,128,512]{2,1,0:T(8,128)S(1)}, u32[]{:S(2)}, u32[]{:S(2)}) async-start(f32[4,128,512]{2,1,0:T(8,128)} %reduce-scatter.2.cloned.1.call-done), calls=%async_computation.2 | async-start | bytes 2097152 | tf_op jit(solution)/shard_map/all_to_all | solution.py:75
  188.5 0.0 copy-done.1
  188.6 1.6 fusion.33
  190.2 0.0 copy-done.4
  190.2 0.0 copy-done.2
  190.2 9.9 %all-to-all-done.1 = f32[4,128,512]{2,1,0:T(8,128)S(1)} async-done(((f32[4,128,512]{2,1,0:T(8,128)}), f32[4,128,512]{2,1,0:T(8,128)S(1)}, u32[]{:S(2)}, u32[]{:S(2)}) %all-to-all-start.1) | async-done | bytes 1048608 | tf_op jit(solution)/shard_map/all_to_all | solution.py:75
  200.1 1.4 convolution_convert_fusion.2
  201.5 0.0 copy-start.3
  201.5 0.0 copy-start.5
  201.5 134.5 %all-gather.2.cloned.1.call-done = bf16[4096,2048]{1,0:T(8,128)(2,1)} async-done(((bf16[512,2048]{1,0:T(8,128)(2,1)}), bf16[4096,2048]{1,0:T(8,128)(2,1)}) %all-gather.2.cloned.1.call-update) | async-done | bytes 16777232 | tf_op jit(solution)/shard_map/all_gather | solution.py:34
  336.0 0.0 copy-done
  336.0 8.3 %convolution_convert_fusion.1 = bf16[256,2048]{1,0:T(8,128)(2,1)S(1)} fusion(bf16[4096,2048]{1,0:T(8,128)(2,1)} %all-gather.2.cloned.1.call-done, bf16[1,256,4096]{2,1,0:T(8,128)(2,1)S(1)} %copy-done), kind=kOutput, calls=%fused_computation.9 | convolution fusion | flops 4295491584 | bytes 19922944 | tf_op jit(solution)/shard_map/dot_general | solution.py:32
  344.3 0.0 copy-done.3
  344.3 0.0 copy-done.5
  344.3 2.3 fusion.15
  (9 shorter events, 0.1 us)
Async XLA Ops:
  7.2 328.8 %copy-start = (bf16[1,256,4096]{2,1,0:T(8,128)(2,1)S(1)}, bf16[1,256,4096]{2,1,0:T(8,128)(2,1)}, u32[]{:S(2)}) copy-start(bf16[1,256,4096]{2,1,0:T(8,128)(2,1)} %param.11) | copy-start | bytes 6291460
  7.2 177.7 %reduce-scatter.2.cloned.1.call-start = ((), (), s32[]{:S(2)}) async-start(), calls=%async_computation.4 | async-start | bytes 9437184 | tf_op jit(solution)/shard_map/reduce_scatter | solution.py:74
  11.0 55.7 %copy-start.6 = (bf16[1,4096,1536]{2,1,0:T(8,128)(2,1)S(1)}, bf16[1,4096,1536]{2,1,0:T(8,128)(2,1)}, u32[]{:S(2)}) copy-start(bf16[1,4096,1536]{2,1,0:T(8,128)(2,1)} %param.19) | copy-start | bytes 37748740
  13.6 61.4 %slice-start = ((s8[12582912]{0:T(1024)(128)(4,1)}), s8[4194304]{0:T(1024)(128)(4,1)S(1)}, s32[]{:S(2)}) async-start(s8[12582912]{0:T(1024)(128)(4,1)} %bitcast.73), calls=%async_computation.5 | async-start | bytes 8388608
  66.7 8.3 %slice-start.1 = ((s8[12582912]{0:T(1024)(128)(4,1)}), s8[4194304]{0:T(1024)(128)(4,1)S(1)}, s32[]{:S(2)}) async-start(s8[12582912]{0:T(1024)(128)(4,1)} %bitcast.73), calls=%async_computation.6 | async-start | bytes 8388608
  66.7 8.3 %slice-start.2 = ((s8[12582912]{0:T(1024)(128)(4,1)}), s8[4194304]{0:T(1024)(128)(4,1)S(1)}, s32[]{:S(2)}) async-start(s8[12582912]{0:T(1024)(128)(4,1)} %bitcast.73), calls=%async_computation.7 | async-start | bytes 8388608
  95.4 93.2 %copy-start.1 = (bf16[4096,4]{0,1:T(4,128)(2,1)S(1)}, bf16[4096,4]{0,1:T(4,128)(2,1)}, u32[]{:S(2)}) copy-start(bf16[4096,4]{0,1:T(4,128)(2,1)} %param.17) | copy-start | bytes 98308
  95.4 240.6 %all-gather.2.cloned.1.call-start = ((), (), s32[]{:S(2)}) async-start(), calls=%async_computation.3 | async-start | bytes 18874368 | tf_op jit(solution)/shard_map/all_gather | solution.py:34
  96.1 94.0 %copy-start.4 = (s32[128,2]{0,1:T(2,128)S(1)}, s32[128,2]{0,1:T(2,128)}, u32[]{:S(2)}) copy-start(s32[128,2]{0,1:T(2,128)} %param.18) | copy-start | bytes 3076
  96.1 94.1 %copy-start.2 = (f32[4,2048]{1,0:T(4,128)S(1)}, f32[4,2048]{1,0:T(4,128)}, u32[]{:S(2)}) copy-start(f32[4,2048]{1,0:T(4,128)} %param.14) | copy-start | bytes 98308
  184.8 15.3 %all-to-all-start.1 = ((f32[4,128,512]{2,1,0:T(8,128)}), f32[4,128,512]{2,1,0:T(8,128)S(1)}, u32[]{:S(2)}, u32[]{:S(2)}) async-start(f32[4,128,512]{2,1,0:T(8,128)} %reduce-scatter.2.cloned.1.call-done), calls=%async_computation.2 | async-start | bytes 2097152 | tf_op jit(solution)/shard_map/all_to_all | solution.py:75
  201.5 142.7 %copy-start.3 = (bf16[1,3,2048]{2,1,0:T(4,128)(2,1)S(1)}, bf16[1,3,2048]{2,1,0:T(4,128)(2,1)}, u32[]{:S(2)}) copy-start(bf16[1,3,2048]{2,1,0:T(4,128)(2,1)} %param.12) | copy-start | bytes 36868
  201.5 142.7 %copy-start.5 = (f32[2048]{0:T(1024)S(1)}, f32[2048]{0:T(1024)}, u32[]{:S(2)}) copy-start(f32[2048]{0:T(1024)} %param.15) | copy-start | bytes 24580
Sparse Core Ops, SparseCore 0:
  95.5 89.3 reduce-scatter.1
  186.4 149.5 all-gather.1
where the time goes:
time: 354 us; the launch traced here: 353 us
  waiting for transfers between devices  234 us (66%)
  blocking collectives  53.1 us (15%)
  matrix products  42.5 us (12%)
  between operations  14.2 us (4%)
  other arithmetic  4.44 us (1%)
  starting transfers between devices  3.77 us (1%)
    all_gather x1, waiting for transfers between devices, body(): lax.all_gather(in_weight, 'dp', axis=0, tiled=True)  134 us
    reduce_scatter x1, waiting for transfers between devices, body(): shares = lax.psum_scatter(partials, 'dp', scatter_dimension=2, tiled=True)  88.7 us
    all_to_all x1, blocking collectives, body(): lax.all_to_all(send_buffer, 'expert', split_axis=0, concat_axis=0, tiled=...  53.1 us
    dot_general x1, matrix products, expert_ffn(): return jnp.dot(hidden, down_mat, preferred_element_type=jnp.float32)  11.8 us
    all_to_all x1, waiting for transfers between devices, body(): lax.all_to_all(shares, 'expert', split_axis=0, concat_axis=0, tiled=True)  9.86 us
    dot_general x1, matrix products, expert_ffn(): up_val = jnp.dot(inputs, up_mat, preferred_element_type=jnp.float32)  8.53 us
    dot_general x1, matrix products, expert_ffn(): gate_val = jnp.dot(inputs, gate_mat, preferred_element_type=jnp.float32)  8.28 us
    dot_general x1, matrix products, body(): jnp.dot(window, lax.all_gather(in_weight, 'dp', axis=0, tiled=True), pref...  8.25 us
  transfers between devices with their start and end apart: 3, of which 3 were waited for; matrix products, arithmetic and copies ran while one was open for 1% of the time, Pallas kernels for 0%

commit v1 on v0

v1 whole, which is shorter than its diff:
```python
import jax
import jax.numpy as jnp
from jax import lax
from jax.sharding import PartitionSpec as P

F32 = jnp.float32
BF16 = jnp.bfloat16


def xor_send(value, axis, mask):
    pairs = [(i, i ^ mask) for i in range(lax.axis_size(axis))]
    return lax.ppermute(value, axis, pairs)


def body(
    mamba_in,
    conv_state,
    in_weight,
    conv_kernel,
    conv_bias,
    moe_in,
    router,
    expert_ids,
    w_gate,
    w_up,
    w_down,
):
    tokens, width = mamba_in.shape[1:]
    depth, channels = in_weight.shape
    taps = conv_kernel.shape[0]
    dp = lax.axis_size("dp")
    owners = lax.axis_size("expert")
    half = dp // 2
    me = lax.axis_index("dp")
    mine = lax.axis_index("expert")
    core = me % 2
    side = me // half
    local = me % half

    moe_rows = moe_in.shape[0]
    split = width // 2
    part = lax.dynamic_slice(moe_in, (0, core * split), (moe_rows, split))
    blocks = [moe_in]
    for mask in range(1, owners):
        got = xor_send(part, "expert", mask)
        other = xor_send(got, "dp", 1)
        first = jnp.where(core == 0, got, other)
        second = jnp.where(core == 0, other, got)
        blocks.append(jnp.concatenate([first, second], axis=1))

    window = mamba_in[0]
    features = width // 2
    share = tokens // owners
    piece = lax.dynamic_slice(window, (mine * share, (1 - side) * features), (share, features))
    piece = xor_send(piece, "dp", half)
    pieces = [piece] + [xor_send(piece, "expert", mask) for mask in range(1, owners)]
    far = jnp.zeros((tokens, features), BF16)
    for mask, block in enumerate(pieces):
        far = lax.dynamic_update_slice(far, block, ((mine ^ mask) * share, 0))
    near = lax.dynamic_slice(window, (0, side * features), (tokens, features))
    both = jnp.concatenate([near, far], axis=0)
    operands = [
        lax.dynamic_slice(both, (0, (local ^ mask) * depth), (2 * tokens, depth))
        for mask in range(half)
    ]

    chunks = 4
    cols = channels // chunks
    outs = []
    for chunk in range(chunks):
        own = in_weight[:, chunk * cols : (chunk + 1) * cols]
        total = None
        for mask in range(0, half, 2):
            even = own if mask == 0 else xor_send(own, "dp", mask)
            odd = xor_send(even, "dp", 1)
            for offset, weight in enumerate((even, odd)):
                term = jnp.dot(operands[mask + offset], weight, preferred_element_type=F32)
                total = term if total is None else total + term
        back = xor_send(total[tokens:].astype(BF16), "dp", half)
        projected = (total[:tokens] + back.astype(F32)).astype(BF16)
        lanes = slice(chunk * cols, (chunk + 1) * cols)
        extended = jnp.concatenate([conv_state[0][:, lanes], projected], axis=0)
        summed = jnp.zeros((tokens, cols), F32) + conv_bias[None, lanes]
        for tap in range(taps):
            summed = (
                summed
                + extended[tap : tap + tokens].astype(F32) * conv_kernel[tap][None, lanes]
            )
        outs.append(jax.nn.silu(summed).astype(BF16))
    conv_out = jnp.concatenate(outs, axis=1)[None]

    logits = jnp.dot(moe_in, router, preferred_element_type=F32)
    hits = expert_ids[:, :, None] == jnp.arange(router.shape[1], dtype=jnp.int32)[None, None, :]
    chosen = jnp.sum(jnp.where(hits, logits[:, None, :], 0.0), axis=2)
    first_weight = jax.nn.sigmoid(chosen[:, 0] - chosen[:, 1])
    pair = jnp.stack([first_weight, 1.0 - first_weight], axis=1)
    table = jnp.sum(jnp.where(hits, pair[:, :, None], 0.0), axis=1).T
    scales = []
    for mask in range(owners):
        row = lax.dynamic_slice(table, (mine ^ mask, 0), (1, moe_rows))
        scales.append(row if mask == 0 else xor_send(row, "expert", mask))
    scale = jnp.concatenate(scales, axis=1).reshape(-1, 1)

    rows = jnp.concatenate(blocks, axis=0)
    gate = jnp.dot(rows, w_gate[0], preferred_element_type=F32)
    up = jnp.dot(rows, w_up[0], preferred_element_type=F32)
    hidden = (jax.nn.silu(gate) * up).astype(BF16)
    result = jnp.dot(hidden, w_down[0], preferred_element_type=F32) * scale

    final = width // dp
    result = result.reshape(-1, half, 2, final)
    send = lax.dynamic_index_in_dim(result, 1 - core, 2, keepdims=False)
    keep = lax.dynamic_index_in_dim(result, core, 2, keepdims=False)
    keep = keep + xor_send(send, "dp", 1)
    keep = keep.reshape(owners, moe_rows, half, final)
    mixed = keep[0]
    for mask in range(1, owners):
        mixed = mixed + xor_send(keep[mask].astype(BF16), "expert", mask).astype(F32)
    place = me // 2
    answer = lax.dynamic_index_in_dim(mixed, place, 1, keepdims=False)
    for mask in range(1, half):
        share_out = lax.dynamic_index_in_dim(mixed, place ^ mask, 1, keepdims=False)
        answer = answer + xor_send(share_out.astype(BF16), "dp", 2 * mask).astype(F32)
    return conv_out, answer.astype(BF16)


def solution(mesh):
    in_specs = (
        P("dp", None, None),
        P("dp", None, "expert"),
        P("dp", "expert"),
        P(None, "expert"),
        P("expert"),
        P("expert", None),
        P(),
        P("expert", None),
        P("expert", None, "dp"),
        P("expert", None, "dp"),
        P("expert", "dp", None),
    )
    out_specs = (P("dp", None, "expert"), P("expert", "dp"))
    return jax.shard_map(body, mesh=mesh, in_specs=in_specs, out_specs=out_specs, check_vma=False)
```

time: 354 us -> 247 us (0.70)
  waiting for transfers between devices: 234 us -> 110 us
  blocking collectives: 53.1 us -> 0 us
  starting transfers between devices: 3.77 us -> 36.9 us
  local copies, waits for them, and re-layouts: 1.77 us -> 32.6 us
  matrix products: 42.5 us -> 55.8 us
  between operations: 14.2 us -> 1.69 us
  other arithmetic: 4.44 us -> 9.2 us
    all_gather x1 -> x0, waiting for transfers between devices: 134 us -> none  [body(): lax.all_gather(in_weight, 'dp', axis=0, tiled=True)]
    ppermute x0 -> x36, waiting for transfers between devices: none -> 110 us  [xor_send(): return lax.ppermute(value, axis, pairs)]
    reduce_scatter x1 -> x0, waiting for transfers between devices: 88.7 us -> none  [body(): shares = lax.psum_scatter(partials, 'dp', scatter_dimension=2, tiled=True)]
    all_to_all x1 -> x0, blocking collectives: 53.1 us -> none  [body(): lax.all_to_all(send_buffer, 'expert', split_axis=0, concat_axis=0, tiled=...]
    ppermute x0 -> x36, starting transfers between devices: none -> 36.9 us  [xor_send(): return lax.ppermute(value, axis, pairs)]
    dynamic_slice x0 -> x6, local copies, waits for them, and re-layouts: none -> 15.4 us  [the longest x1 11.2 us: body(): keep = lax.dynamic_index_in_dim(result, core, 2, keepdims=False)]
    dot_general x7 -> x19, matrix products: 42.5 us -> 55.8 us  [the longest x1 26.3 us: body(): result = jnp.dot(hidden, w_down[0], preferred_element_type=F32) * scale]
    reshape x2 -> x1, local copies, waits for them, and re-layouts: 0.2 us -> 11.7 us  [body(): result = result.reshape(-1, half, 2, final)]
  transfers between devices with their start and end apart: 3 -> 36, of which waited for: 3 -> 14; matrix products, arithmetic and copies ran while one was open for 1% -> 38% of each run, Pallas kernels for 0% -> 0%
where the time goes in v1:
time: 247 us; the launch traced here: 246 us
  waiting for transfers between devices  110 us (45%)
  matrix products  55.8 us (23%)
  starting transfers between devices  36.9 us (15%)
  local copies, waits for them, and re-layouts  32.6 us (13%)
  other arithmetic  9.2 us (4%)
    ppermute x36, waiting for transfers between devices, xor_send(): return lax.ppermute(value, axis, pairs)  110 us
    ppermute x36, starting transfers between devices, xor_send(): return lax.ppermute(value, axis, pairs)  36.9 us
    dot_general x1, matrix products, body(): result = jnp.dot(hidden, w_down[0], preferred_element_type=F32) * scale  26.3 us
    dot_general x16, matrix products, body(): term = jnp.dot(operands[mask + offset], weight, preferred_element_type=F32)  19.5 us
    reshape x1, local copies, waits for them, and re-layouts, body(): result = result.reshape(-1, half, 2, final)  11.7 us
    dynamic_slice x1, local copies, waits for them, and re-layouts, body(): keep = lax.dynamic_index_in_dim(result, core, 2, keepdims=False)  11.2 us
    dot_general x1, matrix products, body(): gate = jnp.dot(rows, w_gate[0], preferred_element_type=F32)  8.43 us
  transfers between devices with their start and end apart: 36, of which 14 were waited for; matrix products, arithmetic and copies ran while one was open for 38% of the time, Pallas kernels for 0%

profile of v1, /device:TPU:0, one launch (start us, length us, event | category | flops | bytes accessed | tf_op | source)
XLA Modules:
  0.0 246.0 jit_solution(64744257908161116)
XLA Ops:
  0.7 2.0 constant_dynamic-slice_fusion.6
  2.7 2.9 %collective-permute-start.20 = (bf16[128,2048]{1,0:T(8,128)(2,1)}, bf16[128,2048]{1,0:T(8,128)(2,1)}, u32[]{:S(2)}, u32[]{:S(2)}) collective-permute-start(bf16[128,2048]{1,0:T(8,128)(2,1)} %constant_dynamic-slice_fusion.6), channel_id=1, source_target_pairs={{0,1},{1,0},{2,3},{3,2},{4,5},{5,4},{6,7},{7,6},{8,9},{9,8},{10,11... | collective-permute-start | bytes 1572872 | tf_op jit(solution)/shard_map/ppermute | solution.py:12
  5.7 1.6 fusion.64
  8.8 2.0 collective-permute-start.27
  10.8 1.4 collective-permute-start.28
  13.0 2.6 %collective-permute-start = (bf16[64,2048]{1,0:T(8,128)(2,1)}, bf16[64,2048]{1,0:T(8,128)(2,1)S(1)}, u32[]{:S(2)}, u32[]{:S(2)}) collective-permute-start(bf16[64,2048]{1,0:T(8,128)(2,1)} %dynamic-slice_bitcast_fusion.1), channel_id=1, source_target_pairs={{0,16},{4,20},{8,24},{12,28},{16,0},{20,4},{24,8},{28,12},{1,17},{... | collective-permute-start | bytes 786440 | tf_op jit(solution)/shard_map/ppermute | solution.py:12
  15.6 2.9 %fusion.52 = (bf16[512,512]{1,0:T(8,128)(2,1)}, bf16[512,512]{1,0:T(8,128)(2,1)}, bf16[512,512]{1,0:T(8,128)(2,1)}, bf16[512,512]{1,0:T(8,128)(2,1)}) fusion(bf16[512,2048]{1,0:T(8,128)(2,1)} %param.13), kind=kLoop, calls=%fused_computation.123 | loop fusion | bytes 4194304 | tf_op jit(solution)/shard_map/slice | solution.py:71
  20.5 1.6 collective-permute-start.22
  22.6 4.1 %collective-permute-done = bf16[64,2048]{1,0:T(8,128)(2,1)S(1)} collective-permute-done((bf16[64,2048]{1,0:T(8,128)(2,1)}, bf16[64,2048]{1,0:T(8,128)(2,1)S(1)}, u32[]{:S(2)}, u32[]{:S(2)}) %collective-permute-start) | collective-permute-done | bytes 262176 | tf_op jit(solution)/shard_map/ppermute | solution.py:12
  27.2 1.6 collective-permute-start.2
  29.0 10.9 %collective-permute-done.1 = bf16[64,2048]{1,0:T(8,128)(2,1)S(1)} collective-permute-done((bf16[64,2048]{1,0:T(8,128)(2,1)S(1)}, bf16[64,2048]{1,0:T(8,128)(2,1)S(1)}, u32[]{:S(2)}, u32[]{:S(2)}) %collective-permute-start.1) | collective-permute-done | bytes 262176 | tf_op jit(solution)/shard_map/ppermute | solution.py:12
  39.9 1.6 collective-permute-start.3
  41.5 14.0 %collective-permute-done.2 = bf16[64,2048]{1,0:T(8,128)(2,1)S(1)} collective-permute-done((bf16[64,2048]{1,0:T(8,128)(2,1)S(1)}, bf16[64,2048]{1,0:T(8,128)(2,1)S(1)}, u32[]{:S(2)}, u32[]{:S(2)}) %collective-permute-start.2) | collective-permute-done | bytes 262176 | tf_op jit(solution)/shard_map/ppermute | solution.py:12
  55.5 1.6 collective-permute-start.5
  59.0 11.2 %collective-permute-done.5 = bf16[512,512]{1,0:T(8,128)(2,1)} collective-permute-done((bf16[512,512]{1,0:T(8,128)(2,1)}, bf16[512,512]{1,0:T(8,128)(2,1)}, u32[]{:S(2)}, u32[]{:S(2)}) %collective-permute-start.5) | collective-permute-done | bytes 524320 | tf_op jit(solution)/shard_map/ppermute | solution.py:12
  70.3 1.6 collective-permute-start.9
  71.8 1.6 fusion.57
  73.5 2.5 fusion.16
  75.9 1.4 fusion.58
  77.8 7.4 %collective-permute-done.9 = bf16[512,512]{1,0:T(8,128)(2,1)} collective-permute-done((bf16[512,512]{1,0:T(8,128)(2,1)S(1)}, bf16[512,512]{1,0:T(8,128)(2,1)}, u32[]{:S(2)}, u32[]{:S(2)}) %collective-permute-start.9) | collective-permute-done | bytes 524320 | tf_op jit(solution)/shard_map/ppermute | solution.py:12
  85.2 2.4 fusion.59
  88.2 1.4 fusion.60
  89.7 1.6 collective-permute-start.17
  91.4 1.1 broadcast_select_fusion.5
  93.5 8.4 %fusion.4 = f32[512,1536]{1,0:T(8,128)} fusion(bf16[1,4096,1536]{2,1,0:T(8,128)(2,1)S(1)} %bitcast.117, bf16[128,2048]{1,0:T(8,128)(2,1)S(1)} %get-tuple-element.27, bf16[128,2048]{1,0:T(8,128)(2,1)S(1)} %get-tuple-element.26, bf16[128,2048]{1,0:T(8,128)(2,1)S(1)} %get-tuple-element.25, bf16[128,2048]{1,0:T(8,128)(2,1)S(1)} %get-tuple-element.24, ...), kind=kOutput, calls=%fused_computation.4 | convolution fusion | flops 6471811072 | bytes 19922944 | tf_op jit(solution)/shard_map/dot_general | solution.py:105
  101.9 26.3 %broadcast_multiply_fusion = f32[512,4096]{1,0:T(8,128)} fusion(f32[512]{0:T(512)S(1)} %bitcast.115, bf16[1,1536,4096]{2,1,0:T(8,128)(2,1)} %param.21, f32[512,1536]{1,0:T(8,128)} %fusion.4, bf16[1,4096,1536]{2,1,0:T(8,128)(2,1)} %param.20, bf16[128,2048]{1,0:T(8,128)(2,1)} %copy-done.17, bf16[128,2048]{1,0:T(8,128)(2,1)} %copy-done.16, ...), kind=kOutput, calls=%fused_computation.9 | convolution fusion | flops 12921077760 | bytes 40896512 | tf_op jit(solution)/shard_map/dot_general | solution.py:108
  128.2 11.7 %reshape.66 = f32[512,4,2,512]{3,2,1,0:T(2,128)} reshape(f32[512,4096]{1,0:T(8,128)} %broadcast_multiply_fusion) | data formatting | bytes 16777216 | tf_op jit(solution)/shard_map/reshape | solution.py:111
  139.9 11.2 %constant_dynamic-slice_fusion.1 = (f32[512,4,1,512]{3,2,1,0:T(1,128)S(1)}, f32[512,4,1,512]{3,2,1,0:T(1,128)S(1)}) fusion(f32[512,4,2,512]{3,2,1,0:T(2,128)} %reshape.66, s32[]{:T(128)S(6)} %select_n.147, s32[]{:T(128)S(6)} %select_n.148), kind=kLoop, calls=%fused_computation.95 | loop fusion | bytes 16777224 | tf_op jit(solution)/shard_map/jit(dynamic_index_in_dim)/dynamic_slice | solution.py:113
  151.2 1.4 copy.27
  153.0 1.5 fusion.61
  155.4 1.5 fusion.63
  157.6 1.6 fusion.62
  159.7 1.5 convolution_add_fusion.6
  162.0 1.5 convolution_add_fusion.4
  163.6 2.3 collective-permute-start.11
  167.7 2.3 collective-permute-start.19
  170.0 23.1 %collective-permute-done.7 = bf16[256,512]{1,0:T(8,128)(2,1)S(1)} collective-permute-done((bf16[256,512]{1,0:T(8,128)(2,1)S(1)}, bf16[256,512]{1,0:T(8,128)(2,1)S(1)}, u32[]{:S(2)}, u32[]{:S(2)}) %collective-permute-start.7) | collective-permute-done | bytes 262176 | tf_op jit(solution)/shard_map/ppermute | solution.py:12
  193.2 5.5 %collective-permute-done.11 = bf16[256,512]{1,0:T(8,128)(2,1)S(1)} collective-permute-done((bf16[256,512]{1,0:T(8,128)(2,1)S(1)}, bf16[256,512]{1,0:T(8,128)(2,1)S(1)}, u32[]{:S(2)}, u32[]{:S(2)}) %collective-permute-start.11) | collective-permute-done | bytes 262176 | tf_op jit(solution)/shard_map/ppermute | solution.py:12
  199.7 4.7 %collective-permute-done.15 = bf16[256,512]{1,0:T(8,128)(2,1)S(1)} collective-permute-done((bf16[256,512]{1,0:T(8,128)(2,1)S(1)}, bf16[256,512]{1,0:T(8,128)(2,1)S(1)}, u32[]{:S(2)}, u32[]{:S(2)}) %collective-permute-start.15) | collective-permute-done | bytes 262176 | tf_op jit(solution)/shard_map/ppermute | solution.py:12
  204.5 1.5 fusion.50
  206.8 1.5 collective-permute-start.31
  208.3 1.4 collective-permute-start.32
  210.7 10.4 %collective-permute-done.30 = bf16[128,4,512]{2,0,1:T(8,128)(2,1)S(1)} collective-permute-done((bf16[128,4,512]{2,0,1:T(8,128)(2,1)S(1)}, bf16[128,4,512]{2,0,1:T(8,128)(2,1)S(1)}, u32[]{:S(2)}, u32[]{:S(2)}) %collective-permute-start.30) | collective-permute-done | bytes 524320 | tf_op jit(solution)/shard_map/ppermute | solution.py:12
  221.0 9.6 %collective-permute-done.31 = bf16[128,4,512]{2,0,1:T(8,128)(2,1)S(1)} collective-permute-done((bf16[128,4,512]{2,0,1:T(8,128)(2,1)S(1)}, bf16[128,4,512]{2,0,1:T(8,128)(2,1)S(1)}, u32[]{:S(2)}, u32[]{:S(2)}) %collective-permute-start.31) | collective-permute-done | bytes 524320 | tf_op jit(solution)/shard_map/ppermute | solution.py:12
  230.6 1.6 collective-permute-done.32
  233.6 3.5 %collective-permute-start.35 = (bf16[128,512]{1,0:T(8,128)(2,1)S(1)}, bf16[128,512]{1,0:T(8,128)(2,1)S(1)}, u32[]{:S(2)}, u32[]{:S(2)}) collective-permute-start(bf16[128,512]{1,0:T(8,128)(2,1)S(1)} %get-tuple-element.20), channel_id=1, source_target_pairs={{0,24},{4,28},{8,16},{12,20},{16,8},{20,12},{24,0},{28,4},{1,25},{... | collective-permute-start | bytes 393224 | tf_op jit(solution)/shard_map/ppermute | solution.py:12
  238.2 1.3 collective-permute-done.33
  239.5 5.7 %collective-permute-done.34 = bf16[128,512]{1,0:T(8,128)(2,1)S(1)} collective-permute-done((bf16[128,512]{1,0:T(8,128)(2,1)S(1)}, bf16[128,512]{1,0:T(8,128)(2,1)S(1)}, u32[]{:S(2)}, u32[]{:S(2)}) %collective-permute-start.34) | collective-permute-done | bytes 131104 | tf_op jit(solution)/shard_map/ppermute | solution.py:12
  (185 shorter events, 20.0 us)
Async XLA Ops:
  2.7 74.7 %collective-permute-start.20 = (bf16[128,2048]{1,0:T(8,128)(2,1)}, bf16[128,2048]{1,0:T(8,128)(2,1)}, u32[]{:S(2)}, u32[]{:S(2)}) collective-permute-start(bf16[128,2048]{1,0:T(8,128)(2,1)} %constant_dynamic-slice_fusion.6), channel_id=1, source_target_pairs={{0,1},{1,0},{2,3},{3,2},{4,5},{5,4},{6,7},{7,6},{8,9},{9,8},{10,11... | collective-permute-start | bytes 1572872 | tf_op jit(solution)/shard_map/ppermute | solution.py:12
  8.7 11.8 %collective-permute-start.26 = (f32[1,128]{1,0:T(1,128)S(1)}, f32[1,128]{1,0:T(1,128)S(1)}, u32[]{:S(2)}, u32[]{:S(2)}) collective-permute-start(f32[1,128]{1,0:T(1,128)S(1)} %get-tuple-element.55), channel_id=1, source_target_pairs={{0,1},{1,0},{2,3},{3,2},{4,5},{5,4},{6,7},{7,6},{8,9},{9,8},{10,11... | collective-permute-start | bytes 1544 | tf_op jit(solution)/shard_map/ppermute | solution.py:12
  8.8 13.3 %collective-permute-start.27 = (f32[1,128]{1,0:T(1,128)S(1)}, f32[1,128]{1,0:T(1,128)S(1)}, u32[]{:S(2)}, u32[]{:S(2)}) collective-permute-start(f32[1,128]{1,0:T(1,128)S(1)} %get-tuple-element.54), channel_id=1, source_target_pairs={{0,2},{1,3},{2,0},{3,1},{4,6},{5,7},{6,4},{7,5},{8,10},{9,11},{10,... | collective-permute-start | bytes 1544 | tf_op jit(solution)/shard_map/ppermute | solution.py:12
  10.8 16.3 %collective-permute-start.28 = (f32[1,128]{1,0:T(1,128)S(1)}, f32[1,128]{1,0:T(1,128)S(1)}, u32[]{:S(2)}, u32[]{:S(2)}) collective-permute-start(f32[1,128]{1,0:T(1,128)S(1)} %get-tuple-element.53), channel_id=1, source_target_pairs={{0,3},{1,2},{2,1},{3,0},{4,7},{5,6},{6,5},{7,4},{8,11},{9,10},{10,... | collective-permute-start | bytes 1544 | tf_op jit(solution)/shard_map/ppermute | solution.py:12
  13.0 13.7 %collective-permute-start = (bf16[64,2048]{1,0:T(8,128)(2,1)}, bf16[64,2048]{1,0:T(8,128)(2,1)S(1)}, u32[]{:S(2)}, u32[]{:S(2)}) collective-permute-start(bf16[64,2048]{1,0:T(8,128)(2,1)} %dynamic-slice_bitcast_fusion.1), channel_id=1, source_target_pairs={{0,16},{4,20},{8,24},{12,28},{16,0},{20,4},{24,8},{28,12},{1,17},{... | collective-permute-start | bytes 786440 | tf_op jit(solution)/shard_map/ppermute | solution.py:12
  20.5 67.2 %collective-permute-start.22 = (bf16[128,2048]{1,0:T(8,128)(2,1)}, bf16[128,2048]{1,0:T(8,128)(2,1)S(1)}, u32[]{:S(2)}, u32[]{:S(2)}) collective-permute-start(bf16[128,2048]{1,0:T(8,128)(2,1)} %constant_dynamic-slice_fusion.6), channel_id=1, source_target_pairs={{0,2},{1,3},{2,0},{3,1},{4,6},{5,7},{6,4},{7,5},{8,10},{9,11},{10,... | collective-permute-start | bytes 1572872 | tf_op jit(solution)/shard_map/ppermute | solution.py:12
  22.1 67.6 %collective-permute-start.24 = (bf16[128,2048]{1,0:T(8,128)(2,1)}, bf16[128,2048]{1,0:T(8,128)(2,1)S(1)}, u32[]{:S(2)}, u32[]{:S(2)}) collective-permute-start(bf16[128,2048]{1,0:T(8,128)(2,1)} %constant_dynamic-slice_fusion.6), channel_id=1, source_target_pairs={{0,3},{1,2},{2,1},{3,0},{4,7},{5,6},{6,5},{7,4},{8,11},{9,10},{10,... | collective-permute-start | bytes 1572872 | tf_op jit(solution)/shard_map/ppermute | solution.py:12
  26.7 13.2 %collective-permute-start.1 = (bf16[64,2048]{1,0:T(8,128)(2,1)S(1)}, bf16[64,2048]{1,0:T(8,128)(2,1)S(1)}, u32[]{:S(2)}, u32[]{:S(2)}) collective-permute-start(bf16[64,2048]{1,0:T(8,128)(2,1)S(1)} %collective-permute-done), channel_id=1, source_target_pairs={{0,1},{1,0},{2,3},{3,2},{4,5},{5,4},{6,7},{7,6},{8,9},{9,8},{10,11... | collective-permute-start | bytes 786440 | tf_op jit(solution)/shard_map/ppermute | solution.py:12
  27.2 28.3 %collective-permute-start.2 = (bf16[64,2048]{1,0:T(8,128)(2,1)S(1)}, bf16[64,2048]{1,0:T(8,128)(2,1)S(1)}, u32[]{:S(2)}, u32[]{:S(2)}) collective-permute-start(bf16[64,2048]{1,0:T(8,128)(2,1)S(1)} %collective-permute-done), channel_id=1, source_target_pairs={{0,2},{1,3},{2,0},{3,1},{4,6},{5,7},{6,4},{7,5},{8,10},{9,11},{10,... | collective-permute-start | bytes 786440 | tf_op jit(solution)/shard_map/ppermute | solution.py:12
  28.9 41.4 %copy-start.18 = (bf16[512,512]{1,0:T(8,128)(2,1)S(1)}, bf16[512,512]{1,0:T(8,128)(2,1)}, u32[]{:S(2)}) copy-start(bf16[512,512]{1,0:T(8,128)(2,1)} %get-tuple-element.12) | copy-start | bytes 1572868
  39.9 15.7 %collective-permute-start.3 = (bf16[64,2048]{1,0:T(8,128)(2,1)S(1)}, bf16[64,2048]{1,0:T(8,128)(2,1)S(1)}, u32[]{:S(2)}, u32[]{:S(2)}) collective-permute-start(bf16[64,2048]{1,0:T(8,128)(2,1)S(1)} %collective-permute-done), channel_id=1, source_target_pairs={{0,3},{1,2},{2,1},{3,0},{4,7},{5,6},{6,5},{7,4},{8,11},{9,10},{10,... | collective-permute-start | bytes 786440 | tf_op jit(solution)/shard_map/ppermute | solution.py:12
  55.5 2.8 %collective-permute-start.4 = (bf16[512,512]{1,0:T(8,128)(2,1)}, bf16[512,512]{1,0:T(8,128)(2,1)S(1)}, u32[]{:S(2)}, u32[]{:S(2)}) collective-permute-start(bf16[512,512]{1,0:T(8,128)(2,1)} %get-tuple-element.11), channel_id=1, source_target_pairs={{0,4},{4,0},{8,12},{12,8},{16,20},{20,16},{24,28},{28,24},{1,5},{5... | collective-permute-start | bytes 1572872 | tf_op jit(solution)/shard_map/ppermute | solution.py:12
  55.5 14.7 %collective-permute-start.5 = (bf16[512,512]{1,0:T(8,128)(2,1)}, bf16[512,512]{1,0:T(8,128)(2,1)}, u32[]{:S(2)}, u32[]{:S(2)}) collective-permute-start(bf16[512,512]{1,0:T(8,128)(2,1)} %get-tuple-element.11), channel_id=1, source_target_pairs={{0,8},{4,12},{8,0},{12,4},{16,24},{20,28},{24,16},{28,20},{1,9},{5... | collective-permute-start | bytes 1572872 | tf_op jit(solution)/shard_map/ppermute | solution.py:12
  57.2 36.2 %slice-start = ((s8[12582912]{0:T(1024)(128)(4,1)}), s8[4194304]{0:T(1024)(128)(4,1)S(1)}, s32[]{:S(2)}) async-start(s8[12582912]{0:T(1024)(128)(4,1)} %bitcast.116), calls=%async_computation | async-start | bytes 8388608
  58.3 17.6 %collective-permute-start.8 = (bf16[512,512]{1,0:T(8,128)(2,1)}, bf16[512,512]{1,0:T(8,128)(2,1)S(1)}, u32[]{:S(2)}, u32[]{:S(2)}) collective-permute-start(bf16[512,512]{1,0:T(8,128)(2,1)} %get-tuple-element.12), channel_id=1, source_target_pairs={{0,4},{4,0},{8,12},{12,8},{16,20},{20,16},{24,28},{28,24},{1,5},{5... | collective-permute-start | bytes 1572872 | tf_op jit(solution)/shard_map/ppermute | solution.py:12
  70.3 14.9 %collective-permute-start.9 = (bf16[512,512]{1,0:T(8,128)(2,1)S(1)}, bf16[512,512]{1,0:T(8,128)(2,1)}, u32[]{:S(2)}, u32[]{:S(2)}) collective-permute-start(bf16[512,512]{1,0:T(8,128)(2,1)S(1)} %copy-done.18), channel_id=1, source_target_pairs={{0,8},{4,12},{8,0},{12,4},{16,24},{20,28},{24,16},{28,20},{1,9},{5... | collective-permute-start | bytes 1572872 | tf_op jit(solution)/shard_map/ppermute | solution.py:12
  75.9 12.2 %collective-permute-start.12 = (bf16[512,512]{1,0:T(8,128)(2,1)}, bf16[512,512]{1,0:T(8,128)(2,1)S(1)}, u32[]{:S(2)}, u32[]{:S(2)}) collective-permute-start(bf16[512,512]{1,0:T(8,128)(2,1)} %get-tuple-element.14), channel_id=1, source_target_pairs={{0,4},{4,0},{8,12},{12,8},{16,20},{20,16},{24,28},{28,24},{1,5},{5... | collective-permute-start | bytes 1572872 | tf_op jit(solution)/shard_map/ppermute | solution.py:12
  77.4 75.2 %collective-permute-start.13 = (bf16[512,512]{1,0:T(8,128)(2,1)}, bf16[512,512]{1,0:T(8,128)(2,1)}, u32[]{:S(2)}, u32[]{:S(2)}) collective-permute-start(bf16[512,512]{1,0:T(8,128)(2,1)} %get-tuple-element.14), channel_id=1, source_target_pairs={{0,8},{4,12},{8,0},{12,4},{16,24},{20,28},{24,16},{28,20},{1,9},{5... | collective-permute-start | bytes 1572872 | tf_op jit(solution)/shard_map/ppermute | solution.py:12
  85.2 6.0 %collective-permute-start.21 = (bf16[128,2048]{1,0:T(8,128)(2,1)}, bf16[128,2048]{1,0:T(8,128)(2,1)S(1)}, u32[]{:S(2)}, u32[]{:S(2)}) collective-permute-start(bf16[128,2048]{1,0:T(8,128)(2,1)} %collective-permute-done.20), channel_id=1, source_target_pairs={{0,4},{4,0},{8,12},{12,8},{16,20},{20,16},{24,28},{28,24},{1,5},{5... | collective-permute-start | bytes 1572872 | tf_op jit(solution)/shard_map/ppermute | solution.py:12
  87.7 69.7 %collective-permute-start.16 = (bf16[512,512]{1,0:T(8,128)(2,1)}, bf16[512,512]{1,0:T(8,128)(2,1)}, u32[]{:S(2)}, u32[]{:S(2)}) collective-permute-start(bf16[512,512]{1,0:T(8,128)(2,1)} %get-tuple-element.13), channel_id=1, source_target_pairs={{0,4},{4,0},{8,12},{12,8},{16,20},{20,16},{24,28},{28,24},{1,5},{5... | collective-permute-start | bytes 1572872 | tf_op jit(solution)/shard_map/ppermute | solution.py:12
  88.2 4.4 %collective-permute-start.23 = (bf16[128,2048]{1,0:T(8,128)(2,1)S(1)}, bf16[128,2048]{1,0:T(8,128)(2,1)S(1)}, u32[]{:S(2)}, u32[]{:S(2)}) collective-permute-start(bf16[128,2048]{1,0:T(8,128)(2,1)S(1)} %collective-permute-done.22), channel_id=1, source_target_pairs={{0,4},{4,0},{8,12},{12,8},{16,20},{20,16},{24,28},{28,24},{1,5},{5... | collective-permute-start | bytes 1572872 | tf_op jit(solution)/shard_map/ppermute | solution.py:12
  89.7 65.4 %collective-permute-start.17 = (bf16[512,512]{1,0:T(8,128)(2,1)}, bf16[512,512]{1,0:T(8,128)(2,1)}, u32[]{:S(2)}, u32[]{:S(2)}) collective-permute-start(bf16[512,512]{1,0:T(8,128)(2,1)} %get-tuple-element.13), channel_id=1, source_target_pairs={{0,8},{4,12},{8,0},{12,4},{16,24},{20,28},{24,16},{28,20},{1,9},{5... | collective-permute-start | bytes 1572872 | tf_op jit(solution)/shard_map/ppermute | solution.py:12
  91.2 1.9 collective-permute-start.25
  92.5 67.2 %collective-permute-start.6 = (bf16[512,512]{1,0:T(8,128)(2,1)}, bf16[512,512]{1,0:T(8,128)(2,1)}, u32[]{:S(2)}, u32[]{:S(2)}) collective-permute-start(bf16[512,512]{1,0:T(8,128)(2,1)} %collective-permute-done.5), channel_id=1, source_target_pairs={{0,4},{4,0},{8,12},{12,8},{16,20},{20,16},{24,28},{28,24},{1,5},{5... | collective-permute-start | bytes 1572872 | tf_op jit(solution)/shard_map/ppermute | solution.py:12
  93.2 68.9 %collective-permute-start.10 = (bf16[512,512]{1,0:T(8,128)(2,1)}, bf16[512,512]{1,0:T(8,128)(2,1)}, u32[]{:S(2)}, u32[]{:S(2)}) collective-permute-start(bf16[512,512]{1,0:T(8,128)(2,1)} %collective-permute-done.9), channel_id=1, source_target_pairs={{0,4},{4,0},{8,12},{12,8},{16,20},{20,16},{24,28},{28,24},{1,5},{5... | collective-permute-start | bytes 1572872 | tf_op jit(solution)/shard_map/ppermute | solution.py:12
  152.6 51.8 %collective-permute-start.29 = (f32[512,4,512]{2,0,1:T(8,128)S(1)}, f32[512,4,512]{2,0,1:T(8,128)S(1)}, u32[]{:S(2)}, u32[]{:S(2)}) collective-permute-start(f32[512,4,512]{2,0,1:T(8,128)S(1)} %bitcast.97), channel_id=1, source_target_pairs={{0,4},{4,0},{8,12},{12,8},{16,20},{20,16},{24,28},{28,24},{1,5},{5... | collective-permute-start | bytes 12582920 | tf_op jit(solution)/shard_map/ppermute | solution.py:12
  155.0 10.9 %collective-permute-start.14 = (bf16[512,512]{1,0:T(8,128)(2,1)}, bf16[512,512]{1,0:T(8,128)(2,1)S(1)}, u32[]{:S(2)}, u32[]{:S(2)}) collective-permute-start(bf16[512,512]{1,0:T(8,128)(2,1)} %collective-permute-done.13), channel_id=1, source_target_pairs={{0,4},{4,0},{8,12},{12,8},{16,20},{20,16},{24,28},{28,24},{1,5},{5... | collective-permute-start | bytes 1572872 | tf_op jit(solution)/shard_map/ppermute | solution.py:12
  157.4 9.8 %collective-permute-start.18 = (bf16[512,512]{1,0:T(8,128)(2,1)}, bf16[512,512]{1,0:T(8,128)(2,1)S(1)}, u32[]{:S(2)}, u32[]{:S(2)}) collective-permute-start(bf16[512,512]{1,0:T(8,128)(2,1)} %collective-permute-done.17), channel_id=1, source_target_pairs={{0,4},{4,0},{8,12},{12,8},{16,20},{20,16},{24,28},{28,24},{1,5},{5... | collective-permute-start | bytes 1572872 | tf_op jit(solution)/shard_map/ppermute | solution.py:12
  161.3 31.8 %collective-permute-start.7 = (bf16[256,512]{1,0:T(8,128)(2,1)S(1)}, bf16[256,512]{1,0:T(8,128)(2,1)S(1)}, u32[]{:S(2)}, u32[]{:S(2)}) collective-permute-start(bf16[256,512]{1,0:T(8,128)(2,1)S(1)} %slice.389), channel_id=1, source_target_pairs={{0,16},{4,20},{8,24},{12,28},{16,0},{20,4},{24,8},{28,12},{1,17},{... | collective-permute-start | bytes 786440 | tf_op jit(solution)/shard_map/ppermute | solution.py:12
  163.6 35.2 %copy-start.23 = (bf16[3,512]{1,0:T(4,128)(2,1)S(1)}, bf16[3,512]{1,0:T(4,128)(2,1)}, u32[]{:S(2)}) copy-start(bf16[3,512]{1,0:T(4,128)(2,1)} %get-tuple-element.44) | copy-start | bytes 9220
  163.6 35.2 %copy-start.37 = (f32[1,512]{1,0:T(1,128)S(1)}, f32[1,512]{1,0:T(1,128)}, u32[]{:S(2)}) copy-start(f32[1,512]{1,0:T(1,128)} %get-tuple-element.28) | copy-start | bytes 6148
  163.6 35.2 %copy-start.38 = (f32[1,512]{1,0:T(1,128)S(1)}, f32[1,512]{1,0:T(1,128)}, u32[]{:S(2)}) copy-start(f32[1,512]{1,0:T(1,128)} %get-tuple-element.39) | copy-start | bytes 6148
  163.6 35.2 %copy-start.39 = (f32[1,512]{1,0:T(1,128)S(1)}, f32[1,512]{1,0:T(1,128)}, u32[]{:S(2)}) copy-start(f32[1,512]{1,0:T(1,128)} %get-tuple-element.40) | copy-start | bytes 6148
  163.6 35.2 %copy-start.40 = (f32[1,512]{1,0:T(1,128)S(1)}, f32[1,512]{1,0:T(1,128)}, u32[]{:S(2)}) copy-start(f32[1,512]{1,0:T(1,128)} %get-tuple-element.41) | copy-start | bytes 6148
  163.6 35.2 %copy-start.44 = (f32[512]{0:T(512)S(1)}, f32[512]{0:T(512)}, u32[]{:S(2)}) copy-start(f32[512]{0:T(512)} %get-tuple-element.48) | copy-start | bytes 6148
  163.6 35.1 %collective-permute-start.11 = (bf16[256,512]{1,0:T(8,128)(2,1)S(1)}, bf16[256,512]{1,0:T(8,128)(2,1)S(1)}, u32[]{:S(2)}, u32[]{:S(2)}) collective-permute-start(bf16[256,512]{1,0:T(8,128)(2,1)S(1)} %slice.388), channel_id=1, source_target_pairs={{0,16},{4,20},{8,24},{12,28},{16,0},{20,4},{24,8},{28,12},{1,17},{... | collective-permute-start | bytes 786440 | tf_op jit(solution)/shard_map/ppermute | solution.py:12
  166.3 32.9 %copy-start.22 = (bf16[3,512]{1,0:T(4,128)(2,1)S(1)}, bf16[3,512]{1,0:T(4,128)(2,1)}, u32[]{:S(2)}) copy-start(bf16[3,512]{1,0:T(4,128)(2,1)} %get-tuple-element.47) | copy-start | bytes 9220
  166.4 32.9 %copy-start.33 = (f32[1,512]{1,0:T(1,128)S(1)}, f32[1,512]{1,0:T(1,128)}, u32[]{:S(2)}) copy-start(f32[1,512]{1,0:T(1,128)} %get-tuple-element.35) | copy-start | bytes 6148
  166.4 32.9 %copy-start.34 = (f32[1,512]{1,0:T(1,128)S(1)}, f32[1,512]{1,0:T(1,128)}, u32[]{:S(2)}) copy-start(f32[1,512]{1,0:T(1,128)} %get-tuple-element.36) | copy-start | bytes 6148
  166.4 37.9 %collective-permute-start.15 = (bf16[256,512]{1,0:T(8,128)(2,1)S(1)}, bf16[256,512]{1,0:T(8,128)(2,1)S(1)}, u32[]{:S(2)}, u32[]{:S(2)}) collective-permute-start(bf16[256,512]{1,0:T(8,128)(2,1)S(1)} %slice.387), channel_id=1, source_target_pairs={{0,16},{4,20},{8,24},{12,28},{16,0},{20,4},{24,8},{28,12},{1,17},{... | collective-permute-start | bytes 786440 | tf_op jit(solution)/shard_map/ppermute | solution.py:12
  167.7 42.4 %collective-permute-start.19 = (bf16[256,512]{1,0:T(8,128)(2,1)S(1)}, bf16[256,512]{1,0:T(8,128)(2,1)S(1)}, u32[]{:S(2)}, u32[]{:S(2)}) collective-permute-start(bf16[256,512]{1,0:T(8,128)(2,1)S(1)} %slice.386), channel_id=1, source_target_pairs={{0,16},{4,20},{8,24},{12,28},{16,0},{20,4},{24,8},{28,12},{1,17},{... | collective-permute-start | bytes 786440 | tf_op jit(solution)/shard_map/ppermute | solution.py:12
  206.2 14.9 %collective-permute-start.30 = (bf16[128,4,512]{2,0,1:T(8,128)(2,1)S(1)}, bf16[128,4,512]{2,0,1:T(8,128)(2,1)S(1)}, u32[]{:S(2)}, u32[]{:S(2)}) collective-permute-start(bf16[128,4,512]{2,0,1:T(8,128)(2,1)S(1)} %get-tuple-element.8), channel_id=1, source_target_pairs={{0,1},{1,0},{2,3},{3,2},{4,5},{5,4},{6,7},{7,6},{8,9},{9,8},{10,11... | collective-permute-start | bytes 1572872 | tf_op jit(solution)/shard_map/ppermute | solution.py:12
  206.8 23.8 %collective-permute-start.31 = (bf16[128,4,512]{2,0,1:T(8,128)(2,1)S(1)}, bf16[128,4,512]{2,0,1:T(8,128)(2,1)S(1)}, u32[]{:S(2)}, u32[]{:S(2)}) collective-permute-start(bf16[128,4,512]{2,0,1:T(8,128)(2,1)S(1)} %get-tuple-element.10), channel_id=1, source_target_pairs={{0,2},{1,3},{2,0},{3,1},{4,6},{5,7},{6,4},{7,5},{8,10},{9,11},{10,... | collective-permute-start | bytes 1572872 | tf_op jit(solution)/shard_map/ppermute | solution.py:12
  208.3 23.9 %collective-permute-start.32 = (bf16[128,4,512]{2,0,1:T(8,128)(2,1)S(1)}, bf16[128,4,512]{2,0,1:T(8,128)(2,1)S(1)}, u32[]{:S(2)}, u32[]{:S(2)}) collective-permute-start(bf16[128,4,512]{2,0,1:T(8,128)(2,1)S(1)} %get-tuple-element.9), channel_id=1, source_target_pairs={{0,3},{1,2},{2,1},{3,0},{4,7},{5,6},{6,5},{7,4},{8,11},{9,10},{10,... | collective-permute-start | bytes 1572872 | tf_op jit(solution)/shard_map/ppermute | solution.py:12
  210.1 35.8 %copy-start.1 = (bf16[1,256,4096]{2,1,0:T(8,128)(2,1)S(1)}, bf16[1,256,4096]{2,1,0:T(8,128)(2,1)}, u32[]{:S(2)}) copy-start(bf16[1,256,4096]{2,1,0:T(8,128)(2,1)} %param.11) | copy-start | bytes 6291460
  232.6 6.9 %collective-permute-start.33 = (bf16[128,512]{1,0:T(8,128)(2,1)S(1)}, bf16[128,512]{1,0:T(8,128)(2,1)S(1)}, u32[]{:S(2)}, u32[]{:S(2)}) collective-permute-start(bf16[128,512]{1,0:T(8,128)(2,1)S(1)} %get-tuple-element.19), channel_id=1, source_target_pairs={{0,8},{4,12},{8,0},{12,4},{16,24},{20,28},{24,16},{28,20},{1,9},{5... | collective-permute-start | bytes 393224 | tf_op jit(solution)/shard_map/ppermute | solution.py:12
  232.7 12.5 %collective-permute-start.34 = (bf16[128,512]{1,0:T(8,128)(2,1)S(1)}, bf16[128,512]{1,0:T(8,128)(2,1)S(1)}, u32[]{:S(2)}, u32[]{:S(2)}) collective-permute-start(bf16[128,512]{1,0:T(8,128)(2,1)S(1)} %get-tuple-element.21), channel_id=1, source_target_pairs={{0,16},{4,20},{8,24},{12,28},{16,0},{20,4},{24,8},{28,12},{1,17},{... | collective-permute-start | bytes 393224 | tf_op jit(solution)/shard_map/ppermute | solution.py:12
  233.6 11.6 %collective-permute-start.35 = (bf16[128,512]{1,0:T(8,128)(2,1)S(1)}, bf16[128,512]{1,0:T(8,128)(2,1)S(1)}, u32[]{:S(2)}, u32[]{:S(2)}) collective-permute-start(bf16[128,512]{1,0:T(8,128)(2,1)S(1)} %get-tuple-element.20), channel_id=1, source_target_pairs={{0,24},{4,28},{8,16},{12,20},{16,8},{20,12},{24,0},{28,4},{1,25},{... | collective-permute-start | bytes 393224 | tf_op jit(solution)/shard_map/ppermute | solution.py:12
  (37 other events, 393.7 us)

commit v2 on v0

v2 whole, which is shorter than its diff:
```python
import functools

import jax
import jax.numpy as jnp
from jax import lax
from jax.experimental import pallas as pl
from jax.experimental.pallas import tpu as pltpu
from jax.sharding import PartitionSpec as P

F32 = jnp.float32
BF16 = jnp.bfloat16
LANES = 128
VMEM = 56 << 20
SMEM_SPEC = pl.BlockSpec(memory_space=pltpu.SMEM)
CHUNKS = 2


def xor_send(value, mask):
    pairs = [(i, i ^ mask) for i in range(lax.axis_size("dp"))]
    return lax.ppermute(value, "dp", pairs)


def owner_send(value, mask):
    pairs = [(i, i ^ mask) for i in range(lax.axis_size("expert"))]
    return lax.ppermute(value, "expert", pairs)


def after(value, *earlier):
    return lax.optimization_barrier((value, *earlier))[0]


def dot(left, right):
    return jnp.dot(left, right, preferred_element_type=F32)


def dot_t(left, right):
    return lax.dot_general(left, right, (((1,), (1,)), ((), ())), preferred_element_type=F32)


def whole(array):
    return pl.BlockSpec(array.shape, lambda *_: (0,) * array.ndim)


def tile_of(size, tile):
    return tile if size % tile == 0 else size


def half_product_kernel(blocks, depth, pieces, where, window, *refs):
    fars, weights = refs[:pieces], refs[pieces : pieces + blocks]
    near_out, far_out, rows = refs[pieces + blocks :]
    tokens = window.shape[1]

    @pl.when(pl.program_id(0) == 0)
    def _():
        for mask in range(blocks):
            source = pl.ds(pl.multiple_of((where[0] ^ mask) * depth, LANES), depth)
            lanes = slice(mask * depth, (mask + 1) * depth)
            rows[:tokens, lanes] = window[0, :, source]
            first = tokens
            for far in fars:
                rows[first : first + far.shape[0], lanes] = far[:, source]
                first += far.shape[0]

    total = None
    for mask in range(blocks):
        term = dot(rows[:, mask * depth : (mask + 1) * depth], weights[mask][...])
        total = term if mask == 0 else total + term
    near_out[...] = total[:tokens]
    far_out[...] = total[tokens:].astype(BF16)


def half_product(where, window, fars, weights, offset, cols):
    tokens, features = window.shape[1], fars[0].shape[1]
    depth = weights[0].shape[0]
    tile = tile_of(cols, 512)
    base = offset // tile

    def spec(weight):
        first = base if weight.shape[1] != cols else 0
        return pl.BlockSpec((depth, tile), lambda i, where: (0, first + i))

    return pl.pallas_call(
        functools.partial(half_product_kernel, len(weights), depth, len(fars)),
        grid_spec=pltpu.PrefetchScalarGridSpec(
            num_scalar_prefetch=1,
            grid=(cols // tile,),
            in_specs=[pl.BlockSpec((1, tokens, features), lambda i, where: (0, 0, where[1]))]
            + [whole(far) for far in fars]
            + [spec(weight) for weight in weights],
            out_specs=[pl.BlockSpec((tokens, tile), lambda i, where: (0, i))] * 2,
            scratch_shapes=[pltpu.VMEM((2 * tokens, features), BF16)],
        ),
        out_shape=[
            jax.ShapeDtypeStruct((tokens, cols), F32),
            jax.ShapeDtypeStruct((tokens, cols), BF16),
        ],
        compiler_params=pltpu.CompilerParams(vmem_limit_bytes=VMEM),
        cost_estimate=pl.CostEstimate(
            flops=4 * tokens * features * cols,
            transcendentals=0,
            bytes_accessed=2 * features * (2 * tokens + cols) + 6 * tokens * cols,
        ),
        name="half_product",
    )(where, window, *fars, *weights)


def conv_kernel_body(pad, pieces, where, own, back, state, taps, bias, *refs):
    out, rows = refs[-2:]
    tokens = own.shape[0]
    count = taps.shape[0]
    rows[pad - (count - 1) : pad, :] = state[0].astype(F32)
    share = tokens // pieces
    for mask in range(pieces):
        start = pl.multiple_of((where[1] ^ mask) * share, 8)
        piece = back[mask * share : (mask + 1) * share, :].astype(F32)
        value = (own[pl.ds(start, share), :] + piece).astype(BF16).astype(F32)
        rows[pl.ds(pl.multiple_of(pad + start, 8), share), :] = value
    summed = bias[...]
    for tap in range(count):
        first = pad - (count - 1) + tap
        summed = summed + rows[first : first + tokens, :] * taps[tap : tap + 1, :]
    out[0] = jax.nn.silu(summed).astype(BF16)


def conv(where, pieces, own, back, state, taps, bias, offset, channels, earlier):
    tokens, cols = own.shape
    tile = tile_of(cols, 512)
    base = offset // tile
    count = taps.shape[0]
    pad = 8
    inputs = [where, own, back, state, taps, bias]
    in_specs = [
        SMEM_SPEC,
        pl.BlockSpec((tokens, tile), lambda i: (0, i)),
        pl.BlockSpec((tokens, tile), lambda i: (0, i)),
        pl.BlockSpec((1, count - 1, tile), lambda i: (0, 0, base + i)),
        pl.BlockSpec((count, tile), lambda i: (0, base + i)),
        pl.BlockSpec((1, tile), lambda i: (0, base + i)),
    ]
    aliases = {}
    if earlier is not None:
        inputs.append(earlier)
        in_specs.append(pl.BlockSpec(memory_space=pl.ANY))
        aliases = {6: 0}
    return pl.pallas_call(
        functools.partial(conv_kernel_body, pad, pieces),
        grid=(cols // tile,),
        in_specs=in_specs,
        out_specs=pl.BlockSpec((1, tokens, tile), lambda i: (0, 0, base + i)),
        out_shape=jax.ShapeDtypeStruct((1, tokens, channels), BF16),
        scratch_shapes=[pltpu.VMEM((pad + tokens, tile), F32)],
        input_output_aliases=aliases,
        compiler_params=pltpu.CompilerParams(vmem_limit_bytes=VMEM),
        cost_estimate=pl.CostEstimate(
            flops=12 * tokens * cols,
            transcendentals=tokens * cols,
            bytes_accessed=8 * tokens * cols,
        ),
        name="conv",
    )(*inputs)


def hidden_kernel(quarter, where, *refs):
    inputs, router, gates, ups = refs[:4], refs[4], refs[5:9], refs[9:13]
    hidden, scale = refs[13:]
    gated = raised = None
    for source, gate, up in zip(inputs, gates, ups):
        rows = source[:, :quarter]
        one, two = dot(rows, gate[0]), dot(rows, up[0])
        gated = one if gated is None else gated + one
        raised = two if raised is None else raised + two
    hidden[...] = (jax.nn.silu(gated) * raised).astype(BF16)

    @pl.when(pl.program_id(0) == 0)
    def _():
        core, owner = where[0], where[1]
        logits = None
        for number, source in enumerate(inputs):
            block = 2 * core + number if number < 2 else 2 * (1 - core) + number - 2
            lanes = pl.ds(pl.multiple_of(block * quarter, LANES), quarter)
            term = dot_t(source[:, :quarter], router[:, lanes])
            logits = term if logits is None else logits + term
        lane = lax.broadcasted_iota(jnp.int32, logits.shape, 1)
        ids = inputs[1][:, quarter:].astype(jnp.int32)
        ids_a, ids_b = ids[:, 0:1], ids[:, 1:2]
        chosen_a = jnp.sum(jnp.where(lane == ids_a, logits, 0.0), axis=1, keepdims=True)
        chosen_b = jnp.sum(jnp.where(lane == ids_b, logits, 0.0), axis=1, keepdims=True)
        weight = jax.nn.sigmoid(chosen_a - chosen_b)
        mixed = jnp.where(ids_a == owner, weight, 0.0) + jnp.where(
            ids_b == owner, 1.0 - weight, 0.0
        )
        scale[...] = jnp.broadcast_to(mixed, scale.shape)


def hidden_units(where, inputs, router, w_gate, w_up):
    rows, quarter = inputs[0].shape
    width, units = w_gate.shape[1:]
    tile = tile_of(units, 256)

    def spec(number):
        def place(i, where):
            return 0, 2 * where[0] + number if number < 2 else 2 - 2 * where[0] + number - 2, i

        return pl.BlockSpec((1, quarter, tile), place)

    specs = [spec(number) for number in range(4)]
    return pl.pallas_call(
        functools.partial(hidden_kernel, quarter),
        grid_spec=pltpu.PrefetchScalarGridSpec(
            num_scalar_prefetch=1,
            grid=(units // tile,),
            in_specs=[whole(array) for array in (*inputs, router)] + specs + specs,
            out_specs=[
                pl.BlockSpec((rows, tile), lambda i, where: (0, i)),
                pl.BlockSpec((rows, LANES), lambda i, where: (0, 0)),
            ],
        ),
        out_shape=[
            jax.ShapeDtypeStruct((rows, units), BF16),
            jax.ShapeDtypeStruct((rows, LANES), F32),
        ],
        compiler_params=pltpu.CompilerParams(vmem_limit_bytes=VMEM),
        cost_estimate=pl.CostEstimate(
            flops=4 * rows * width * units,
            transcendentals=rows * units,
            bytes_accessed=4 * width * units + 4 * rows * width,
        ),
        name="hidden_units",
    )(where, *inputs, router, *[w_gate] * 4, *[w_up] * 4)


def down_kernel(steps, where, hidden, scale, down, send, keep):
    value = dot(hidden[...], down[0]) * scale[:, 0:1]

    @pl.when(pl.program_id(0) < steps)
    def _():
        send[...] = value.astype(BF16)

    @pl.when(pl.program_id(0) >= steps)
    def _():
        keep[...] = value


def down_units(where, hidden, scale, w_down, final):
    rows, units = hidden.shape
    width = w_down.shape[2]
    steps = width // final // 2

    def place(i, where):
        parity = jnp.where(i < steps, 1 - where[0], where[0])
        return 0, 0, 2 * lax.rem(i, steps) + parity

    return pl.pallas_call(
        functools.partial(down_kernel, steps),
        grid_spec=pltpu.PrefetchScalarGridSpec(
            num_scalar_prefetch=1,
            grid=(2 * steps,),
            in_specs=[
                pl.BlockSpec(hidden.shape, lambda i, where: (0, 0)),
                pl.BlockSpec(scale.shape, lambda i, where: (0, 0)),
                pl.BlockSpec((1, units, final), place),
            ],
            out_specs=[
                pl.BlockSpec((rows, final), lambda i, where: (0, jnp.minimum(i, steps - 1))),
                pl.BlockSpec((rows, final), lambda i, where: (0, jnp.maximum(i - steps, 0))),
            ],
        ),
        out_shape=[
            jax.ShapeDtypeStruct((rows, width // 2), BF16),
            jax.ShapeDtypeStruct((rows, width // 2), F32),
        ],
        compiler_params=pltpu.CompilerParams(vmem_limit_bytes=VMEM),
        cost_estimate=pl.CostEstimate(
            flops=2 * rows * width * units,
            transcendentals=0,
            bytes_accessed=2 * width * units + 2 * rows * (units + width),
        ),
        name="down_units",
    )(where, hidden, scale, w_down)


def collect_kernel(places, final, where, *refs):
    count = len(refs) - places - 1
    sides, outs, rows = refs[:count], refs[count:-1], refs[-1]
    offset = 0
    for pair in range(0, count, 2):
        value = sides[pair][...] + sides[pair + 1][...].astype(F32)
        rows[:, offset : offset + value.shape[1]] = value
        offset += value.shape[1]
    for mask in range(places):
        start = pl.multiple_of((where[2] ^ mask) * final, LANES)
        value = rows[:, pl.ds(start, final)]
        outs[mask][...] = value if mask == 0 else value.astype(BF16)


def collect(where, sides, final, places):
    rows = sides[0].shape[0]
    vmem = pl.BlockSpec(memory_space=pltpu.VMEM)
    return pl.pallas_call(
        functools.partial(collect_kernel, places, final),
        in_specs=[SMEM_SPEC] + [vmem] * len(sides),
        out_specs=[vmem] * places,
        out_shape=[jax.ShapeDtypeStruct((rows, final), F32)]
        + [jax.ShapeDtypeStruct((rows, final), BF16)] * (places - 1),
        scratch_shapes=[pltpu.VMEM((rows, places * final), F32)],
        name="collect",
    )(where, *sides)


def body(
    mamba_in,
    conv_state,
    in_weight,
    conv_kernel,
    conv_bias,
    moe_in,
    router,
    expert_ids,
    w_gate,
    w_up,
    w_down,
):
    tokens, width = mamba_in.shape[1:]
    channels = in_weight.shape[1]
    dp = lax.axis_size("dp")
    owners = lax.axis_size("expert")
    half = dp // 2
    me = lax.axis_index("dp")
    mine = lax.axis_index("expert")
    core = me & 1
    side = jnp.where(me >= half, 1, 0)
    local = me & (half - 1)
    place = me >> 1
    final = width // dp
    moe_rows = moe_in.shape[0]
    split = width // 2
    quarter = split // 2
    features = width // 2
    share = tokens // owners
    cols = channels // CHUNKS
    where = jnp.stack([core, mine, place])
    spot = jnp.stack([local, side])
    columns = range(2, owners, 2)

    piece = lax.dynamic_slice(
        mamba_in, (0, mine * share, (1 - side) * features), (1, share, features)
    )[0]
    piece = xor_send(piece, half)

    left = lax.dynamic_slice(moe_in, (0, core * split), (moe_rows, quarter))
    right = lax.dynamic_slice(moe_in, (0, core * split + quarter), (moe_rows, quarter))
    names = jnp.pad(expert_ids.astype(BF16), ((0, 0), (0, LANES - expert_ids.shape[1])))
    right = jnp.concatenate([right, names], axis=1)
    lefts = {0: left, 1: owner_send(left, 1)}
    rights = {0: right}
    for mask in columns:
        rights[mask] = owner_send(right, mask)
    both = jnp.concatenate([lefts[0], lefts[1]], axis=0)
    for mask in columns:
        got = owner_send(both, mask)
        lefts[mask], lefts[mask + 1] = got[:moe_rows], got[moe_rows:]
    got = owner_send(jnp.concatenate([rights[mask] for mask in range(0, owners, 2)], axis=0), 1)
    for mask in range(0, owners, 2):
        rights[mask + 1] = got[mask // 2 * moe_rows : (mask // 2 + 1) * moe_rows]
    lefts = jnp.concatenate([lefts[mask] for mask in range(owners)], axis=0)
    rights = jnp.concatenate([rights[mask] for mask in range(owners)], axis=0)
    inputs = [lefts, rights, xor_send(lefts, 1), xor_send(rights[:, :quarter], 1)]

    fars = [piece, owner_send(piece, 1)]
    both = jnp.concatenate(fars, axis=0)
    for mask in columns:
        fars.append(owner_send(both, mask))

    paired = xor_send(in_weight, 1)
    weights, arrived = [], []
    for chunk in range(CHUNKS):
        block = in_weight[:, chunk * cols : (chunk + 1) * cols]
        entry, direct = [in_weight, paired], []
        for mask in range(2, half, 2):
            if chunk:
                block = after(block, *fars[1:])
            direct.append(xor_send(block, mask))
            entry += [direct[-1], xor_send(direct[-1], 1)]
        weights.append(entry)
        arrived.append(direct)

    def product(chunk, *earlier):
        own, out = half_product(
            spot, mamba_in, [after(fars[0], *earlier), *fars[1:]], weights[chunk], chunk * cols, cols
        )
        return own, out, xor_send(out, half)

    def convolve(chunk, own, come, before):
        return conv(
            where,
            owners,
            own,
            come,
            conv_state,
            conv_kernel,
            conv_bias[None],
            chunk * cols,
            channels,
            before,
        )

    inputs[0] = after(inputs[0], *fars, *arrived[0], paired)
    hidden, scale = hidden_units(where, inputs, router.T, w_gate, w_up)
    own_0, out_0, come_0 = product(0, hidden)
    hidden = after(hidden, out_0, *arrived[1])
    send, keep = down_units(where, hidden, scale, w_down, final)
    taken = xor_send(send, 1)
    own_1, out_1, come_1 = product(1, keep)
    taken = after(taken, out_1)
    total = (keep + taken.astype(F32)).reshape(owners, moe_rows, split)
    left, right = total[:, :, :quarter], total[:, :, quarter:]
    got = owner_send(jnp.concatenate([left[m] for m in range(1, owners, 2)], 0).astype(BF16), 1)
    got = got.reshape(owners // 2, moe_rows, quarter)
    left = {mask: left[mask] + got[mask // 2].astype(F32) for mask in range(0, owners, 2)}
    firsts, seconds = right[0], right[1]
    for mask in columns:
        got = owner_send(right[mask : mask + 2].reshape(-1, quarter).astype(BF16), mask)
        firsts = firsts + got[:moe_rows].astype(F32)
        seconds = seconds + got[moe_rows:].astype(F32)
    conv_out = convolve(0, after(own_0, firsts), come_0, None)
    lefts = left[0]
    for mask in columns:
        come = owner_send(left[mask].astype(BF16), mask)
        if mask != columns[-1]:
            lefts = lefts + come.astype(F32)
    sides = [lefts, come, firsts, owner_send(seconds.astype(BF16), 1)]
    answer, *outs = collect(where, sides, final, half)
    for mask, out in enumerate(outs, 1):
        answer = answer + xor_send(out, 2 * mask).astype(F32)
    conv_out = convolve(1, own_1, come_1, conv_out)
    return conv_out, answer.astype(BF16)


def solution(mesh):
    in_specs = (
        P("dp", None, None),
        P("dp", None, "expert"),
        P("dp", "expert"),
        P(None, "expert"),
        P("expert"),
        P("expert", None),
        P(),
        P("expert", None),
        P("expert", None, "dp"),
        P("expert", None, "dp"),
        P("expert", "dp", None),
    )
    out_specs = (P("dp", None, "expert"), P("expert", "dp"))
    return jax.shard_map(body, mesh=mesh, in_specs=in_specs, out_specs=out_specs, check_vma=False)
```

time: 354 us -> 175 us (0.49)
  waiting for transfers between devices: 234 us -> 69.9 us
  Pallas kernels: 0 us -> 58.8 us
  blocking collectives: 53.1 us -> 0 us
  matrix products: 42.5 us -> 0 us
  starting transfers between devices: 3.77 us -> 27.8 us
  between operations: 14.2 us -> 0.92 us
  local copies, waits for them, and re-layouts: 1.77 us -> 9.63 us
    all_gather x1 -> x0, waiting for transfers between devices: 134 us -> none  [body(): lax.all_gather(in_weight, 'dp', axis=0, tiled=True)]
    reduce_scatter x1 -> x0, waiting for transfers between devices: 88.7 us -> none  [body(): shares = lax.psum_scatter(partials, 'dp', scatter_dimension=2, tiled=True)]
    ppermute x0 -> x24, waiting for transfers between devices: none -> 69.9 us  [the longest x10 44.6 us: owner_send(): return lax.ppermute(value, 'expert', pairs)]
    pallas_call x0 -> x7, Pallas kernels: none -> 58.8 us  [the longest x1 22 us: hidden_units(): pl.pallas_call(functools.partial(hidden_kernel, quarter), grid_spec=pltpu...]
    all_to_all x1 -> x0, blocking collectives: 53.1 us -> none  [body(): lax.all_to_all(send_buffer, 'expert', split_axis=0, concat_axis=0, tiled=...]
    dot_general x7 -> x0, matrix products: 42.5 us -> none  [the longest x1 11.8 us: expert_ffn(): return jnp.dot(hidden, down_mat, preferred_element_type=jnp.float32)]
    ppermute x0 -> x24, starting transfers between devices: none -> 27.8 us  [the longest x10 14 us: owner_send(): return lax.ppermute(value, 'expert', pairs)]
    all_to_all x1 -> x0, waiting for transfers between devices: 9.86 us -> none  [body(): lax.all_to_all(shares, 'expert', split_axis=0, concat_axis=0, tiled=True)]
  transfers between devices with their start and end apart: 3 -> 24, of which waited for: 3 -> 13; matrix products, arithmetic and copies ran while one was open for 1% -> 5% of each run, Pallas kernels for 0% -> 26%
where the time goes in v2:
time: 175 us; the launch traced here: 174 us
  waiting for transfers between devices  69.9 us (40%)
  Pallas kernels  58.8 us (34%)
  starting transfers between devices  27.8 us (16%)
  local copies, waits for them, and re-layouts  9.63 us (6%)
  other arithmetic  7.18 us (4%)
    ppermute x10, waiting for transfers between devices, owner_send(): return lax.ppermute(value, 'expert', pairs)  44.6 us
    ppermute x14, waiting for transfers between devices, xor_send(): return lax.ppermute(value, 'dp', pairs)  25.3 us
    pallas_call x1, Pallas kernels, hidden_units(): pl.pallas_call(functools.partial(hidden_kernel, quarter), grid_spec=pltpu...  22 us
    pallas_call x1, Pallas kernels, down_units(): pl.pallas_call(functools.partial(down_kernel, steps), grid_spec=pltpu.Pre...  14.3 us
    ppermute x10, starting transfers between devices, owner_send(): return lax.ppermute(value, 'expert', pairs)  14 us
    pallas_call x2, Pallas kernels, half_product(): pl.pallas_call(functools.partial(half_product_kernel, len(weights), depth...  14 us
    ppermute x14, starting transfers between devices, xor_send(): return lax.ppermute(value, 'dp', pairs)  13.8 us
    pallas_call x2, Pallas kernels, conv(): pl.pallas_call(functools.partial(conv_kernel_body, pad, pieces), grid=(co...  6.17 us
  transfers between devices with their start and end apart: 24, of which 13 were waited for; matrix products, arithmetic and copies ran while one was open for 5% of the time, Pallas kernels for 26%

profile of v2, /device:TPU:0, one launch (start us, length us, event | category | flops | bytes accessed | tf_op | source)
XLA Modules:
  0.0 174.2 jit_solution(12551313411571188531)
XLA Ops:
  0.6 1.2 constant_dynamic-slice_fusion
  1.9 3.0 %collective-permute-start.1 = (bf16[128,1024]{1,0:T(8,128)(2,1)S(1)}, bf16[128,1024]{1,0:T(8,128)(2,1)S(1)}, u32[]{:S(2)}, u32[]{:S(2)}) collective-permute-start(bf16[128,1024]{1,0:T(8,128)(2,1)S(1)} %get-tuple-element.51), channel_id=1, source_target_pairs={{0,1},{1,0},{2,3},{3,2},{4,5},{5,4},{6,7},{7,6},{8,9},{9,8},{10,11... | collective-permute-start | bytes 786440 | tf_op jit(solution)/shard_map/ppermute | solution.py:25
  4.9 0.7 convert_element_type.43
  5.8 1.6 collective-permute-start.7
  7.3 3.8 %collective-permute-done.1 = bf16[128,1024]{1,0:T(8,128)(2,1)S(1)} collective-permute-done((bf16[128,1024]{1,0:T(8,128)(2,1)S(1)}, bf16[128,1024]{1,0:T(8,128)(2,1)S(1)}, u32[]{:S(2)}, u32[]{:S(2)}) %collective-permute-start.1) | collective-permute-done | bytes 262176 | tf_op jit(solution)/shard_map/ppermute | solution.py:25
  11.2 1.8 %collective-permute-start.2 = (bf16[256,1024]{1,0:T(8,128)(2,1)S(1)}, bf16[256,1024]{1,0:T(8,128)(2,1)S(1)}, u32[]{:S(2)}, u32[]{:S(2)}) collective-permute-start(bf16[256,1024]{1,0:T(8,128)(2,1)S(1)} %pad_maximum_fusion.3), channel_id=1, source_target_pairs={{0,2},{1,3},{2,0},{3,1},{4,6},{5,7},{6,4},{7,5},{8,10},{9,11},{10,... | collective-permute-start | bytes 1572872 | tf_op jit(solution)/shard_map/ppermute | solution.py:25
  13.1 2.3 %collective-permute-done.7 = bf16[128,1152]{1,0:T(8,128)(2,1)S(1)} collective-permute-done((bf16[128,1152]{1,0:T(8,128)(2,1)S(1)}, bf16[128,1152]{1,0:T(8,128)(2,1)S(1)}, u32[]{:S(2)}, u32[]{:S(2)}) %collective-permute-start.7) | collective-permute-done | bytes 294944 | tf_op jit(solution)/shard_map/ppermute | solution.py:25
  15.5 1.0 dynamic-slice_bitcast_fusion
  16.5 2.7 %collective-permute-start = (bf16[64,2048]{1,0:T(8,128)(2,1)S(1)}, bf16[64,2048]{1,0:T(8,128)(2,1)S(1)}, u32[]{:S(2)}, u32[]{:S(2)}) collective-permute-start(bf16[64,2048]{1,0:T(8,128)(2,1)S(1)} %dynamic-slice_bitcast_fusion), channel_id=1, source_target_pairs={{0,16},{4,20},{8,24},{12,28},{16,0},{20,4},{24,8},{28,12},{1,17},{... | collective-permute-start | bytes 786440 | tf_op jit(solution)/shard_map/ppermute | solution.py:20
  19.2 1.5 fusion.6
  20.7 1.6 collective-permute-start.5
  22.4 3.2 %collective-permute-done.2 = bf16[256,1024]{1,0:T(8,128)(2,1)S(1)} collective-permute-done((bf16[256,1024]{1,0:T(8,128)(2,1)S(1)}, bf16[256,1024]{1,0:T(8,128)(2,1)S(1)}, u32[]{:S(2)}, u32[]{:S(2)}) %collective-permute-start.2) | collective-permute-done | bytes 524320 | tf_op jit(solution)/shard_map/ppermute | solution.py:25
  25.5 1.1 pad_maximum_fusion.1.refs_0_
  26.6 1.7 collective-permute-done.8
  28.5 1.3 slice.83
  29.8 0.9 collective-permute-start.3
  30.7 7.8 %collective-permute-done.3.refs_1_ = bf16[64,2048]{1,0:T(8,128)(2,1)S(1)} collective-permute-done((bf16[64,2048]{1,0:T(8,128)(2,1)S(1)}, bf16[64,2048]{1,0:T(8,128)(2,1)S(1)}, u32[]{:S(2)}, u32[]{:S(2)}) %collective-permute-start.3) | collective-permute-done | bytes 262176 | tf_op jit(solution)/shard_map/ppermute | solution.py:25
  38.5 0.9 pad_maximum_fusion.4
  39.4 1.5 collective-permute-start.4
  41.6 0.7 pad_add_fusion.where
  42.3 11.1 %collective-permute-done.4.refs_2_ = bf16[128,2048]{1,0:T(8,128)(2,1)} collective-permute-done((bf16[128,2048]{1,0:T(8,128)(2,1)}, bf16[128,2048]{1,0:T(8,128)(2,1)}, u32[]{:S(2)}, u32[]{:S(2)}) %collective-permute-start.4) | collective-permute-done | bytes 524320 | tf_op jit(solution)/shard_map/ppermute | solution.py:25
  53.3 1.6 collective-permute-start.12
  54.9 22.0 %hidden_units.1 = (bf16[512,1536]{1,0:T(8,128)(2,1)}, f32[512,128]{1,0:T(8,128)}) custom-call(s32[3]{0:T(128)} %pad_add_fusion.where, bf16[512,1024]{1,0:T(8,128)(2,1)} %pad_maximum_fusion.1.refs_0_, bf16[512,1152]{1,0:T(8,128)(2,1)} %copy-done.1, bf16[512,1024]{1,0:T(8,128)(2,1)} %collective-permute-done.9.refs_2_, ...), custom_call_target="tpu_custom_call" | custom-call | flops 12884901888 | bytes 33554432 | tf_op jit(solution)/shard_map/hidden_units/pallas_call | solution.py:207
  77.0 1.0 copy-done.8
  78.0 6.8 %half_product.2 = (f32[256,1024]{1,0:T(8,128)}, bf16[256,1024]{1,0:T(8,128)(2,1)}) custom-call(s32[2]{0:T(128)} %pad_add_fusion.1.where, bf16[1,256,4096]{2,1,0:T(8,128)(2,1)} %window.3, bf16[64,2048]{1,0:T(8,128)(2,1)} %copy-done.3, bf16[64,2048]{1,0:T(8,128)(2,1)} %copy-done.4, bf16[128,2048]{1,0:T(8,128)(2,1)} %collective-permute-done.4.refs_2_, ...), custom_call_target="tpu_custom_call" | custom-call | flops 2147483648 | bytes 7864320 | tf_op jit(solution)/shard_map/half_product/pallas_call | solution.py:82
  84.8 14.3 %down_units.1 = (bf16[512,2048]{1,0:T(8,128)(2,1)}, f32[512,2048]{1,0:T(8,128)}) custom-call(s32[3]{0:T(128)} %pad_add_fusion.where, bf16[512,1536]{1,0:T(8,128)(2,1)} %get-tuple-element.26.hidden, f32[512,128]{1,0:T(8,128)} %get-tuple-element.27.scale, bf16[1,1536,4096]{2,1,0:T(8,128)(2,1)} %down.1), custom_call_target="tpu_custom_call" | custom-call | flops 6442450944 | bytes 18350080 | tf_op jit(solution)/shard_map/down_units/pallas_call | solution.py:253
  99.6 5.1 %collective-permute-done.13.refs_6_ = bf16[512,1024]{1,0:T(8,128)(2,1)S(1)} collective-permute-done((bf16[512,1024]{1,0:T(8,128)(2,1)S(1)}, bf16[512,1024]{1,0:T(8,128)(2,1)S(1)}, u32[]{:S(2)}, u32[]{:S(2)}) %collective-permute-start.13) | collective-permute-done | bytes 1048608 | tf_op jit(solution)/shard_map/ppermute | solution.py:20
  104.7 1.0 copy-done.9
  105.7 7.2 %half_product.3 = (f32[256,1024]{1,0:T(8,128)}, bf16[256,1024]{1,0:T(8,128)(2,1)}) custom-call(s32[2]{0:T(128)} %pad_add_fusion.1.where, bf16[1,256,4096]{2,1,0:T(8,128)(2,1)} %window.3, bf16[64,2048]{1,0:T(8,128)(2,1)} %copy-done.3, bf16[64,2048]{1,0:T(8,128)(2,1)} %copy-done.4, bf16[128,2048]{1,0:T(8,128)(2,1)} %collective-permute-done.4.refs_2_, ...), custom_call_target="tpu_custom_call" | custom-call | flops 2147483648 | bytes 7864320 | tf_op jit(solution)/shard_map/half_product/pallas_call | solution.py:82
  114.6 1.5 collective-permute-start.16
  116.2 2.4 %collective-permute-start.17 = (bf16[256,1024]{1,0:T(8,128)(2,1)S(1)}, bf16[256,1024]{1,0:T(8,128)(2,1)S(1)}, u32[]{:S(2)}, u32[]{:S(2)}) collective-permute-start(bf16[256,1024]{1,0:T(8,128)(2,1)S(1)} %copy-done.17), channel_id=1, source_target_pairs={{0,16},{4,20},{8,24},{12,28},{16,0},{20,4},{24,8},{28,12},{1,17},{... | collective-permute-start | bytes 1572872 | tf_op jit(solution)/shard_map/ppermute | solution.py:20
  119.1 8.9 %collective-permute-done.18 = bf16[256,1024]{1,0:T(8,128)(2,1)S(1)} collective-permute-done((bf16[256,1024]{1,0:T(8,128)(2,1)S(1)}, bf16[256,1024]{1,0:T(8,128)(2,1)S(1)}, u32[]{:S(2)}, u32[]{:S(2)}) %collective-permute-start.18) | collective-permute-done | bytes 524320 | tf_op jit(solution)/shard_map/ppermute | solution.py:25
  128.3 1.3 fusion.1
  129.6 1.5 collective-permute-start.19
  131.1 1.5 collective-permute-start.20
  132.6 4.2 %collective-permute-done.19.refs_1_ = bf16[128,1024]{1,0:T(8,128)(2,1)S(1)} collective-permute-done((bf16[128,1024]{1,0:T(8,128)(2,1)S(1)}, bf16[128,1024]{1,0:T(8,128)(2,1)S(1)}, u32[]{:S(2)}, u32[]{:S(2)}) %collective-permute-start.19) | collective-permute-done | bytes 262176 | tf_op jit(solution)/shard_map/ppermute | solution.py:25
  136.8 1.3 collective-permute-done.20.refs_3_
  138.1 0.7 copy-done.16
  138.8 2.3 %collect.1 = (f32[128,512]{1,0:T(8,128)}, bf16[128,512]{1,0:T(8,128)(2,1)}, bf16[128,512]{1,0:T(8,128)(2,1)}, bf16[128,512]{1,0:T(8,128)(2,1)}) custom-call(s32[3]{0:T(128)} %pad_add_fusion.where, f32[128,1024]{1,0:T(8,128)} %get-tuple-element.44.refs_0_, bf16[128,1024]{1,0:T(8,128)(2,1)} %copy-done.15, f32[128,1024]{1,0:T(8,128)} %get-tuple-element.41.refs_2_, ...), custom_call_target="tpu_custom_call" | custom-call | tf_op jit(solution)/shard_map/collect/pallas_call | solution.py:299
  141.4 2.6 %collective-permute-start.22 = (bf16[128,512]{1,0:T(8,128)(2,1)}, bf16[128,512]{1,0:T(8,128)(2,1)S(1)}, u32[]{:S(2)}, u32[]{:S(2)}) collective-permute-start(bf16[128,512]{1,0:T(8,128)(2,1)} %get-tuple-element.38), channel_id=1, source_target_pairs={{0,16},{4,20},{8,24},{12,28},{16,0},{20,4},{24,8},{28,12},{1,17},{... | collective-permute-start | bytes 393224 | tf_op jit(solution)/shard_map/ppermute | solution.py:20
  144.0 1.5 collective-permute-start.23
  145.5 12.8 %collective-permute-done.17.back = bf16[256,1024]{1,0:T(8,128)(2,1)S(1)} collective-permute-done((bf16[256,1024]{1,0:T(8,128)(2,1)S(1)}, bf16[256,1024]{1,0:T(8,128)(2,1)S(1)}, u32[]{:S(2)}, u32[]{:S(2)}) %collective-permute-start.17) | collective-permute-done | bytes 524320 | tf_op jit(solution)/shard_map/ppermute | solution.py:20
  158.3 0.8 copy-done.13
  159.2 3.1 %conv.2.refs_0_ = bf16[1,256,2048]{2,1,0:T(8,128)(2,1)} custom-call(s32[3]{0:T(128)} %pad_add_fusion.where, f32[256,1024]{1,0:T(8,128)} %get-tuple-element.35.own, bf16[256,1024]{1,0:T(8,128)(2,1)} %copy-done.13, bf16[1,3,2048]{2,1,0:T(4,128)(2,1)} %state.3, f32[4,2048]{1,0:T(4,128)} %taps.3, f32[1,2048]{1,0:T(1,128)} %bitcast.39), custom_call_target="tpu_custom_call" | custom-call | flops 3145728 | bytes 2097152 | tf_op jit(solution)/shard_map/conv/pallas_call | solution.py:145
  162.2 7.3 %collective-permute-done.14.back = bf16[256,1024]{1,0:T(8,128)(2,1)S(1)} collective-permute-done((bf16[256,1024]{1,0:T(8,128)(2,1)S(1)}, bf16[256,1024]{1,0:T(8,128)(2,1)S(1)}, u32[]{:S(2)}, u32[]{:S(2)}) %collective-permute-start.14) | collective-permute-done | bytes 524320 | tf_op jit(solution)/shard_map/ppermute | solution.py:20
  169.6 0.8 copy-done.12
  170.4 3.1 %conv.3 = bf16[1,256,2048]{2,1,0:T(8,128)(2,1)} custom-call(s32[3]{0:T(128)} %pad_add_fusion.where, f32[256,1024]{1,0:T(8,128)} %get-tuple-element.30.own, bf16[256,1024]{1,0:T(8,128)(2,1)} %copy-done.12, bf16[1,3,2048]{2,1,0:T(4,128)(2,1)} %state.3, f32[4,2048]{1,0:T(4,128)} %taps.3, f32[1,2048]{1,0:T(1,128)} %bitcast.40, ...), custom_call_target="tpu_custom_call", output_to_operand_aliasing={{}: (6, {})} | custom-call | flops 3145728 | bytes 2097152 | tf_op jit(solution)/shard_map/conv/pallas_call | solution.py:145
  173.5 0.7 add_convert_fusion
  (68 shorter events, 4.4 us)
Async XLA Ops:
  0.6 18.5 %copy-start = (bf16[512,2048]{1,0:T(8,128)(2,1)S(1)}, bf16[512,2048]{1,0:T(8,128)(2,1)}, u32[]{:S(2)}) copy-start(bf16[512,2048]{1,0:T(8,128)(2,1)} %refs_3_.3) | copy-start | bytes 6291460
  1.9 9.3 %collective-permute-start.1 = (bf16[128,1024]{1,0:T(8,128)(2,1)S(1)}, bf16[128,1024]{1,0:T(8,128)(2,1)S(1)}, u32[]{:S(2)}, u32[]{:S(2)}) collective-permute-start(bf16[128,1024]{1,0:T(8,128)(2,1)S(1)} %get-tuple-element.51), channel_id=1, source_target_pairs={{0,1},{1,0},{2,3},{3,2},{4,5},{5,4},{6,7},{7,6},{8,9},{9,8},{10,11... | collective-permute-start | bytes 786440 | tf_op jit(solution)/shard_map/ppermute | solution.py:25
  5.7 15.0 %copy-start.10 = (bf16[128,128]{1,0:T(8,128)(2,1)}, bf16[128,128]{1,0:T(8,128)(2,1)S(1)}, u32[]{:S(2)}) copy-start(bf16[128,128]{1,0:T(8,128)(2,1)S(1)} %pad.4) | copy-start | bytes 98308
  5.8 9.6 %collective-permute-start.7 = (bf16[128,1152]{1,0:T(8,128)(2,1)S(1)}, bf16[128,1152]{1,0:T(8,128)(2,1)S(1)}, u32[]{:S(2)}, u32[]{:S(2)}) collective-permute-start(bf16[128,1152]{1,0:T(8,128)(2,1)S(1)} %pad_maximum_fusion.6), channel_id=1, source_target_pairs={{0,2},{1,3},{2,0},{3,1},{4,6},{5,7},{6,4},{7,5},{8,10},{9,11},{10,... | collective-permute-start | bytes 884744 | tf_op jit(solution)/shard_map/ppermute | solution.py:25
  11.2 14.3 %collective-permute-start.2 = (bf16[256,1024]{1,0:T(8,128)(2,1)S(1)}, bf16[256,1024]{1,0:T(8,128)(2,1)S(1)}, u32[]{:S(2)}, u32[]{:S(2)}) collective-permute-start(bf16[256,1024]{1,0:T(8,128)(2,1)S(1)} %pad_maximum_fusion.3), channel_id=1, source_target_pairs={{0,2},{1,3},{2,0},{3,1},{4,6},{5,7},{6,4},{7,5},{8,10},{9,11},{10,... | collective-permute-start | bytes 1572872 | tf_op jit(solution)/shard_map/ppermute | solution.py:25
  15.3 5.4 %copy-start.5 = (bf16[128,1152]{1,0:T(8,128)(2,1)}, bf16[128,1152]{1,0:T(8,128)(2,1)S(1)}, u32[]{:S(2)}) copy-start(bf16[128,1152]{1,0:T(8,128)(2,1)S(1)} %collective-permute-done.7) | copy-start | bytes 884740
  15.4 12.9 %collective-permute-start.8 = (bf16[256,1152]{1,0:T(8,128)(2,1)S(1)}, bf16[256,1152]{1,0:T(8,128)(2,1)S(1)}, u32[]{:S(2)}, u32[]{:S(2)}) collective-permute-start(bf16[256,1152]{1,0:T(8,128)(2,1)S(1)} %pad_maximum_fusion.2), channel_id=1, source_target_pairs={{0,1},{1,0},{2,3},{3,2},{4,5},{5,4},{6,7},{7,6},{8,9},{9,8},{10,11... | collective-permute-start | bytes 1769480 | tf_op jit(solution)/shard_map/ppermute | solution.py:25
  16.5 13.3 %collective-permute-start = (bf16[64,2048]{1,0:T(8,128)(2,1)S(1)}, bf16[64,2048]{1,0:T(8,128)(2,1)S(1)}, u32[]{:S(2)}, u32[]{:S(2)}) collective-permute-start(bf16[64,2048]{1,0:T(8,128)(2,1)S(1)} %dynamic-slice_bitcast_fusion), channel_id=1, source_target_pairs={{0,16},{4,20},{8,24},{12,28},{16,0},{20,4},{24,8},{28,12},{1,17},{... | collective-permute-start | bytes 786440 | tf_op jit(solution)/shard_map/ppermute | solution.py:20
  19.2 35.7 %collective-permute-start.6 = (bf16[512,2048]{1,0:T(8,128)(2,1)S(1)}, bf16[512,2048]{1,0:T(8,128)(2,1)}, u32[]{:S(2)}, u32[]{:S(2)}) collective-permute-start(bf16[512,2048]{1,0:T(8,128)(2,1)S(1)} %copy-done), channel_id=1, source_target_pairs={{0,4},{4,0},{8,12},{12,8},{16,20},{20,16},{24,28},{28,24},{1,5},{5... | collective-permute-start | bytes 6291464 | tf_op jit(solution)/shard_map/ppermute | solution.py:20
  20.7 7.6 %copy-start.6 = (bf16[128,1152]{1,0:T(8,128)(2,1)S(1)}, bf16[128,1152]{1,0:T(8,128)(2,1)}, u32[]{:S(2)}) copy-start(bf16[128,1152]{1,0:T(8,128)(2,1)} %copy-done.5) | copy-start | bytes 884740
  20.7 7.6 %copy-start.11 = (bf16[128,128]{1,0:T(8,128)(2,1)S(1)}, bf16[128,128]{1,0:T(8,128)(2,1)}, u32[]{:S(2)}) copy-start(bf16[128,128]{1,0:T(8,128)(2,1)} %copy-done.10) | copy-start | bytes 98308
  20.7 34.2 %collective-permute-start.5 = (bf16[512,1024]{1,0:T(8,128)(2,1)}, bf16[512,1024]{1,0:T(8,128)(2,1)}, u32[]{:S(2)}, u32[]{:S(2)}) collective-permute-start(bf16[512,1024]{1,0:T(8,128)(2,1)} %get-tuple-element.49), channel_id=1, source_target_pairs={{0,8},{4,12},{8,0},{12,4},{16,24},{20,28},{24,16},{28,20},{1,9},{5... | collective-permute-start | bytes 3145736 | tf_op jit(solution)/shard_map/ppermute | solution.py:20
  26.6 28.3 %collective-permute-start.9 = (bf16[512,1024]{1,0:T(8,128)(2,1)}, bf16[512,1024]{1,0:T(8,128)(2,1)}, u32[]{:S(2)}, u32[]{:S(2)}) collective-permute-start(bf16[512,1024]{1,0:T(8,128)(2,1)} %pad_maximum_fusion.1.refs_0_), channel_id=1, source_target_pairs={{0,4},{4,0},{8,12},{12,8},{16,20},{20,16},{24,28},{28,24},{1,5},{5... | collective-permute-start | bytes 3145736 | tf_op jit(solution)/shard_map/ppermute | solution.py:20
  28.5 26.5 %copy-start.1 = (bf16[512,1152]{1,0:T(8,128)(2,1)}, bf16[512,1152]{1,0:T(8,128)(2,1)S(1)}, u32[]{:S(2)}) copy-start(bf16[512,1152]{1,0:T(8,128)(2,1)S(1)} %pad_maximum_fusion.refs_1_) | copy-start | bytes 3538948
  29.8 25.1 %collective-permute-start.10 = (bf16[512,1024]{1,0:T(8,128)(2,1)}, bf16[512,1024]{1,0:T(8,128)(2,1)}, u32[]{:S(2)}, u32[]{:S(2)}) collective-permute-start(bf16[512,1024]{1,0:T(8,128)(2,1)} %slice.83), channel_id=1, source_target_pairs={{0,4},{4,0},{8,12},{12,8},{16,20},{20,16},{24,28},{28,24},{1,5},{5... | collective-permute-start | bytes 3145736 | tf_op jit(solution)/shard_map/ppermute | solution.py:20
  29.8 8.7 %copy-start.3 = (bf16[64,2048]{1,0:T(8,128)(2,1)}, bf16[64,2048]{1,0:T(8,128)(2,1)S(1)}, u32[]{:S(2)}) copy-start(bf16[64,2048]{1,0:T(8,128)(2,1)S(1)} %collective-permute-done.refs_0_) | copy-start | bytes 786436
  29.8 8.7 %collective-permute-start.3 = (bf16[64,2048]{1,0:T(8,128)(2,1)S(1)}, bf16[64,2048]{1,0:T(8,128)(2,1)S(1)}, u32[]{:S(2)}, u32[]{:S(2)}) collective-permute-start(bf16[64,2048]{1,0:T(8,128)(2,1)S(1)} %collective-permute-done.refs_0_), channel_id=1, source_target_pairs={{0,1},{1,0},{2,3},{3,2},{4,5},{5,4},{6,7},{7,6},{8,9},{9,8},{10,11... | collective-permute-start | bytes 786440 | tf_op jit(solution)/shard_map/ppermute | solution.py:25
  38.5 38.5 %copy-start.4 = (bf16[64,2048]{1,0:T(8,128)(2,1)}, bf16[64,2048]{1,0:T(8,128)(2,1)S(1)}, u32[]{:S(2)}) copy-start(bf16[64,2048]{1,0:T(8,128)(2,1)S(1)} %collective-permute-done.3.refs_1_) | copy-start | bytes 786436
  39.4 13.9 %collective-permute-start.4 = (bf16[128,2048]{1,0:T(8,128)(2,1)}, bf16[128,2048]{1,0:T(8,128)(2,1)}, u32[]{:S(2)}, u32[]{:S(2)}) collective-permute-start(bf16[128,2048]{1,0:T(8,128)(2,1)} %pad_maximum_fusion.4), channel_id=1, source_target_pairs={{0,2},{1,3},{2,0},{3,1},{4,6},{5,7},{6,4},{7,5},{8,10},{9,11},{10,... | collective-permute-start | bytes 1572872 | tf_op jit(solution)/shard_map/ppermute | solution.py:25
  53.3 31.4 %collective-permute-start.12 = (bf16[512,1024]{1,0:T(8,128)(2,1)}, bf16[512,1024]{1,0:T(8,128)(2,1)S(1)}, u32[]{:S(2)}, u32[]{:S(2)}) collective-permute-start(bf16[512,1024]{1,0:T(8,128)(2,1)} %get-tuple-element.25), channel_id=1, source_target_pairs={{0,8},{4,12},{8,0},{12,4},{16,24},{20,28},{24,16},{28,20},{1,9},{5... | collective-permute-start | bytes 3145736 | tf_op jit(solution)/shard_map/ppermute | solution.py:20
  54.9 22.1 %collective-permute-start.11 = (bf16[512,1024]{1,0:T(8,128)(2,1)}, bf16[512,1024]{1,0:T(8,128)(2,1)S(1)}, u32[]{:S(2)}, u32[]{:S(2)}) collective-permute-start(bf16[512,1024]{1,0:T(8,128)(2,1)} %collective-permute-done.5.refs_5_), channel_id=1, source_target_pairs={{0,4},{4,0},{8,12},{12,8},{16,20},{20,16},{24,28},{28,24},{1,5},{5... | collective-permute-start | bytes 3145736 | tf_op jit(solution)/shard_map/ppermute | solution.py:20
  77.0 1.0 copy-start.8
  84.8 14.7 %copy-start.7 = (bf16[512,1024]{1,0:T(8,128)(2,1)}, bf16[512,1024]{1,0:T(8,128)(2,1)S(1)}, u32[]{:S(2)}) copy-start(bf16[512,1024]{1,0:T(8,128)(2,1)S(1)} %collective-permute-done.12.refs_5_) | copy-start | bytes 3145732
  99.0 13.9 %collective-permute-start.15 = (bf16[512,2048]{1,0:T(8,128)(2,1)}, bf16[512,2048]{1,0:T(8,128)(2,1)S(1)}, u32[]{:S(2)}, u32[]{:S(2)}) collective-permute-start(bf16[512,2048]{1,0:T(8,128)(2,1)} %get-tuple-element.33), channel_id=1, source_target_pairs={{0,4},{4,0},{8,12},{12,8},{16,20},{20,16},{24,28},{28,24},{1,5},{5... | collective-permute-start | bytes 6291464 | tf_op jit(solution)/shard_map/ppermute | solution.py:20
  99.4 5.3 %collective-permute-start.13 = (bf16[512,1024]{1,0:T(8,128)(2,1)S(1)}, bf16[512,1024]{1,0:T(8,128)(2,1)S(1)}, u32[]{:S(2)}, u32[]{:S(2)}) collective-permute-start(bf16[512,1024]{1,0:T(8,128)(2,1)S(1)} %collective-permute-done.12.refs_5_), channel_id=1, source_target_pairs={{0,4},{4,0},{8,12},{12,8},{16,20},{20,16},{24,28},{28,24},{1,5},{5... | collective-permute-start | bytes 3145736 | tf_op jit(solution)/shard_map/ppermute | solution.py:20
  104.7 1.0 copy-start.9
  105.7 7.2 %copy-start.2 = (f32[512,2048]{1,0:T(8,128)S(1)}, f32[512,2048]{1,0:T(8,128)}, u32[]{:S(2)}) copy-start(f32[512,2048]{1,0:T(8,128)} %get-tuple-element.28) | copy-start | bytes 12582916
  113.9 2.3 %copy-start.17 = (bf16[256,1024]{1,0:T(8,128)(2,1)S(1)}, bf16[256,1024]{1,0:T(8,128)(2,1)}, u32[]{:S(2)}) copy-start(bf16[256,1024]{1,0:T(8,128)(2,1)} %get-tuple-element.24) | copy-start | bytes 1572868
  113.9 4.7 %copy-start.18 = (bf16[256,1024]{1,0:T(8,128)(2,1)S(1)}, bf16[256,1024]{1,0:T(8,128)(2,1)}, u32[]{:S(2)}) copy-start(bf16[256,1024]{1,0:T(8,128)(2,1)} %get-tuple-element.31) | copy-start | bytes 1572868
  114.0 14.0 %collective-permute-start.18 = (bf16[256,1024]{1,0:T(8,128)(2,1)S(1)}, bf16[256,1024]{1,0:T(8,128)(2,1)S(1)}, u32[]{:S(2)}, u32[]{:S(2)}) collective-permute-start(bf16[256,1024]{1,0:T(8,128)(2,1)S(1)} %pad_maximum_fusion.5), channel_id=1, source_target_pairs={{0,1},{1,0},{2,3},{3,2},{4,5},{5,4},{6,7},{7,6},{8,9},{9,8},{10,11... | collective-permute-start | bytes 1572872 | tf_op jit(solution)/shard_map/ppermute | solution.py:25
  114.6 13.6 %collective-permute-start.16 = (bf16[256,1024]{1,0:T(8,128)(2,1)S(1)}, bf16[256,1024]{1,0:T(8,128)(2,1)S(1)}, u32[]{:S(2)}, u32[]{:S(2)}) collective-permute-start(bf16[256,1024]{1,0:T(8,128)(2,1)S(1)} %bitcast.37), channel_id=1, source_target_pairs={{0,2},{1,3},{2,0},{3,1},{4,6},{5,7},{6,4},{7,5},{8,10},{9,11},{10,... | collective-permute-start | bytes 1572872 | tf_op jit(solution)/shard_map/ppermute | solution.py:25
  116.2 42.2 %collective-permute-start.17 = (bf16[256,1024]{1,0:T(8,128)(2,1)S(1)}, bf16[256,1024]{1,0:T(8,128)(2,1)S(1)}, u32[]{:S(2)}, u32[]{:S(2)}) collective-permute-start(bf16[256,1024]{1,0:T(8,128)(2,1)S(1)} %copy-done.17), channel_id=1, source_target_pairs={{0,16},{4,20},{8,24},{12,28},{16,0},{20,4},{24,8},{28,12},{1,17},{... | collective-permute-start | bytes 1572872 | tf_op jit(solution)/shard_map/ppermute | solution.py:20
  118.6 51.0 %collective-permute-start.14 = (bf16[256,1024]{1,0:T(8,128)(2,1)S(1)}, bf16[256,1024]{1,0:T(8,128)(2,1)S(1)}, u32[]{:S(2)}, u32[]{:S(2)}) collective-permute-start(bf16[256,1024]{1,0:T(8,128)(2,1)S(1)} %copy-done.18), channel_id=1, source_target_pairs={{0,16},{4,20},{8,24},{12,28},{16,0},{20,4},{24,8},{28,12},{1,17},{... | collective-permute-start | bytes 1572872 | tf_op jit(solution)/shard_map/ppermute | solution.py:20
  129.6 7.2 %collective-permute-start.19 = (bf16[128,1024]{1,0:T(8,128)(2,1)S(1)}, bf16[128,1024]{1,0:T(8,128)(2,1)S(1)}, u32[]{:S(2)}, u32[]{:S(2)}) collective-permute-start(bf16[128,1024]{1,0:T(8,128)(2,1)S(1)} %get-tuple-element.45), channel_id=1, source_target_pairs={{0,2},{1,3},{2,0},{3,1},{4,6},{5,7},{6,4},{7,5},{8,10},{9,11},{10,... | collective-permute-start | bytes 786440 | tf_op jit(solution)/shard_map/ppermute | solution.py:25
  131.1 7.0 %collective-permute-start.20 = (bf16[128,1024]{1,0:T(8,128)(2,1)S(1)}, bf16[128,1024]{1,0:T(8,128)(2,1)S(1)}, u32[]{:S(2)}, u32[]{:S(2)}) collective-permute-start(bf16[128,1024]{1,0:T(8,128)(2,1)S(1)} %get-tuple-element.40), channel_id=1, source_target_pairs={{0,1},{1,0},{2,3},{3,2},{4,5},{5,4},{6,7},{7,6},{8,9},{9,8},{10,11... | collective-permute-start | bytes 786440 | tf_op jit(solution)/shard_map/ppermute | solution.py:25
  136.8 1.3 copy-start.15
  138.1 0.7 copy-start.16
  141.1 32.4 %collective-permute-start.21 = (bf16[128,512]{1,0:T(8,128)(2,1)}, bf16[128,512]{1,0:T(8,128)(2,1)S(1)}, u32[]{:S(2)}, u32[]{:S(2)}) collective-permute-start(bf16[128,512]{1,0:T(8,128)(2,1)} %get-tuple-element.37), channel_id=1, source_target_pairs={{0,8},{4,12},{8,0},{12,4},{16,24},{20,28},{24,16},{28,20},{1,9},{5... | collective-permute-start | bytes 393224 | tf_op jit(solution)/shard_map/ppermute | solution.py:20
  141.4 32.1 %collective-permute-start.22 = (bf16[128,512]{1,0:T(8,128)(2,1)}, bf16[128,512]{1,0:T(8,128)(2,1)S(1)}, u32[]{:S(2)}, u32[]{:S(2)}) collective-permute-start(bf16[128,512]{1,0:T(8,128)(2,1)} %get-tuple-element.38), channel_id=1, source_target_pairs={{0,16},{4,20},{8,24},{12,28},{16,0},{20,4},{24,8},{28,12},{1,17},{... | collective-permute-start | bytes 393224 | tf_op jit(solution)/shard_map/ppermute | solution.py:20
  144.0 29.5 %collective-permute-start.23 = (bf16[128,512]{1,0:T(8,128)(2,1)}, bf16[128,512]{1,0:T(8,128)(2,1)S(1)}, u32[]{:S(2)}, u32[]{:S(2)}) collective-permute-start(bf16[128,512]{1,0:T(8,128)(2,1)} %get-tuple-element.39), channel_id=1, source_target_pairs={{0,24},{4,28},{8,16},{12,20},{16,8},{20,12},{24,0},{28,4},{1,25},{... | collective-permute-start | bytes 393224 | tf_op jit(solution)/shard_map/ppermute | solution.py:20
  158.3 0.8 copy-start.13
  162.2 11.2 %copy-start.14 = (f32[128,512]{1,0:T(8,128)S(1)}, f32[128,512]{1,0:T(8,128)}, u32[]{:S(2)}) copy-start(f32[128,512]{1,0:T(8,128)} %get-tuple-element.36) | copy-start | bytes 786436
  169.6 0.8 copy-start.12

commit v3 on v2

--- a/solution.py
+++ b/solution.py
@@ -1,4 +1,5 @@
 import functools
+import math
 
 import jax
 import jax.numpy as jnp
@@ -10,9 +11,10 @@
 F32 = jnp.float32
 BF16 = jnp.bfloat16
 LANES = 128
-VMEM = 56 << 20
+VMEM = 24 << 20
+VMEM_ALL = 56 << 20
 SMEM_SPEC = pl.BlockSpec(memory_space=pltpu.SMEM)
-CHUNKS = 2
+CHUNKS = (1, 1, 2)
 
 
 def xor_send(value, mask):
@@ -72,7 +74,7 @@
 def half_product(where, window, fars, weights, offset, cols):
     tokens, features = window.shape[1], fars[0].shape[1]
     depth = weights[0].shape[0]
-    tile = tile_of(cols, 512)
+    tile = math.gcd(offset, cols, 512)
     base = offset // tile
 
     def spec(weight):
@@ -124,7 +126,7 @@
 
 def conv(where, pieces, own, back, state, taps, bias, offset, channels, earlier):
     tokens, cols = own.shape
-    tile = tile_of(cols, 512)
+    tile = math.gcd(offset, cols, 512)
     base = offset // tile
     count = taps.shape[0]
     pad = 8
@@ -162,7 +164,7 @@
 
 def hidden_kernel(quarter, where, *refs):
     inputs, router, gates, ups = refs[:4], refs[4], refs[5:9], refs[9:13]
-    hidden, scale = refs[13:]
+    hidden, *scales = refs[13:]
     gated = raised = None
     for source, gate, up in zip(inputs, gates, ups):
         rows = source[:, :quarter]
@@ -170,6 +172,9 @@
         gated = one if gated is None else gated + one
         raised = two if raised is None else raised + two
     hidden[...] = (jax.nn.silu(gated) * raised).astype(BF16)
+
+    if not scales:
+        return
 
     @pl.when(pl.program_id(0) == 0)
     def _():
@@ -189,17 +194,19 @@
         mixed = jnp.where(ids_a == owner, weight, 0.0) + jnp.where(
             ids_b == owner, 1.0 - weight, 0.0
         )
-        scale[...] = jnp.broadcast_to(mixed, scale.shape)
-
-
-def hidden_units(where, inputs, router, w_gate, w_up):
+        scales[0][...] = jnp.broadcast_to(mixed, scales[0].shape)
+
+
+def hidden_units(where, inputs, router, w_gate, w_up, offset, units):
     rows, quarter = inputs[0].shape
-    width, units = w_gate.shape[1:]
-    tile = tile_of(units, 256)
+    width = w_gate.shape[1]
+    tile = math.gcd(offset, units, 256)
+    base = offset // tile
+    count = 1 if offset else 2
 
     def spec(number):
         def place(i, where):
-            return 0, 2 * where[0] + number if number < 2 else 2 - 2 * where[0] + number - 2, i
+            return 0, 2 * where[0] + number if number < 2 else 2 - 2 * where[0] + number - 2, base + i
 
         return pl.BlockSpec((1, quarter, tile), place)
 
@@ -213,13 +220,13 @@
             out_specs=[
                 pl.BlockSpec((rows, tile), lambda i, where: (0, i)),
                 pl.BlockSpec((rows, LANES), lambda i, where: (0, 0)),
-            ],
+            ][:count],
         ),
         out_shape=[
             jax.ShapeDtypeStruct((rows, units), BF16),
             jax.ShapeDtypeStruct((rows, LANES), F32),
-        ],
-        compiler_params=pltpu.CompilerParams(vmem_limit_bytes=VMEM),
+        ][:count],
+        compiler_params=pltpu.CompilerParams(vmem_limit_bytes=VMEM_ALL),
         cost_estimate=pl.CostEstimate(
             flops=4 * rows * width * units,
             transcendentals=rows * units,
@@ -242,8 +249,8 @@
 
 
 def down_units(where, hidden, scale, w_down, final):
-    rows, units = hidden.shape
-    width = w_down.shape[2]
+    rows = hidden.shape[0]
+    units, width = w_down.shape[1:]
     steps = width // final // 2
 
     def place(i, where):
@@ -256,8 +263,8 @@
             num_scalar_prefetch=1,
             grid=(2 * steps,),
             in_specs=[
-                pl.BlockSpec(hidden.shape, lambda i, where: (0, 0)),
-                pl.BlockSpec(scale.shape, lambda i, where: (0, 0)),
+                whole(hidden),
+                whole(scale),
                 pl.BlockSpec((1, units, final), place),
             ],
             out_specs=[
@@ -269,7 +276,7 @@
             jax.ShapeDtypeStruct((rows, width // 2), BF16),
             jax.ShapeDtypeStruct((rows, width // 2), F32),
         ],
-        compiler_params=pltpu.CompilerParams(vmem_limit_bytes=VMEM),
+        compiler_params=pltpu.CompilerParams(vmem_limit_bytes=VMEM_ALL),
         cost_estimate=pl.CostEstimate(
             flops=2 * rows * width * units,
             transcendentals=0,
@@ -303,6 +310,7 @@
         out_shape=[jax.ShapeDtypeStruct((rows, final), F32)]
         + [jax.ShapeDtypeStruct((rows, final), BF16)] * (places - 1),
         scratch_shapes=[pltpu.VMEM((rows, places * final), F32)],
+        compiler_params=pltpu.CompilerParams(vmem_limit_bytes=VMEM),
         name="collect",
     )(where, *sides)
 
@@ -337,20 +345,35 @@
     quarter = split // 2
     features = width // 2
     share = tokens // owners
-    cols = channels // CHUNKS
+    pieces = [channels * number // sum(CHUNKS) for number in CHUNKS]
+    starts = [sum(pieces[:number]) for number in range(len(pieces))]
     where = jnp.stack([core, mine, place])
     spot = jnp.stack([local, side])
     columns = range(2, owners, 2)
 
-    piece = lax.dynamic_slice(
+    piece_out = lax.dynamic_slice(
         mamba_in, (0, mine * share, (1 - side) * features), (1, share, features)
     )[0]
-    piece = xor_send(piece, half)
-
+    piece = xor_send(piece_out, half)
+
+    moe_in = after(moe_in, piece_out)
     left = lax.dynamic_slice(moe_in, (0, core * split), (moe_rows, quarter))
     right = lax.dynamic_slice(moe_in, (0, core * split + quarter), (moe_rows, quarter))
     names = jnp.pad(expert_ids.astype(BF16), ((0, 0), (0, LANES - expert_ids.shape[1])))
     right = jnp.concatenate([right, names], axis=1)
+    paired = xor_send(in_weight, 1)
+    weights, arrived = [], []
+    for start, cols in zip(starts, pieces):
+        block = in_weight[:, start : start + cols]
+        if len(arrived) == 1:
+            block = after(block, *arrived[0], piece)
+        entry, direct = [in_weight, paired], []
+        for mask in range(2, half, 2):
+            direct.append(xor_send(block, mask))
+            entry += [direct[-1], xor_send(direct[-1], 1)]
+        weights.append(entry)
+        arrived.append(direct)
+
     lefts = {0: left, 1: owner_send(left, 1)}
     rights = {0: right}
     for mask in columns:
@@ -359,34 +382,23 @@
     for mask in columns:
         got = owner_send(both, mask)
         lefts[mask], lefts[mask + 1] = got[:moe_rows], got[moe_rows:]
-    got = owner_send(jnp.concatenate([rights[mask] for mask in range(0, owners, 2)], axis=0), 1)
+    both = jnp.concatenate([rights[mask] for mask in range(0, owners, 2)], axis=0)
+    got = owner_send(both, 1)
     for mask in range(0, owners, 2):
         rights[mask + 1] = got[mask // 2 * moe_rows : (mask // 2 + 1) * moe_rows]
-    lefts = jnp.concatenate([lefts[mask] for mask in range(owners)], axis=0)
-    rights = jnp.concatenate([rights[mask] for mask in range(owners)], axis=0)
-    inputs = [lefts, rights, xor_send(lefts, 1), xor_send(rights[:, :quarter], 1)]
-
     fars = [piece, owner_send(piece, 1)]
     both = jnp.concatenate(fars, axis=0)
     for mask in columns:
         fars.append(owner_send(both, mask))
 
-    paired = xor_send(in_weight, 1)
-    weights, arrived = [], []
-    for chunk in range(CHUNKS):
-        block = in_weight[:, chunk * cols : (chunk + 1) * cols]
-        entry, direct = [in_weight, paired], []
-        for mask in range(2, half, 2):
-            if chunk:
-                block = after(block, *fars[1:])
-            direct.append(xor_send(block, mask))
-            entry += [direct[-1], xor_send(direct[-1], 1)]
-        weights.append(entry)
-        arrived.append(direct)
+    lefts = jnp.concatenate([lefts[mask] for mask in range(owners)], axis=0)
+    lefts = after(lefts, fars[1], *arrived[0], *arrived[1])
+    rights = jnp.concatenate([rights[mask] for mask in range(owners)], axis=0)
+    inputs = [lefts, rights, xor_send(lefts, 1), xor_send(rights[:, :quarter], 1)]
 
     def product(chunk, *earlier):
         own, out = half_product(
-            spot, mamba_in, [after(fars[0], *earlier), *fars[1:]], weights[chunk], chunk * cols, cols
+            spot, mamba_in, [after(fars[0], *earlier), *fars[1:]], weights[chunk], starts[chunk], pieces[chunk]
         )
         return own, out, xor_send(out, half)
 
@@ -399,19 +411,20 @@
             conv_state,
             conv_kernel,
             conv_bias[None],
-            chunk * cols,
+            starts[chunk],
             channels,
             before,
         )
 
-    inputs[0] = after(inputs[0], *fars, *arrived[0], paired)
-    hidden, scale = hidden_units(where, inputs, router.T, w_gate, w_up)
-    own_0, out_0, come_0 = product(0, hidden)
-    hidden = after(hidden, out_0, *arrived[1])
+    inputs[0] = after(inputs[0], paired)
+    hidden, scale = hidden_units(where, inputs, router.T, w_gate, w_up, 0, w_gate.shape[2])
+    own_0, out_0, come_0 = product(0, hidden, *weights[1][3::2])
+    hidden = after(hidden, out_0, *arrived[2])
     send, keep = down_units(where, hidden, scale, w_down, final)
-    taken = xor_send(send, 1)
-    own_1, out_1, come_1 = product(1, keep)
-    taken = after(taken, out_1)
+    own_1, out_1, come_1 = product(1, keep, come_0)
+    taken = xor_send(after(send, out_1), 1)
+    own_2, out_2, come_2 = product(2, out_1)
+    taken = after(taken, out_2)
     total = (keep + taken.astype(F32)).reshape(owners, moe_rows, split)
     left, right = total[:, :, :quarter], total[:, :, quarter:]
     got = owner_send(jnp.concatenate([left[m] for m in range(1, owners, 2)], 0).astype(BF16), 1)
@@ -429,10 +442,12 @@
         if mask != columns[-1]:
             lefts = lefts + come.astype(F32)
     sides = [lefts, come, firsts, owner_send(seconds.astype(BF16), 1)]
+    sides[0] = after(sides[0], come_2)
     answer, *outs = collect(where, sides, final, half)
     for mask, out in enumerate(outs, 1):
         answer = answer + xor_send(out, 2 * mask).astype(F32)
     conv_out = convolve(1, own_1, come_1, conv_out)
+    conv_out = convolve(2, own_2, come_2, conv_out)
     return conv_out, answer.astype(BF16)
 
 

time: 175 us -> 155 us (0.89)
  waiting for transfers between devices: 69.9 us -> 61.3 us
  local copies, waits for them, and re-layouts: 9.63 us -> 4.94 us
  Pallas kernels: 58.8 us -> 54.3 us
  other arithmetic: 7.18 us -> 5.05 us
    ppermute x10, waiting for transfers between devices: 44.6 us -> 20.5 us  [owner_send(): return lax.ppermute(value, 'expert', pairs)]
    ppermute x14 -> x17, waiting for transfers between devices: 25.3 us -> 40.8 us  [xor_send(): return lax.ppermute(value, 'dp', pairs)]
    unnamed x38 -> x18, local copies, waits for them, and re-layouts: 4.35 us -> 0.03 us
    pallas_call x2 -> x3, Pallas kernels: 14 us -> 11 us  [half_product(): pl.pallas_call(functools.partial(half_product_kernel, len(weights), depth...]
    ppermute x14 -> x17, starting transfers between devices: 13.8 us -> 15.8 us  [xor_send(): return lax.ppermute(value, 'dp', pairs)]
    ppermute x10, starting transfers between devices: 14 us -> 12.1 us  [owner_send(): return lax.ppermute(value, 'expert', pairs)]
    pallas_call x2 -> x3, Pallas kernels: 6.17 us -> 6.19 us  [conv(): pl.pallas_call(functools.partial(conv_kernel_body, pad, pieces), grid=(co...]
  transfers between devices with their start and end apart: 24 -> 27, of which waited for: 13 -> 9; matrix products, arithmetic and copies ran while one was open for 5% -> 3% of each run, Pallas kernels for 26% -> 33%
where the time goes in v3:
time: 155 us; the launch traced here: 154 us
  waiting for transfers between devices  61.3 us (40%)
  Pallas kernels  54.3 us (35%)
  starting transfers between devices  27.9 us (18%)
  other arithmetic  5.05 us (3%)
  local copies, waits for them, and re-layouts  4.94 us (3%)
    ppermute x17, waiting for transfers between devices, xor_send(): return lax.ppermute(value, 'dp', pairs)  40.8 us
    pallas_call x1, Pallas kernels, hidden_units(): pl.pallas_call(functools.partial(hidden_kernel, quarter), grid_spec=pltpu...  22.2 us
    ppermute x10, waiting for transfers between devices, owner_send(): return lax.ppermute(value, 'expert', pairs)  20.5 us
    ppermute x17, starting transfers between devices, xor_send(): return lax.ppermute(value, 'dp', pairs)  15.8 us
    pallas_call x1, Pallas kernels, down_units(): pl.pallas_call(functools.partial(down_kernel, steps), grid_spec=pltpu.Pre...  14.3 us
    ppermute x10, starting transfers between devices, owner_send(): return lax.ppermute(value, 'expert', pairs)  12.1 us
    pallas_call x3, Pallas kernels, half_product(): pl.pallas_call(functools.partial(half_product_kernel, len(weights), depth...  11 us
    pallas_call x3, Pallas kernels, conv(): pl.pallas_call(functools.partial(conv_kernel_body, pad, pieces), grid=(co...  6.19 us
  transfers between devices with their start and end apart: 27, of which 9 were waited for; matrix products, arithmetic and copies ran while one was open for 3% of the time, Pallas kernels for 33%

profile of v3, /device:TPU:0, one launch (start us, length us, event | category | flops | bytes accessed | tf_op | source)
XLA Modules:
  0.0 154.4 jit_solution(18161274183426588156)
XLA Ops:
  0.7 1.1 dynamic-slice_bitcast_fusion
  1.8 0.7 convert_element_type.43
  2.6 1.1 constant_dynamic-slice_fusion
  3.7 3.0 %collective-permute-start.7 = (bf16[128,1152]{1,0:T(8,128)(2,1)S(1)}, bf16[128,1152]{1,0:T(8,128)(2,1)S(1)}, u32[]{:S(2)}, u32[]{:S(2)}) collective-permute-start(bf16[128,1152]{1,0:T(8,128)(2,1)S(1)} %pad_maximum_fusion.6), channel_id=1, source_target_pairs={{0,2},{1,3},{2,0},{3,1},{4,6},{5,7},{6,4},{7,5},{8,10},{9,11},{10,... | collective-permute-start | bytes 884744 | tf_op jit(solution)/shard_map/ppermute | solution.py:27
  6.8 1.5 collective-permute-start.1
  8.3 1.6 %collective-permute-start.4 = (bf16[512,512]{1,0:T(8,128)(2,1)S(1)}, bf16[512,512]{1,0:T(8,128)(2,1)S(1)}, u32[]{:S(2)}, u32[]{:S(2)}) collective-permute-start(bf16[512,512]{1,0:T(8,128)(2,1)S(1)} %get-tuple-element.63), channel_id=1, source_target_pairs={{0,8},{4,12},{8,0},{12,4},{16,24},{20,28},{24,16},{28,20},{1,9},{5... | collective-permute-start | bytes 1572872 | tf_op jit(solution)/shard_map/ppermute | solution.py:22
  10.0 4.5 %collective-permute-done.1 = bf16[128,1024]{1,0:T(8,128)(2,1)S(1)} collective-permute-done((bf16[128,1024]{1,0:T(8,128)(2,1)S(1)}, bf16[128,1024]{1,0:T(8,128)(2,1)S(1)}, u32[]{:S(2)}, u32[]{:S(2)}) %collective-permute-start.1) | collective-permute-done | bytes 262176 | tf_op jit(solution)/shard_map/ppermute | solution.py:27
  14.6 0.4 collective-permute-start.2
  15.0 1.7 %collective-permute-start.8 = (bf16[256,1152]{1,0:T(8,128)(2,1)S(1)}, bf16[256,1152]{1,0:T(8,128)(2,1)S(1)}, u32[]{:S(2)}, u32[]{:S(2)}) collective-permute-start(bf16[256,1152]{1,0:T(8,128)(2,1)S(1)} %pad_maximum_fusion.2), channel_id=1, source_target_pairs={{0,1},{1,0},{2,3},{3,2},{4,5},{5,4},{6,7},{7,6},{8,9},{9,8},{10,11... | collective-permute-start | bytes 1769480 | tf_op jit(solution)/shard_map/ppermute | solution.py:27
  16.7 2.6 %collective-permute-start = (bf16[64,2048]{1,0:T(8,128)(2,1)S(1)}, bf16[64,2048]{1,0:T(8,128)(2,1)S(1)}, u32[]{:S(2)}, u32[]{:S(2)}) collective-permute-start(bf16[64,2048]{1,0:T(8,128)(2,1)S(1)} %dynamic-slice_bitcast_fusion), channel_id=1, source_target_pairs={{0,16},{4,20},{8,24},{12,28},{16,0},{20,4},{24,8},{28,12},{1,17},{... | collective-permute-start | bytes 786440 | tf_op jit(solution)/shard_map/ppermute | solution.py:22
  19.3 10.3 %collective-permute-done.refs_0_ = bf16[64,2048]{1,0:T(8,128)(2,1)S(1)} collective-permute-done((bf16[64,2048]{1,0:T(8,128)(2,1)S(1)}, bf16[64,2048]{1,0:T(8,128)(2,1)S(1)}, u32[]{:S(2)}, u32[]{:S(2)}) %collective-permute-start) | collective-permute-done | bytes 262176 | tf_op jit(solution)/shard_map/ppermute | solution.py:22
  29.7 0.7 collective-permute-start.3
  30.3 0.6 collective-permute-start.5
  30.9 1.1 pad_maximum_fusion.1.refs_0_
  32.2 1.3 slice.87
  33.5 2.6 %collective-permute-done.3.refs_1_ = bf16[64,2048]{1,0:T(8,128)(2,1)S(1)} collective-permute-done((bf16[64,2048]{1,0:T(8,128)(2,1)S(1)}, bf16[64,2048]{1,0:T(8,128)(2,1)S(1)}, u32[]{:S(2)}, u32[]{:S(2)}) %collective-permute-start.3) | collective-permute-done | bytes 262176 | tf_op jit(solution)/shard_map/ppermute | solution.py:27
  36.0 4.9 %collective-permute-done.5.refs_5_ = bf16[512,512]{1,0:T(8,128)(2,1)} collective-permute-done((bf16[512,512]{1,0:T(8,128)(2,1)S(1)}, bf16[512,512]{1,0:T(8,128)(2,1)}, u32[]{:S(2)}, u32[]{:S(2)}) %collective-permute-start.5) | collective-permute-done | bytes 524320 | tf_op jit(solution)/shard_map/ppermute | solution.py:22
  41.0 1.1 slice.73
  42.0 1.5 collective-permute-start.14
  43.6 0.7 pad_add_fusion.where
  44.3 2.1 %collective-permute-start.12 = (bf16[128,2048]{1,0:T(8,128)(2,1)S(1)}, bf16[128,2048]{1,0:T(8,128)(2,1)S(1)}, u32[]{:S(2)}, u32[]{:S(2)}) collective-permute-start(bf16[128,2048]{1,0:T(8,128)(2,1)S(1)} %pad_maximum_fusion.4), channel_id=1, source_target_pairs={{0,2},{1,3},{2,0},{3,1},{4,6},{5,7},{6,4},{7,5},{8,10},{9,11},{10,... | collective-permute-start | bytes 1572872 | tf_op jit(solution)/shard_map/ppermute | solution.py:27
  46.5 0.5 collective-permute-start.11
  47.0 22.2 %hidden_units.1 = (bf16[512,1536]{1,0:T(8,128)(2,1)}, f32[512,128]{1,0:T(8,128)}) custom-call(s32[3]{0:T(128)} %pad_add_fusion.where, bf16[512,1024]{1,0:T(8,128)(2,1)} %pad_maximum_fusion.1.refs_0_, bf16[512,1152]{1,0:T(8,128)(2,1)} %copy-done.6, bf16[512,1024]{1,0:T(8,128)(2,1)} %collective-permute-done.9.refs_2_, ...), custom_call_target="tpu_custom_call" | custom-call | flops 12884901888 | bytes 33554432 | tf_op jit(solution)/shard_map/hidden_units/pallas_call | solution.py:214
  69.2 2.9 %half_product.3 = (f32[256,512]{1,0:T(8,128)S(1)}, bf16[256,512]{1,0:T(8,128)(2,1)S(1)}) custom-call(s32[2]{0:T(128)S(1)} %pad_add_fusion.1.where, bf16[1,256,4096]{2,1,0:T(8,128)(2,1)S(1)} %copy-done.1, bf16[64,2048]{1,0:T(8,128)(2,1)S(1)} %collective-permute-done.refs_0_, bf16[64,2048]{1,0:T(8,128)(2,1)S(1)} %collective-permute-done.3.refs_1_, ...), custom_call_target="tpu_custom_call" | custom-call | flops 1073741824 | bytes 4980736 | tf_op jit(solution)/shard_map/half_product/pallas_call | solution.py:84
  72.2 3.4 %collective-permute-start.15 = (bf16[256,512]{1,0:T(8,128)(2,1)S(1)}, bf16[256,512]{1,0:T(8,128)(2,1)S(1)}, u32[]{:S(2)}, u32[]{:S(2)}) collective-permute-start(bf16[256,512]{1,0:T(8,128)(2,1)S(1)} %get-tuple-element.34), channel_id=1, source_target_pairs={{0,16},{4,20},{8,24},{12,28},{16,0},{20,4},{24,8},{28,12},{1,17},{... | collective-permute-start | bytes 786440 | tf_op jit(solution)/shard_map/ppermute | solution.py:22
  75.6 14.3 %down_units.1 = (bf16[512,2048]{1,0:T(8,128)(2,1)}, f32[512,2048]{1,0:T(8,128)}) custom-call(s32[3]{0:T(128)} %pad_add_fusion.where, bf16[512,1536]{1,0:T(8,128)(2,1)} %get-tuple-element.35.hidden, f32[512,128]{1,0:T(8,128)} %get-tuple-element.36.scale, bf16[1,1536,4096]{2,1,0:T(8,128)(2,1)} %down.1), custom_call_target="tpu_custom_call" | custom-call | flops 6442450944 | bytes 18350080 | tf_op jit(solution)/shard_map/down_units/pallas_call | solution.py:260
  89.9 3.1 %half_product.4 = (f32[256,512]{1,0:T(8,128)S(1)}, bf16[256,512]{1,0:T(8,128)(2,1)S(1)}) custom-call(s32[2]{0:T(128)S(1)} %pad_add_fusion.1.where, bf16[1,256,4096]{2,1,0:T(8,128)(2,1)S(1)} %copy-done.1, bf16[64,2048]{1,0:T(8,128)(2,1)S(1)} %collective-permute-done.refs_0_, bf16[64,2048]{1,0:T(8,128)(2,1)S(1)} %collective-permute-done.3.refs_1_, ...), custom_call_target="tpu_custom_call" | custom-call | flops 1073741824 | bytes 4980736 | tf_op jit(solution)/shard_map/half_product/pallas_call | solution.py:84
  93.1 0.5 collective-permute-start.16
  93.6 5.0 %collective-permute-done.16.refs_6_ = bf16[512,1024]{1,0:T(8,128)(2,1)S(1)} collective-permute-done((bf16[512,1024]{1,0:T(8,128)(2,1)}, bf16[512,1024]{1,0:T(8,128)(2,1)S(1)}, u32[]{:S(2)}, u32[]{:S(2)}) %collective-permute-start.16) | collective-permute-done | bytes 1048608 | tf_op jit(solution)/shard_map/ppermute | solution.py:22
  98.6 5.0 %half_product.5 = (f32[256,1024]{1,0:T(8,128)S(1)}, bf16[256,1024]{1,0:T(8,128)(2,1)S(1)}) custom-call(s32[2]{0:T(128)S(1)} %pad_add_fusion.1.where, bf16[1,256,4096]{2,1,0:T(8,128)(2,1)S(1)} %copy-done.1, bf16[64,2048]{1,0:T(8,128)(2,1)S(1)} %collective-permute-done.refs_0_, bf16[64,2048]{1,0:T(8,128)(2,1)S(1)} %collective-permute-done.3.refs_1_, ...), custom_call_target="tpu_custom_call" | custom-call | flops 2147483648 | bytes 7864320 | tf_op jit(solution)/shard_map/half_product/pallas_call | solution.py:84
  103.6 0.9 convert_add_fusion
  104.4 0.3 convert.9
  104.9 1.6 %collective-permute-start.21 = (bf16[256,1024]{1,0:T(8,128)(2,1)S(1)}, bf16[256,1024]{1,0:T(8,128)(2,1)S(1)}, u32[]{:S(2)}, u32[]{:S(2)}) collective-permute-start(bf16[256,1024]{1,0:T(8,128)(2,1)S(1)} %pad_maximum_fusion.5), channel_id=1, source_target_pairs={{0,1},{1,0},{2,3},{3,2},{4,5},{5,4},{6,7},{7,6},{8,9},{9,8},{10,11... | collective-permute-start | bytes 1572872 | tf_op jit(solution)/shard_map/ppermute | solution.py:27
  106.6 0.4 collective-permute-start.17
  107.0 12.1 %collective-permute-done.21 = bf16[256,1024]{1,0:T(8,128)(2,1)S(1)} collective-permute-done((bf16[256,1024]{1,0:T(8,128)(2,1)S(1)}, bf16[256,1024]{1,0:T(8,128)(2,1)S(1)}, u32[]{:S(2)}, u32[]{:S(2)}) %collective-permute-start.21) | collective-permute-done | bytes 524320 | tf_op jit(solution)/shard_map/ppermute | solution.py:27
  119.1 1.3 collective-permute-done.20
  120.4 0.4 fusion.1
  120.8 0.4 collective-permute-start.22
  121.1 0.5 collective-permute-start.23
  121.8 16.3 %collective-permute-done.17.back = bf16[256,1024]{1,0:T(8,128)(2,1)S(1)} collective-permute-done((bf16[256,1024]{1,0:T(8,128)(2,1)S(1)}, bf16[256,1024]{1,0:T(8,128)(2,1)S(1)}, u32[]{:S(2)}, u32[]{:S(2)}) %collective-permute-start.17) | collective-permute-done | bytes 524320 | tf_op jit(solution)/shard_map/ppermute | solution.py:22
  138.0 0.7 collect.1
  138.8 2.0 %collective-permute-start.25 = (bf16[128,512]{1,0:T(8,128)(2,1)S(1)}, bf16[128,512]{1,0:T(8,128)(2,1)S(1)}, u32[]{:S(2)}, u32[]{:S(2)}) collective-permute-start(bf16[128,512]{1,0:T(8,128)(2,1)S(1)} %get-tuple-element.52), channel_id=1, source_target_pairs={{0,16},{4,20},{8,24},{12,28},{16,0},{20,4},{24,8},{28,12},{1,17},{... | collective-permute-start | bytes 393224 | tf_op jit(solution)/shard_map/ppermute | solution.py:22
  140.9 2.3 %collective-permute-start.26 = (bf16[128,512]{1,0:T(8,128)(2,1)S(1)}, bf16[128,512]{1,0:T(8,128)(2,1)S(1)}, u32[]{:S(2)}, u32[]{:S(2)}) collective-permute-start(bf16[128,512]{1,0:T(8,128)(2,1)S(1)} %get-tuple-element.53), channel_id=1, source_target_pairs={{0,24},{4,28},{8,16},{12,20},{16,8},{20,12},{24,0},{28,4},{1,25},{... | collective-permute-start | bytes 393224 | tf_op jit(solution)/shard_map/ppermute | solution.py:22
  143.2 1.8 %conv.3.refs_0_ = bf16[1,256,2048]{2,1,0:T(8,128)(2,1)} custom-call(s32[3]{0:T(128)S(1)} %copy-done.5, f32[256,512]{1,0:T(8,128)S(1)} %get-tuple-element.48.own, bf16[256,512]{1,0:T(8,128)(2,1)S(1)} %collective-permute-done.15.back, bf16[1,3,2048]{2,1,0:T(4,128)(2,1)S(1)} %copy-done.3, f32[4,2048]{1,0:T(4,128)S(1)} %copy-done.2, f32[1,2048]{1,0:T(1,128)S(1)} %bitcast.35), custom_call_target="tpu_custom_call" | custom-call | flops 1572864 | bytes 1048576 | tf_op jit(solution)/shard_map/conv/pallas_call | solution.py:147
  145.0 4.3 %collective-permute-done.18.back = bf16[256,512]{1,0:T(8,128)(2,1)S(1)} collective-permute-done((bf16[256,512]{1,0:T(8,128)(2,1)S(1)}, bf16[256,512]{1,0:T(8,128)(2,1)S(1)}, u32[]{:S(2)}, u32[]{:S(2)}) %collective-permute-start.18) | collective-permute-done | bytes 262176 | tf_op jit(solution)/shard_map/ppermute | solution.py:22
  149.3 1.8 %conv.4.refs_0_ = bf16[1,256,2048]{2,1,0:T(8,128)(2,1)} custom-call(s32[3]{0:T(128)S(1)} %copy-done.5, f32[256,512]{1,0:T(8,128)S(1)} %get-tuple-element.43.own, bf16[256,512]{1,0:T(8,128)(2,1)S(1)} %collective-permute-done.18.back, bf16[1,3,2048]{2,1,0:T(4,128)(2,1)S(1)} %copy-done.3, f32[4,2048]{1,0:T(4,128)S(1)} %copy-done.2, ...), custom_call_target="tpu_custom_call", output_to_operand_aliasing={{}: (6, {})} | custom-call | flops 1572864 | bytes 1048576 | tf_op jit(solution)/shard_map/conv/pallas_call | solution.py:147
  151.1 2.5 %conv.5 = bf16[1,256,2048]{2,1,0:T(8,128)(2,1)} custom-call(s32[3]{0:T(128)S(1)} %copy-done.5, f32[256,1024]{1,0:T(8,128)S(1)} %get-tuple-element.41.own, bf16[256,1024]{1,0:T(8,128)(2,1)S(1)} %collective-permute-done.17.back, bf16[1,3,2048]{2,1,0:T(4,128)(2,1)S(1)} %copy-done.3, f32[4,2048]{1,0:T(4,128)S(1)} %copy-done.2, ...), custom_call_target="tpu_custom_call", output_to_operand_aliasing={{}: (6, {})} | custom-call | flops 3145728 | bytes 2097152 | tf_op jit(solution)/shard_map/conv/pallas_call | solution.py:147
  153.7 0.7 add_convert_fusion
  (57 shorter events, 1.2 us)
Async XLA Ops:
  0.6 7.6 %copy-start = (bf16[512,2048]{1,0:T(8,128)(2,1)S(1)}, bf16[512,2048]{1,0:T(8,128)(2,1)}, u32[]{:S(2)}) copy-start(bf16[512,2048]{1,0:T(8,128)(2,1)} %refs_3_.5) | copy-start | bytes 6291460
  3.7 11.3 %collective-permute-start.7 = (bf16[128,1152]{1,0:T(8,128)(2,1)S(1)}, bf16[128,1152]{1,0:T(8,128)(2,1)S(1)}, u32[]{:S(2)}, u32[]{:S(2)}) collective-permute-start(bf16[128,1152]{1,0:T(8,128)(2,1)S(1)} %pad_maximum_fusion.6), channel_id=1, source_target_pairs={{0,2},{1,3},{2,0},{3,1},{4,6},{5,7},{6,4},{7,5},{8,10},{9,11},{10,... | collective-permute-start | bytes 884744 | tf_op jit(solution)/shard_map/ppermute | solution.py:27
  6.8 7.8 %collective-permute-start.1 = (bf16[128,1024]{1,0:T(8,128)(2,1)S(1)}, bf16[128,1024]{1,0:T(8,128)(2,1)S(1)}, u32[]{:S(2)}, u32[]{:S(2)}) collective-permute-start(bf16[128,1024]{1,0:T(8,128)(2,1)S(1)} %get-tuple-element.65), channel_id=1, source_target_pairs={{0,1},{1,0},{2,3},{3,2},{4,5},{5,4},{6,7},{7,6},{8,9},{9,8},{10,11... | collective-permute-start | bytes 786440 | tf_op jit(solution)/shard_map/ppermute | solution.py:27
  8.3 22.0 %collective-permute-start.4 = (bf16[512,512]{1,0:T(8,128)(2,1)S(1)}, bf16[512,512]{1,0:T(8,128)(2,1)S(1)}, u32[]{:S(2)}, u32[]{:S(2)}) collective-permute-start(bf16[512,512]{1,0:T(8,128)(2,1)S(1)} %get-tuple-element.63), channel_id=1, source_target_pairs={{0,8},{4,12},{8,0},{12,4},{16,24},{20,28},{24,16},{28,20},{1,9},{5... | collective-permute-start | bytes 1572872 | tf_op jit(solution)/shard_map/ppermute | solution.py:22
  14.6 16.4 %collective-permute-start.2 = (bf16[256,1024]{1,0:T(8,128)(2,1)S(1)}, bf16[256,1024]{1,0:T(8,128)(2,1)S(1)}, u32[]{:S(2)}, u32[]{:S(2)}) collective-permute-start(bf16[256,1024]{1,0:T(8,128)(2,1)S(1)} %pad_maximum_fusion.3), channel_id=1, source_target_pairs={{0,2},{1,3},{2,0},{3,1},{4,6},{5,7},{6,4},{7,5},{8,10},{9,11},{10,... | collective-permute-start | bytes 1572872 | tf_op jit(solution)/shard_map/ppermute | solution.py:27
  15.0 17.0 %collective-permute-start.8 = (bf16[256,1152]{1,0:T(8,128)(2,1)S(1)}, bf16[256,1152]{1,0:T(8,128)(2,1)S(1)}, u32[]{:S(2)}, u32[]{:S(2)}) collective-permute-start(bf16[256,1152]{1,0:T(8,128)(2,1)S(1)} %pad_maximum_fusion.2), channel_id=1, source_target_pairs={{0,1},{1,0},{2,3},{3,2},{4,5},{5,4},{6,7},{7,6},{8,9},{9,8},{10,11... | collective-permute-start | bytes 1769480 | tf_op jit(solution)/shard_map/ppermute | solution.py:27
  16.7 12.9 %collective-permute-start = (bf16[64,2048]{1,0:T(8,128)(2,1)S(1)}, bf16[64,2048]{1,0:T(8,128)(2,1)S(1)}, u32[]{:S(2)}, u32[]{:S(2)}) collective-permute-start(bf16[64,2048]{1,0:T(8,128)(2,1)S(1)} %dynamic-slice_bitcast_fusion), channel_id=1, source_target_pairs={{0,16},{4,20},{8,24},{12,28},{16,0},{20,4},{24,8},{28,12},{1,17},{... | collective-permute-start | bytes 786440 | tf_op jit(solution)/shard_map/ppermute | solution.py:22
  19.3 27.1 %collective-permute-start.6 = (bf16[512,2048]{1,0:T(8,128)(2,1)S(1)}, bf16[512,2048]{1,0:T(8,128)(2,1)}, u32[]{:S(2)}, u32[]{:S(2)}) collective-permute-start(bf16[512,2048]{1,0:T(8,128)(2,1)S(1)} %copy-done), channel_id=1, source_target_pairs={{0,4},{4,0},{8,12},{12,8},{16,20},{20,16},{24,28},{28,24},{1,5},{5... | collective-permute-start | bytes 6291464 | tf_op jit(solution)/shard_map/ppermute | solution.py:22
  29.7 6.4 %collective-permute-start.3 = (bf16[64,2048]{1,0:T(8,128)(2,1)S(1)}, bf16[64,2048]{1,0:T(8,128)(2,1)S(1)}, u32[]{:S(2)}, u32[]{:S(2)}) collective-permute-start(bf16[64,2048]{1,0:T(8,128)(2,1)S(1)} %collective-permute-done.refs_0_), channel_id=1, source_target_pairs={{0,1},{1,0},{2,3},{3,2},{4,5},{5,4},{6,7},{7,6},{8,9},{9,8},{10,11... | collective-permute-start | bytes 786440 | tf_op jit(solution)/shard_map/ppermute | solution.py:27
  30.3 10.7 %collective-permute-start.5 = (bf16[512,512]{1,0:T(8,128)(2,1)S(1)}, bf16[512,512]{1,0:T(8,128)(2,1)}, u32[]{:S(2)}, u32[]{:S(2)}) collective-permute-start(bf16[512,512]{1,0:T(8,128)(2,1)S(1)} %get-tuple-element.29), channel_id=1, source_target_pairs={{0,8},{4,12},{8,0},{12,4},{16,24},{20,28},{24,16},{28,20},{1,9},{5... | collective-permute-start | bytes 1572872 | tf_op jit(solution)/shard_map/ppermute | solution.py:22
  32.2 9.9 %copy-start.6 = (bf16[512,1152]{1,0:T(8,128)(2,1)}, bf16[512,1152]{1,0:T(8,128)(2,1)S(1)}, u32[]{:S(2)}) copy-start(bf16[512,1152]{1,0:T(8,128)(2,1)S(1)} %pad_maximum_fusion.refs_1_) | copy-start | bytes 3538948
  33.5 13.0 %collective-permute-start.10 = (bf16[512,1024]{1,0:T(8,128)(2,1)}, bf16[512,1024]{1,0:T(8,128)(2,1)}, u32[]{:S(2)}, u32[]{:S(2)}) collective-permute-start(bf16[512,1024]{1,0:T(8,128)(2,1)} %slice.87), channel_id=1, source_target_pairs={{0,4},{4,0},{8,12},{12,8},{16,20},{20,16},{24,28},{28,24},{1,5},{5... | collective-permute-start | bytes 3145736 | tf_op jit(solution)/shard_map/ppermute | solution.py:22
  41.0 6.0 %collective-permute-start.9 = (bf16[512,1024]{1,0:T(8,128)(2,1)}, bf16[512,1024]{1,0:T(8,128)(2,1)}, u32[]{:S(2)}, u32[]{:S(2)}) collective-permute-start(bf16[512,1024]{1,0:T(8,128)(2,1)} %pad_maximum_fusion.1.refs_0_), channel_id=1, source_target_pairs={{0,4},{4,0},{8,12},{12,8},{16,20},{20,16},{24,28},{28,24},{1,5},{5... | collective-permute-start | bytes 3145736 | tf_op jit(solution)/shard_map/ppermute | solution.py:22
  42.0 33.6 %collective-permute-start.14 = (bf16[512,1024]{1,0:T(8,128)(2,1)}, bf16[512,1024]{1,0:T(8,128)(2,1)}, u32[]{:S(2)}, u32[]{:S(2)}) collective-permute-start(bf16[512,1024]{1,0:T(8,128)(2,1)} %slice.73), channel_id=1, source_target_pairs={{0,8},{4,12},{8,0},{12,4},{16,24},{20,28},{24,16},{28,20},{1,9},{5... | collective-permute-start | bytes 3145736 | tf_op jit(solution)/shard_map/ppermute | solution.py:22
  44.3 24.9 %collective-permute-start.12 = (bf16[128,2048]{1,0:T(8,128)(2,1)S(1)}, bf16[128,2048]{1,0:T(8,128)(2,1)S(1)}, u32[]{:S(2)}, u32[]{:S(2)}) collective-permute-start(bf16[128,2048]{1,0:T(8,128)(2,1)S(1)} %pad_maximum_fusion.4), channel_id=1, source_target_pairs={{0,2},{1,3},{2,0},{3,1},{4,6},{5,7},{6,4},{7,5},{8,10},{9,11},{10,... | collective-permute-start | bytes 1572872 | tf_op jit(solution)/shard_map/ppermute | solution.py:27
  46.5 22.7 %collective-permute-start.13 = (bf16[512,512]{1,0:T(8,128)(2,1)S(1)}, bf16[512,512]{1,0:T(8,128)(2,1)S(1)}, u32[]{:S(2)}, u32[]{:S(2)}) collective-permute-start(bf16[512,512]{1,0:T(8,128)(2,1)S(1)} %collective-permute-done.4.refs_5_), channel_id=1, source_target_pairs={{0,4},{4,0},{8,12},{12,8},{16,20},{20,16},{24,28},{28,24},{1,5},{5... | collective-permute-start | bytes 1572872 | tf_op jit(solution)/shard_map/ppermute | solution.py:22
  46.5 22.7 %collective-permute-start.11 = (bf16[512,512]{1,0:T(8,128)(2,1)}, bf16[512,512]{1,0:T(8,128)(2,1)S(1)}, u32[]{:S(2)}, u32[]{:S(2)}) collective-permute-start(bf16[512,512]{1,0:T(8,128)(2,1)} %collective-permute-done.5.refs_5_), channel_id=1, source_target_pairs={{0,4},{4,0},{8,12},{12,8},{16,20},{20,16},{24,28},{28,24},{1,5},{5... | collective-permute-start | bytes 1572872 | tf_op jit(solution)/shard_map/ppermute | solution.py:22
  47.0 22.2 %copy-start.1 = (bf16[1,256,4096]{2,1,0:T(8,128)(2,1)S(1)}, bf16[1,256,4096]{2,1,0:T(8,128)(2,1)}, u32[]{:S(2)}) copy-start(bf16[1,256,4096]{2,1,0:T(8,128)(2,1)} %window.5) | copy-start | bytes 6291460
  72.2 17.7 %collective-permute-start.15 = (bf16[256,512]{1,0:T(8,128)(2,1)S(1)}, bf16[256,512]{1,0:T(8,128)(2,1)S(1)}, u32[]{:S(2)}, u32[]{:S(2)}) collective-permute-start(bf16[256,512]{1,0:T(8,128)(2,1)S(1)} %get-tuple-element.34), channel_id=1, source_target_pairs={{0,16},{4,20},{8,24},{12,28},{16,0},{20,4},{24,8},{28,12},{1,17},{... | collective-permute-start | bytes 786440 | tf_op jit(solution)/shard_map/ppermute | solution.py:22
  89.9 3.1 %copy-start.8 = (bf16[512,2048]{1,0:T(8,128)(2,1)S(1)}, bf16[512,2048]{1,0:T(8,128)(2,1)}, u32[]{:S(2)}) copy-start(bf16[512,2048]{1,0:T(8,128)(2,1)} %get-tuple-element.46) | copy-start | bytes 6291460
  93.0 10.5 %collective-permute-start.19 = (bf16[512,2048]{1,0:T(8,128)(2,1)S(1)}, bf16[512,2048]{1,0:T(8,128)(2,1)S(1)}, u32[]{:S(2)}, u32[]{:S(2)}) collective-permute-start(bf16[512,2048]{1,0:T(8,128)(2,1)S(1)} %copy-done.8), channel_id=1, source_target_pairs={{0,4},{4,0},{8,12},{12,8},{16,20},{20,16},{24,28},{28,24},{1,5},{5... | collective-permute-start | bytes 6291464 | tf_op jit(solution)/shard_map/ppermute | solution.py:22
  93.1 5.5 %collective-permute-start.16 = (bf16[512,1024]{1,0:T(8,128)(2,1)}, bf16[512,1024]{1,0:T(8,128)(2,1)S(1)}, u32[]{:S(2)}, u32[]{:S(2)}) collective-permute-start(bf16[512,1024]{1,0:T(8,128)(2,1)} %collective-permute-done.14.refs_5_), channel_id=1, source_target_pairs={{0,4},{4,0},{8,12},{12,8},{16,20},{20,16},{24,28},{28,24},{1,5},{5... | collective-permute-start | bytes 3145736 | tf_op jit(solution)/shard_map/ppermute | solution.py:22
  98.6 5.0 %copy-start.7 = (f32[512,2048]{1,0:T(8,128)S(1)}, f32[512,2048]{1,0:T(8,128)}, u32[]{:S(2)}) copy-start(f32[512,2048]{1,0:T(8,128)} %get-tuple-element.37) | copy-start | bytes 12582916
  104.9 14.2 %collective-permute-start.21 = (bf16[256,1024]{1,0:T(8,128)(2,1)S(1)}, bf16[256,1024]{1,0:T(8,128)(2,1)S(1)}, u32[]{:S(2)}, u32[]{:S(2)}) collective-permute-start(bf16[256,1024]{1,0:T(8,128)(2,1)S(1)} %pad_maximum_fusion.5), channel_id=1, source_target_pairs={{0,1},{1,0},{2,3},{3,2},{4,5},{5,4},{6,7},{7,6},{8,9},{9,8},{10,11... | collective-permute-start | bytes 1572872 | tf_op jit(solution)/shard_map/ppermute | solution.py:27
  106.5 31.6 %copy-start.5 = (s32[3]{0:T(128)S(1)}, s32[3]{0:T(128)}, u32[]{:S(2)}) copy-start(s32[3]{0:T(128)} %pad_add_fusion.where) | copy-start | bytes 40
  106.5 36.7 %copy-start.2 = (f32[4,2048]{1,0:T(4,128)S(1)}, f32[4,2048]{1,0:T(4,128)}, u32[]{:S(2)}) copy-start(f32[4,2048]{1,0:T(4,128)} %taps.5) | copy-start | bytes 98308
  106.5 36.7 %copy-start.3 = (bf16[1,3,2048]{2,1,0:T(4,128)(2,1)S(1)}, bf16[1,3,2048]{2,1,0:T(4,128)(2,1)}, u32[]{:S(2)}) copy-start(bf16[1,3,2048]{2,1,0:T(4,128)(2,1)} %state.5) | copy-start | bytes 36868
  106.5 36.7 %copy-start.4 = (f32[2048]{0:T(1024)S(1)}, f32[2048]{0:T(1024)}, u32[]{:S(2)}) copy-start(f32[2048]{0:T(1024)} %param.15) | copy-start | bytes 24580
  106.5 13.9 %collective-permute-start.20 = (bf16[256,1024]{1,0:T(8,128)(2,1)S(1)}, bf16[256,1024]{1,0:T(8,128)(2,1)S(1)}, u32[]{:S(2)}, u32[]{:S(2)}) collective-permute-start(bf16[256,1024]{1,0:T(8,128)(2,1)S(1)} %bitcast.40), channel_id=1, source_target_pairs={{0,2},{1,3},{2,0},{3,1},{4,6},{5,7},{6,4},{7,5},{8,10},{9,11},{10,... | collective-permute-start | bytes 1572872 | tf_op jit(solution)/shard_map/ppermute | solution.py:27
  106.6 31.4 %collective-permute-start.17 = (bf16[256,1024]{1,0:T(8,128)(2,1)S(1)}, bf16[256,1024]{1,0:T(8,128)(2,1)S(1)}, u32[]{:S(2)}, u32[]{:S(2)}) collective-permute-start(bf16[256,1024]{1,0:T(8,128)(2,1)S(1)} %get-tuple-element.42), channel_id=1, source_target_pairs={{0,16},{4,20},{8,24},{12,28},{16,0},{20,4},{24,8},{28,12},{1,17},{... | collective-permute-start | bytes 1572872 | tf_op jit(solution)/shard_map/ppermute | solution.py:22
  120.8 17.3 %collective-permute-start.22 = (bf16[128,1024]{1,0:T(8,128)(2,1)S(1)}, bf16[128,1024]{1,0:T(8,128)(2,1)S(1)}, u32[]{:S(2)}, u32[]{:S(2)}) collective-permute-start(bf16[128,1024]{1,0:T(8,128)(2,1)S(1)} %get-tuple-element.59), channel_id=1, source_target_pairs={{0,2},{1,3},{2,0},{3,1},{4,6},{5,7},{6,4},{7,5},{8,10},{9,11},{10,... | collective-permute-start | bytes 786440 | tf_op jit(solution)/shard_map/ppermute | solution.py:27
  121.1 16.9 %collective-permute-start.23 = (bf16[128,1024]{1,0:T(8,128)(2,1)S(1)}, bf16[128,1024]{1,0:T(8,128)(2,1)S(1)}, u32[]{:S(2)}, u32[]{:S(2)}) collective-permute-start(bf16[128,1024]{1,0:T(8,128)(2,1)S(1)} %get-tuple-element.54), channel_id=1, source_target_pairs={{0,1},{1,0},{2,3},{3,2},{4,5},{5,4},{6,7},{7,6},{8,9},{9,8},{10,11... | collective-permute-start | bytes 786440 | tf_op jit(solution)/shard_map/ppermute | solution.py:27
  121.7 27.6 %collective-permute-start.18 = (bf16[256,512]{1,0:T(8,128)(2,1)S(1)}, bf16[256,512]{1,0:T(8,128)(2,1)S(1)}, u32[]{:S(2)}, u32[]{:S(2)}) collective-permute-start(bf16[256,512]{1,0:T(8,128)(2,1)S(1)} %get-tuple-element.39), channel_id=1, source_target_pairs={{0,16},{4,20},{8,24},{12,28},{16,0},{20,4},{24,8},{28,12},{1,17},{... | collective-permute-start | bytes 786440 | tf_op jit(solution)/shard_map/ppermute | solution.py:22
  138.7 14.9 %collective-permute-start.24 = (bf16[128,512]{1,0:T(8,128)(2,1)S(1)}, bf16[128,512]{1,0:T(8,128)(2,1)S(1)}, u32[]{:S(2)}, u32[]{:S(2)}) collective-permute-start(bf16[128,512]{1,0:T(8,128)(2,1)S(1)} %get-tuple-element.51), channel_id=1, source_target_pairs={{0,8},{4,12},{8,0},{12,4},{16,24},{20,28},{24,16},{28,20},{1,9},{5... | collective-permute-start | bytes 393224 | tf_op jit(solution)/shard_map/ppermute | solution.py:22
  138.8 14.8 %collective-permute-start.25 = (bf16[128,512]{1,0:T(8,128)(2,1)S(1)}, bf16[128,512]{1,0:T(8,128)(2,1)S(1)}, u32[]{:S(2)}, u32[]{:S(2)}) collective-permute-start(bf16[128,512]{1,0:T(8,128)(2,1)S(1)} %get-tuple-element.52), channel_id=1, source_target_pairs={{0,16},{4,20},{8,24},{12,28},{16,0},{20,4},{24,8},{28,12},{1,17},{... | collective-permute-start | bytes 393224 | tf_op jit(solution)/shard_map/ppermute | solution.py:22
  140.9 12.8 %collective-permute-start.26 = (bf16[128,512]{1,0:T(8,128)(2,1)S(1)}, bf16[128,512]{1,0:T(8,128)(2,1)S(1)}, u32[]{:S(2)}, u32[]{:S(2)}) collective-permute-start(bf16[128,512]{1,0:T(8,128)(2,1)S(1)} %get-tuple-element.53), channel_id=1, source_target_pairs={{0,24},{4,28},{8,16},{12,20},{16,8},{20,12},{24,0},{28,4},{1,25},{... | collective-permute-start | bytes 393224 | tf_op jit(solution)/shard_map/ppermute | solution.py:22

commit v4 on v3

--- a/solution.py
+++ b/solution.py
@@ -370,7 +370,8 @@
         entry, direct = [in_weight, paired], []
         for mask in range(2, half, 2):
             direct.append(xor_send(block, mask))
-            entry += [direct[-1], xor_send(direct[-1], 1)]
+            if len(arrived) < 2:
+                entry += [direct[-1], xor_send(direct[-1], 1)]
         weights.append(entry)
         arrived.append(direct)
 
@@ -419,23 +420,25 @@
     inputs[0] = after(inputs[0], paired)
     hidden, scale = hidden_units(where, inputs, router.T, w_gate, w_up, 0, w_gate.shape[2])
     own_0, out_0, come_0 = product(0, hidden, *weights[1][3::2])
-    hidden = after(hidden, out_0, *arrived[2])
+    hidden = after(hidden, out_0)
+    for block in arrived[2]:
+        weights[2] += [block, xor_send(after(block, hidden), 1)]
     send, keep = down_units(where, hidden, scale, w_down, final)
-    own_1, out_1, come_1 = product(1, keep, come_0)
+    own_1, out_1, come_1 = product(1, keep, come_0, *weights[2][3::2])
     taken = xor_send(after(send, out_1), 1)
     own_2, out_2, come_2 = product(2, out_1)
     taken = after(taken, out_2)
     total = (keep + taken.astype(F32)).reshape(owners, moe_rows, split)
     left, right = total[:, :, :quarter], total[:, :, quarter:]
     got = owner_send(jnp.concatenate([left[m] for m in range(1, owners, 2)], 0).astype(BF16), 1)
-    got = got.reshape(owners // 2, moe_rows, quarter)
+    conv_out = convolve(0, after(own_0, out_2), come_0, None)
+    got = after(got, conv_out).reshape(owners // 2, moe_rows, quarter)
     left = {mask: left[mask] + got[mask // 2].astype(F32) for mask in range(0, owners, 2)}
     firsts, seconds = right[0], right[1]
     for mask in columns:
         got = owner_send(right[mask : mask + 2].reshape(-1, quarter).astype(BF16), mask)
         firsts = firsts + got[:moe_rows].astype(F32)
         seconds = seconds + got[moe_rows:].astype(F32)
-    conv_out = convolve(0, after(own_0, firsts), come_0, None)
     lefts = left[0]
     for mask in columns:
         come = owner_send(left[mask].astype(BF16), mask)
@@ -446,8 +449,8 @@
     answer, *outs = collect(where, sides, final, half)
     for mask, out in enumerate(outs, 1):
         answer = answer + xor_send(out, 2 * mask).astype(F32)
+    conv_out = convolve(2, own_2, come_2, conv_out)
     conv_out = convolve(1, own_1, come_1, conv_out)
-    conv_out = convolve(2, own_2, come_2, conv_out)
     return conv_out, answer.astype(BF16)
 
 

time: 155 us -> 149 us (0.961)
  waiting for transfers between devices: 61.3 us -> 55 us
    ppermute x17, waiting for transfers between devices: 40.8 us -> 36.3 us  [xor_send(): return lax.ppermute(value, 'dp', pairs)]
    ppermute x10, waiting for transfers between devices: 20.5 us -> 18.7 us  [owner_send(): return lax.ppermute(value, 'expert', pairs)]
  transfers between devices with their start and end apart: 27 -> 27, of which waited for: 9 -> 9; matrix products, arithmetic and copies ran while one was open for 3% -> 3% of each run, Pallas kernels for 33% -> 35%
where the time goes in v4:
time: 149 us; the launch traced here: 148 us
  waiting for transfers between devices  55 us (37%)
  Pallas kernels  54.3 us (36%)
  starting transfers between devices  27.3 us (18%)
  local copies, waits for them, and re-layouts  5.71 us (4%)
  other arithmetic  4.99 us (3%)
    ppermute x17, waiting for transfers between devices, xor_send(): return lax.ppermute(value, 'dp', pairs)  36.3 us
    pallas_call x1, Pallas kernels, hidden_units(): pl.pallas_call(functools.partial(hidden_kernel, quarter), grid_spec=pltpu...  22.2 us
    ppermute x10, waiting for transfers between devices, owner_send(): return lax.ppermute(value, 'expert', pairs)  18.7 us
    ppermute x17, starting transfers between devices, xor_send(): return lax.ppermute(value, 'dp', pairs)  15.2 us
    pallas_call x1, Pallas kernels, down_units(): pl.pallas_call(functools.partial(down_kernel, steps), grid_spec=pltpu.Pre...  14.3 us
    ppermute x10, starting transfers between devices, owner_send(): return lax.ppermute(value, 'expert', pairs)  12.1 us
    pallas_call x3, Pallas kernels, half_product(): pl.pallas_call(functools.partial(half_product_kernel, len(weights), depth...  11 us
    pallas_call x3, Pallas kernels, conv(): pl.pallas_call(functools.partial(conv_kernel_body, pad, pieces), grid=(co...  6.19 us
  transfers between devices with their start and end apart: 27, of which 9 were waited for; matrix products, arithmetic and copies ran while one was open for 3% of the time, Pallas kernels for 35%

profile of v4, /device:TPU:0, one launch (start us, length us, event | category | flops | bytes accessed | tf_op | source)
XLA Modules:
  0.0 148.3 jit_solution(15875963773487372880)
XLA Ops:
  0.7 1.1 dynamic-slice_bitcast_fusion
  1.8 0.7 convert_element_type.43
  2.6 1.1 constant_dynamic-slice_fusion
  3.7 3.0 %collective-permute-start.7 = (bf16[128,1152]{1,0:T(8,128)(2,1)S(1)}, bf16[128,1152]{1,0:T(8,128)(2,1)S(1)}, u32[]{:S(2)}, u32[]{:S(2)}) collective-permute-start(bf16[128,1152]{1,0:T(8,128)(2,1)S(1)} %pad_maximum_fusion.6), channel_id=1, source_target_pairs={{0,2},{1,3},{2,0},{3,1},{4,6},{5,7},{6,4},{7,5},{8,10},{9,11},{10,... | collective-permute-start | bytes 884744 | tf_op jit(solution)/shard_map/ppermute | solution.py:27
  6.8 1.5 %collective-permute-start.1 = (bf16[128,1024]{1,0:T(8,128)(2,1)S(1)}, bf16[128,1024]{1,0:T(8,128)(2,1)S(1)}, u32[]{:S(2)}, u32[]{:S(2)}) collective-permute-start(bf16[128,1024]{1,0:T(8,128)(2,1)S(1)} %get-tuple-element.69), channel_id=1, source_target_pairs={{0,1},{1,0},{2,3},{3,2},{4,5},{5,4},{6,7},{7,6},{8,9},{9,8},{10,11... | collective-permute-start | bytes 786440 | tf_op jit(solution)/shard_map/ppermute | solution.py:27
  8.3 1.6 %collective-permute-start.4 = (bf16[512,512]{1,0:T(8,128)(2,1)S(1)}, bf16[512,512]{1,0:T(8,128)(2,1)S(1)}, u32[]{:S(2)}, u32[]{:S(2)}) collective-permute-start(bf16[512,512]{1,0:T(8,128)(2,1)S(1)} %get-tuple-element.67), channel_id=1, source_target_pairs={{0,8},{4,12},{8,0},{12,4},{16,24},{20,28},{24,16},{28,20},{1,9},{5... | collective-permute-start | bytes 1572872 | tf_op jit(solution)/shard_map/ppermute | solution.py:22
  10.0 4.5 %collective-permute-done.1 = bf16[128,1024]{1,0:T(8,128)(2,1)S(1)} collective-permute-done((bf16[128,1024]{1,0:T(8,128)(2,1)S(1)}, bf16[128,1024]{1,0:T(8,128)(2,1)S(1)}, u32[]{:S(2)}, u32[]{:S(2)}) %collective-permute-start.1) | collective-permute-done | bytes 262176 | tf_op jit(solution)/shard_map/ppermute | solution.py:27
  14.6 0.4 collective-permute-start.2
  15.0 1.7 %collective-permute-start.8 = (bf16[256,1152]{1,0:T(8,128)(2,1)S(1)}, bf16[256,1152]{1,0:T(8,128)(2,1)S(1)}, u32[]{:S(2)}, u32[]{:S(2)}) collective-permute-start(bf16[256,1152]{1,0:T(8,128)(2,1)S(1)} %pad_maximum_fusion.2), channel_id=1, source_target_pairs={{0,1},{1,0},{2,3},{3,2},{4,5},{5,4},{6,7},{7,6},{8,9},{9,8},{10,11... | collective-permute-start | bytes 1769480 | tf_op jit(solution)/shard_map/ppermute | solution.py:27
  16.7 2.6 %collective-permute-start = (bf16[64,2048]{1,0:T(8,128)(2,1)S(1)}, bf16[64,2048]{1,0:T(8,128)(2,1)S(1)}, u32[]{:S(2)}, u32[]{:S(2)}) collective-permute-start(bf16[64,2048]{1,0:T(8,128)(2,1)S(1)} %dynamic-slice_bitcast_fusion), channel_id=1, source_target_pairs={{0,16},{4,20},{8,24},{12,28},{16,0},{20,4},{24,8},{28,12},{1,17},{... | collective-permute-start | bytes 786440 | tf_op jit(solution)/shard_map/ppermute | solution.py:22
  19.3 10.3 %collective-permute-done.refs_0_ = bf16[64,2048]{1,0:T(8,128)(2,1)S(1)} collective-permute-done((bf16[64,2048]{1,0:T(8,128)(2,1)S(1)}, bf16[64,2048]{1,0:T(8,128)(2,1)S(1)}, u32[]{:S(2)}, u32[]{:S(2)}) %collective-permute-start) | collective-permute-done | bytes 262176 | tf_op jit(solution)/shard_map/ppermute | solution.py:22
  29.7 0.7 collective-permute-start.3
  30.3 0.6 collective-permute-start.5
  30.9 1.1 pad_maximum_fusion.1.refs_0_
  32.2 1.3 slice.87
  33.4 2.6 %collective-permute-done.3.refs_1_ = bf16[64,2048]{1,0:T(8,128)(2,1)S(1)} collective-permute-done((bf16[64,2048]{1,0:T(8,128)(2,1)S(1)}, bf16[64,2048]{1,0:T(8,128)(2,1)S(1)}, u32[]{:S(2)}, u32[]{:S(2)}) %collective-permute-start.3) | collective-permute-done | bytes 262176 | tf_op jit(solution)/shard_map/ppermute | solution.py:27
  36.0 4.9 %collective-permute-done.5.refs_5_ = bf16[512,512]{1,0:T(8,128)(2,1)} collective-permute-done((bf16[512,512]{1,0:T(8,128)(2,1)S(1)}, bf16[512,512]{1,0:T(8,128)(2,1)}, u32[]{:S(2)}, u32[]{:S(2)}) %collective-permute-start.5) | collective-permute-done | bytes 524320 | tf_op jit(solution)/shard_map/ppermute | solution.py:22
  41.0 1.1 slice.73
  42.0 1.5 %collective-permute-start.15 = (bf16[512,1024]{1,0:T(8,128)(2,1)}, bf16[512,1024]{1,0:T(8,128)(2,1)}, u32[]{:S(2)}, u32[]{:S(2)}) collective-permute-start(bf16[512,1024]{1,0:T(8,128)(2,1)} %slice.73), channel_id=1, source_target_pairs={{0,8},{4,12},{8,0},{12,4},{16,24},{20,28},{24,16},{28,20},{1,9},{5... | collective-permute-start | bytes 3145736 | tf_op jit(solution)/shard_map/ppermute | solution.py:22
  43.6 0.6 pad_add_fusion.where
  44.3 2.1 %collective-permute-start.12 = (bf16[128,2048]{1,0:T(8,128)(2,1)S(1)}, bf16[128,2048]{1,0:T(8,128)(2,1)S(1)}, u32[]{:S(2)}, u32[]{:S(2)}) collective-permute-start(bf16[128,2048]{1,0:T(8,128)(2,1)S(1)} %pad_maximum_fusion.4), channel_id=1, source_target_pairs={{0,2},{1,3},{2,0},{3,1},{4,6},{5,7},{6,4},{7,5},{8,10},{9,11},{10,... | collective-permute-start | bytes 1572872 | tf_op jit(solution)/shard_map/ppermute | solution.py:27
  46.4 0.5 collective-permute-start.11
  46.9 22.2 %hidden_units.1 = (bf16[512,1536]{1,0:T(8,128)(2,1)}, f32[512,128]{1,0:T(8,128)}) custom-call(s32[3]{0:T(128)} %pad_add_fusion.where, bf16[512,1024]{1,0:T(8,128)(2,1)} %pad_maximum_fusion.1.refs_0_, bf16[512,1152]{1,0:T(8,128)(2,1)} %copy-done.8, bf16[512,1024]{1,0:T(8,128)(2,1)} %collective-permute-done.9.refs_2_, ...), custom_call_target="tpu_custom_call" | custom-call | flops 12884901888 | bytes 33554432 | tf_op jit(solution)/shard_map/hidden_units/pallas_call | solution.py:214
  69.1 2.9 %half_product.3 = (f32[256,512]{1,0:T(8,128)S(1)}, bf16[256,512]{1,0:T(8,128)(2,1)S(1)}) custom-call(s32[2]{0:T(128)S(1)} %pad_add_fusion.1.where, bf16[1,256,4096]{2,1,0:T(8,128)(2,1)S(1)} %copy-done.1, bf16[64,2048]{1,0:T(8,128)(2,1)S(1)} %collective-permute-done.refs_0_, bf16[64,2048]{1,0:T(8,128)(2,1)S(1)} %collective-permute-done.3.refs_1_, ...), custom_call_target="tpu_custom_call" | custom-call | flops 1073741824 | bytes 4980736 | tf_op jit(solution)/shard_map/half_product/pallas_call | solution.py:84
  72.1 0.8 copy-done.2
  73.0 3.4 %collective-permute-start.14 = (bf16[256,512]{1,0:T(8,128)(2,1)S(1)}, bf16[256,512]{1,0:T(8,128)(2,1)S(1)}, u32[]{:S(2)}, u32[]{:S(2)}) collective-permute-start(bf16[256,512]{1,0:T(8,128)(2,1)S(1)} %get-tuple-element.36), channel_id=1, source_target_pairs={{0,16},{4,20},{8,24},{12,28},{16,0},{20,4},{24,8},{28,12},{1,17},{... | collective-permute-start | bytes 786440 | tf_op jit(solution)/shard_map/ppermute | solution.py:22
  76.3 14.3 %down_units.1 = (bf16[512,2048]{1,0:T(8,128)(2,1)}, f32[512,2048]{1,0:T(8,128)}) custom-call(s32[3]{0:T(128)} %pad_add_fusion.where, bf16[512,1536]{1,0:T(8,128)(2,1)} %get-tuple-element.37.hidden, f32[512,128]{1,0:T(8,128)} %get-tuple-element.38.scale, bf16[1,1536,4096]{2,1,0:T(8,128)(2,1)} %down.1), custom_call_target="tpu_custom_call" | custom-call | flops 6442450944 | bytes 18350080 | tf_op jit(solution)/shard_map/down_units/pallas_call | solution.py:260
  90.6 3.1 %half_product.4 = (f32[256,512]{1,0:T(8,128)S(1)}, bf16[256,512]{1,0:T(8,128)(2,1)S(1)}) custom-call(s32[2]{0:T(128)S(1)} %pad_add_fusion.1.where, bf16[1,256,4096]{2,1,0:T(8,128)(2,1)S(1)} %copy-done.1, bf16[64,2048]{1,0:T(8,128)(2,1)S(1)} %collective-permute-done.refs_0_, bf16[64,2048]{1,0:T(8,128)(2,1)S(1)} %collective-permute-done.3.refs_1_, ...), custom_call_target="tpu_custom_call" | custom-call | flops 1073741824 | bytes 4980736 | tf_op jit(solution)/shard_map/half_product/pallas_call | solution.py:84
  94.0 5.0 %half_product.5 = (f32[256,1024]{1,0:T(8,128)S(1)}, bf16[256,1024]{1,0:T(8,128)(2,1)S(1)}) custom-call(s32[2]{0:T(128)S(1)} %pad_add_fusion.1.where, bf16[1,256,4096]{2,1,0:T(8,128)(2,1)S(1)} %copy-done.1, bf16[64,2048]{1,0:T(8,128)(2,1)S(1)} %collective-permute-done.refs_0_, bf16[64,2048]{1,0:T(8,128)(2,1)S(1)} %collective-permute-done.3.refs_1_, ...), custom_call_target="tpu_custom_call" | custom-call | flops 2147483648 | bytes 7864320 | tf_op jit(solution)/shard_map/half_product/pallas_call | solution.py:84
  99.0 0.9 convert_add_fusion
  99.8 0.3 convert.9
  100.3 1.6 %collective-permute-start.20 = (bf16[256,1024]{1,0:T(8,128)(2,1)S(1)}, bf16[256,1024]{1,0:T(8,128)(2,1)S(1)}, u32[]{:S(2)}, u32[]{:S(2)}) collective-permute-start(bf16[256,1024]{1,0:T(8,128)(2,1)S(1)} %pad_maximum_fusion.5), channel_id=1, source_target_pairs={{0,1},{1,0},{2,3},{3,2},{4,5},{5,4},{6,7},{7,6},{8,9},{9,8},{10,11... | collective-permute-start | bytes 1572872 | tf_op jit(solution)/shard_map/ppermute | solution.py:27
  102.1 0.2 collective-permute-start.18
  102.4 1.8 %conv.3.refs_0_ = bf16[1,256,2048]{2,1,0:T(8,128)(2,1)} custom-call(s32[3]{0:T(128)S(1)} %copy-done.7, f32[256,512]{1,0:T(8,128)S(1)} %copy-done.3, bf16[256,512]{1,0:T(8,128)(2,1)S(1)} %collective-permute-done.14.back, bf16[1,3,2048]{2,1,0:T(4,128)(2,1)S(1)} %copy-done.5, f32[4,2048]{1,0:T(4,128)S(1)} %copy-done.4, f32[1,2048]{1,0:T(1,128)S(1)} %bitcast.35), custom_call_target="tpu_custom_call" | custom-call | flops 1572864 | bytes 1048576 | tf_op jit(solution)/shard_map/conv/pallas_call | solution.py:147
  104.2 10.3 %collective-permute-done.20 = bf16[256,1024]{1,0:T(8,128)(2,1)S(1)} collective-permute-done((bf16[256,1024]{1,0:T(8,128)(2,1)S(1)}, bf16[256,1024]{1,0:T(8,128)(2,1)S(1)}, u32[]{:S(2)}, u32[]{:S(2)}) %collective-permute-start.20) | collective-permute-done | bytes 524320 | tf_op jit(solution)/shard_map/ppermute | solution.py:27
  114.5 1.3 collective-permute-done.22
  115.8 0.4 fusion.1
  116.2 0.4 collective-permute-start.21
  116.5 0.5 collective-permute-start.23
  117.1 16.4 %collective-permute-done.18.back = bf16[256,1024]{1,0:T(8,128)(2,1)S(1)} collective-permute-done((bf16[256,1024]{1,0:T(8,128)(2,1)S(1)}, bf16[256,1024]{1,0:T(8,128)(2,1)S(1)}, u32[]{:S(2)}, u32[]{:S(2)}) %collective-permute-start.18) | collective-permute-done | bytes 524320 | tf_op jit(solution)/shard_map/ppermute | solution.py:22
  133.5 0.7 collect.1
  134.3 1.9 %collective-permute-start.25 = (bf16[128,512]{1,0:T(8,128)(2,1)S(1)}, bf16[128,512]{1,0:T(8,128)(2,1)S(1)}, u32[]{:S(2)}, u32[]{:S(2)}) collective-permute-start(bf16[128,512]{1,0:T(8,128)(2,1)S(1)} %get-tuple-element.56), channel_id=1, source_target_pairs={{0,16},{4,20},{8,24},{12,28},{16,0},{20,4},{24,8},{28,12},{1,17},{... | collective-permute-start | bytes 393224 | tf_op jit(solution)/shard_map/ppermute | solution.py:22
  136.3 2.4 %collective-permute-start.26 = (bf16[128,512]{1,0:T(8,128)(2,1)S(1)}, bf16[128,512]{1,0:T(8,128)(2,1)S(1)}, u32[]{:S(2)}, u32[]{:S(2)}) collective-permute-start(bf16[128,512]{1,0:T(8,128)(2,1)S(1)} %get-tuple-element.57), channel_id=1, source_target_pairs={{0,24},{4,28},{8,16},{12,20},{16,8},{20,12},{24,0},{28,4},{1,25},{... | collective-permute-start | bytes 393224 | tf_op jit(solution)/shard_map/ppermute | solution.py:22
  138.7 2.5 %conv.4.refs_0_ = bf16[1,256,2048]{2,1,0:T(8,128)(2,1)} custom-call(s32[3]{0:T(128)S(1)} %copy-done.7, f32[256,1024]{1,0:T(8,128)S(1)} %get-tuple-element.45.own, bf16[256,1024]{1,0:T(8,128)(2,1)S(1)} %collective-permute-done.18.back, bf16[1,3,2048]{2,1,0:T(4,128)(2,1)S(1)} %copy-done.5, f32[4,2048]{1,0:T(4,128)S(1)} %copy-done.4, ...), custom_call_target="tpu_custom_call", output_to_operand_aliasing={{}: (6, {})} | custom-call | flops 3145728 | bytes 2097152 | tf_op jit(solution)/shard_map/conv/pallas_call | solution.py:147
  141.2 3.6 %collective-permute-done.17.back = bf16[256,512]{1,0:T(8,128)(2,1)S(1)} collective-permute-done((bf16[256,512]{1,0:T(8,128)(2,1)S(1)}, bf16[256,512]{1,0:T(8,128)(2,1)S(1)}, u32[]{:S(2)}, u32[]{:S(2)}) %collective-permute-start.17) | collective-permute-done | bytes 262176 | tf_op jit(solution)/shard_map/ppermute | solution.py:22
  144.8 1.8 %conv.5 = bf16[1,256,2048]{2,1,0:T(8,128)(2,1)} custom-call(s32[3]{0:T(128)S(1)} %copy-done.7, f32[256,512]{1,0:T(8,128)S(1)} %get-tuple-element.42.own, bf16[256,512]{1,0:T(8,128)(2,1)S(1)} %collective-permute-done.17.back, bf16[1,3,2048]{2,1,0:T(4,128)(2,1)S(1)} %copy-done.5, f32[4,2048]{1,0:T(4,128)S(1)} %copy-done.4, ...), custom_call_target="tpu_custom_call", output_to_operand_aliasing={{}: (6, {})} | custom-call | flops 1572864 | bytes 1048576 | tf_op jit(solution)/shard_map/conv/pallas_call | solution.py:147
  146.6 1.0 collective-permute-done.25
  147.6 0.7 add_convert_fusion
  (61 shorter events, 1.4 us)
Async XLA Ops:
  0.6 7.6 %copy-start = (bf16[512,2048]{1,0:T(8,128)(2,1)S(1)}, bf16[512,2048]{1,0:T(8,128)(2,1)}, u32[]{:S(2)}) copy-start(bf16[512,2048]{1,0:T(8,128)(2,1)} %refs_3_.5) | copy-start | bytes 6291460
  3.7 11.3 %collective-permute-start.7 = (bf16[128,1152]{1,0:T(8,128)(2,1)S(1)}, bf16[128,1152]{1,0:T(8,128)(2,1)S(1)}, u32[]{:S(2)}, u32[]{:S(2)}) collective-permute-start(bf16[128,1152]{1,0:T(8,128)(2,1)S(1)} %pad_maximum_fusion.6), channel_id=1, source_target_pairs={{0,2},{1,3},{2,0},{3,1},{4,6},{5,7},{6,4},{7,5},{8,10},{9,11},{10,... | collective-permute-start | bytes 884744 | tf_op jit(solution)/shard_map/ppermute | solution.py:27
  6.8 7.8 %collective-permute-start.1 = (bf16[128,1024]{1,0:T(8,128)(2,1)S(1)}, bf16[128,1024]{1,0:T(8,128)(2,1)S(1)}, u32[]{:S(2)}, u32[]{:S(2)}) collective-permute-start(bf16[128,1024]{1,0:T(8,128)(2,1)S(1)} %get-tuple-element.69), channel_id=1, source_target_pairs={{0,1},{1,0},{2,3},{3,2},{4,5},{5,4},{6,7},{7,6},{8,9},{9,8},{10,11... | collective-permute-start | bytes 786440 | tf_op jit(solution)/shard_map/ppermute | solution.py:27
  8.3 22.0 %collective-permute-start.4 = (bf16[512,512]{1,0:T(8,128)(2,1)S(1)}, bf16[512,512]{1,0:T(8,128)(2,1)S(1)}, u32[]{:S(2)}, u32[]{:S(2)}) collective-permute-start(bf16[512,512]{1,0:T(8,128)(2,1)S(1)} %get-tuple-element.67), channel_id=1, source_target_pairs={{0,8},{4,12},{8,0},{12,4},{16,24},{20,28},{24,16},{28,20},{1,9},{5... | collective-permute-start | bytes 1572872 | tf_op jit(solution)/shard_map/ppermute | solution.py:22
  14.6 16.4 %collective-permute-start.2 = (bf16[256,1024]{1,0:T(8,128)(2,1)S(1)}, bf16[256,1024]{1,0:T(8,128)(2,1)S(1)}, u32[]{:S(2)}, u32[]{:S(2)}) collective-permute-start(bf16[256,1024]{1,0:T(8,128)(2,1)S(1)} %pad_maximum_fusion.3), channel_id=1, source_target_pairs={{0,2},{1,3},{2,0},{3,1},{4,6},{5,7},{6,4},{7,5},{8,10},{9,11},{10,... | collective-permute-start | bytes 1572872 | tf_op jit(solution)/shard_map/ppermute | solution.py:27
  15.0 17.0 %collective-permute-start.8 = (bf16[256,1152]{1,0:T(8,128)(2,1)S(1)}, bf16[256,1152]{1,0:T(8,128)(2,1)S(1)}, u32[]{:S(2)}, u32[]{:S(2)}) collective-permute-start(bf16[256,1152]{1,0:T(8,128)(2,1)S(1)} %pad_maximum_fusion.2), channel_id=1, source_target_pairs={{0,1},{1,0},{2,3},{3,2},{4,5},{5,4},{6,7},{7,6},{8,9},{9,8},{10,11... | collective-permute-start | bytes 1769480 | tf_op jit(solution)/shard_map/ppermute | solution.py:27
  16.7 12.9 %collective-permute-start = (bf16[64,2048]{1,0:T(8,128)(2,1)S(1)}, bf16[64,2048]{1,0:T(8,128)(2,1)S(1)}, u32[]{:S(2)}, u32[]{:S(2)}) collective-permute-start(bf16[64,2048]{1,0:T(8,128)(2,1)S(1)} %dynamic-slice_bitcast_fusion), channel_id=1, source_target_pairs={{0,16},{4,20},{8,24},{12,28},{16,0},{20,4},{24,8},{28,12},{1,17},{... | collective-permute-start | bytes 786440 | tf_op jit(solution)/shard_map/ppermute | solution.py:22
  19.3 27.1 %collective-permute-start.6 = (bf16[512,2048]{1,0:T(8,128)(2,1)S(1)}, bf16[512,2048]{1,0:T(8,128)(2,1)}, u32[]{:S(2)}, u32[]{:S(2)}) collective-permute-start(bf16[512,2048]{1,0:T(8,128)(2,1)S(1)} %copy-done), channel_id=1, source_target_pairs={{0,4},{4,0},{8,12},{12,8},{16,20},{20,16},{24,28},{28,24},{1,5},{5... | collective-permute-start | bytes 6291464 | tf_op jit(solution)/shard_map/ppermute | solution.py:22
  29.7 6.4 %collective-permute-start.3 = (bf16[64,2048]{1,0:T(8,128)(2,1)S(1)}, bf16[64,2048]{1,0:T(8,128)(2,1)S(1)}, u32[]{:S(2)}, u32[]{:S(2)}) collective-permute-start(bf16[64,2048]{1,0:T(8,128)(2,1)S(1)} %collective-permute-done.refs_0_), channel_id=1, source_target_pairs={{0,1},{1,0},{2,3},{3,2},{4,5},{5,4},{6,7},{7,6},{8,9},{9,8},{10,11... | collective-permute-start | bytes 786440 | tf_op jit(solution)/shard_map/ppermute | solution.py:27
  30.3 10.7 %collective-permute-start.5 = (bf16[512,512]{1,0:T(8,128)(2,1)S(1)}, bf16[512,512]{1,0:T(8,128)(2,1)}, u32[]{:S(2)}, u32[]{:S(2)}) collective-permute-start(bf16[512,512]{1,0:T(8,128)(2,1)S(1)} %get-tuple-element.31), channel_id=1, source_target_pairs={{0,8},{4,12},{8,0},{12,4},{16,24},{20,28},{24,16},{28,20},{1,9},{5... | collective-permute-start | bytes 1572872 | tf_op jit(solution)/shard_map/ppermute | solution.py:22
  32.2 9.9 %copy-start.8 = (bf16[512,1152]{1,0:T(8,128)(2,1)}, bf16[512,1152]{1,0:T(8,128)(2,1)S(1)}, u32[]{:S(2)}) copy-start(bf16[512,1152]{1,0:T(8,128)(2,1)S(1)} %pad_maximum_fusion.refs_1_) | copy-start | bytes 3538948
  33.4 13.0 %collective-permute-start.10 = (bf16[512,1024]{1,0:T(8,128)(2,1)}, bf16[512,1024]{1,0:T(8,128)(2,1)}, u32[]{:S(2)}, u32[]{:S(2)}) collective-permute-start(bf16[512,1024]{1,0:T(8,128)(2,1)} %slice.87), channel_id=1, source_target_pairs={{0,4},{4,0},{8,12},{12,8},{16,20},{20,16},{24,28},{28,24},{1,5},{5... | collective-permute-start | bytes 3145736 | tf_op jit(solution)/shard_map/ppermute | solution.py:22
  41.0 6.0 %collective-permute-start.9 = (bf16[512,1024]{1,0:T(8,128)(2,1)}, bf16[512,1024]{1,0:T(8,128)(2,1)}, u32[]{:S(2)}, u32[]{:S(2)}) collective-permute-start(bf16[512,1024]{1,0:T(8,128)(2,1)} %pad_maximum_fusion.1.refs_0_), channel_id=1, source_target_pairs={{0,4},{4,0},{8,12},{12,8},{16,20},{20,16},{24,28},{28,24},{1,5},{5... | collective-permute-start | bytes 3145736 | tf_op jit(solution)/shard_map/ppermute | solution.py:22
  42.0 30.8 %collective-permute-start.15 = (bf16[512,1024]{1,0:T(8,128)(2,1)}, bf16[512,1024]{1,0:T(8,128)(2,1)}, u32[]{:S(2)}, u32[]{:S(2)}) collective-permute-start(bf16[512,1024]{1,0:T(8,128)(2,1)} %slice.73), channel_id=1, source_target_pairs={{0,8},{4,12},{8,0},{12,4},{16,24},{20,28},{24,16},{28,20},{1,9},{5... | collective-permute-start | bytes 3145736 | tf_op jit(solution)/shard_map/ppermute | solution.py:22
  44.3 24.9 %collective-permute-start.12 = (bf16[128,2048]{1,0:T(8,128)(2,1)S(1)}, bf16[128,2048]{1,0:T(8,128)(2,1)S(1)}, u32[]{:S(2)}, u32[]{:S(2)}) collective-permute-start(bf16[128,2048]{1,0:T(8,128)(2,1)S(1)} %pad_maximum_fusion.4), channel_id=1, source_target_pairs={{0,2},{1,3},{2,0},{3,1},{4,6},{5,7},{6,4},{7,5},{8,10},{9,11},{10,... | collective-permute-start | bytes 1572872 | tf_op jit(solution)/shard_map/ppermute | solution.py:27
  46.4 22.7 %collective-permute-start.13 = (bf16[512,512]{1,0:T(8,128)(2,1)S(1)}, bf16[512,512]{1,0:T(8,128)(2,1)S(1)}, u32[]{:S(2)}, u32[]{:S(2)}) collective-permute-start(bf16[512,512]{1,0:T(8,128)(2,1)S(1)} %collective-permute-done.4.refs_5_), channel_id=1, source_target_pairs={{0,4},{4,0},{8,12},{12,8},{16,20},{20,16},{24,28},{28,24},{1,5},{5... | collective-permute-start | bytes 1572872 | tf_op jit(solution)/shard_map/ppermute | solution.py:22
  46.4 22.7 %collective-permute-start.11 = (bf16[512,512]{1,0:T(8,128)(2,1)}, bf16[512,512]{1,0:T(8,128)(2,1)S(1)}, u32[]{:S(2)}, u32[]{:S(2)}) collective-permute-start(bf16[512,512]{1,0:T(8,128)(2,1)} %collective-permute-done.5.refs_5_), channel_id=1, source_target_pairs={{0,4},{4,0},{8,12},{12,8},{16,20},{20,16},{24,28},{28,24},{1,5},{5... | collective-permute-start | bytes 1572872 | tf_op jit(solution)/shard_map/ppermute | solution.py:22
  46.9 22.2 %copy-start.1 = (bf16[1,256,4096]{2,1,0:T(8,128)(2,1)S(1)}, bf16[1,256,4096]{2,1,0:T(8,128)(2,1)}, u32[]{:S(2)}) copy-start(bf16[1,256,4096]{2,1,0:T(8,128)(2,1)} %window.5) | copy-start | bytes 6291460
  72.1 0.8 copy-start.2
  72.9 17.7 %collective-permute-start.16 = (bf16[512,1024]{1,0:T(8,128)(2,1)}, bf16[512,1024]{1,0:T(8,128)(2,1)S(1)}, u32[]{:S(2)}, u32[]{:S(2)}) collective-permute-start(bf16[512,1024]{1,0:T(8,128)(2,1)} %collective-permute-done.15.refs_5_), channel_id=1, source_target_pairs={{0,4},{4,0},{8,12},{12,8},{16,20},{20,16},{24,28},{28,24},{1,5},{5... | collective-permute-start | bytes 3145736 | tf_op jit(solution)/shard_map/ppermute | solution.py:22
  73.0 17.7 %collective-permute-start.14 = (bf16[256,512]{1,0:T(8,128)(2,1)S(1)}, bf16[256,512]{1,0:T(8,128)(2,1)S(1)}, u32[]{:S(2)}, u32[]{:S(2)}) collective-permute-start(bf16[256,512]{1,0:T(8,128)(2,1)S(1)} %get-tuple-element.36), channel_id=1, source_target_pairs={{0,16},{4,20},{8,24},{12,28},{16,0},{20,4},{24,8},{28,12},{1,17},{... | collective-permute-start | bytes 786440 | tf_op jit(solution)/shard_map/ppermute | solution.py:22
  90.6 3.1 %copy-start.10 = (bf16[512,2048]{1,0:T(8,128)(2,1)S(1)}, bf16[512,2048]{1,0:T(8,128)(2,1)}, u32[]{:S(2)}) copy-start(bf16[512,2048]{1,0:T(8,128)(2,1)} %get-tuple-element.50) | copy-start | bytes 6291460
  93.7 5.2 %collective-permute-start.19 = (bf16[512,2048]{1,0:T(8,128)(2,1)S(1)}, bf16[512,2048]{1,0:T(8,128)(2,1)S(1)}, u32[]{:S(2)}, u32[]{:S(2)}) collective-permute-start(bf16[512,2048]{1,0:T(8,128)(2,1)S(1)} %copy-done.10), channel_id=1, source_target_pairs={{0,4},{4,0},{8,12},{12,8},{16,20},{20,16},{24,28},{28,24},{1,5},{5... | collective-permute-start | bytes 6291464 | tf_op jit(solution)/shard_map/ppermute | solution.py:22
  94.0 5.0 %copy-start.9 = (f32[512,2048]{1,0:T(8,128)S(1)}, f32[512,2048]{1,0:T(8,128)}, u32[]{:S(2)}) copy-start(f32[512,2048]{1,0:T(8,128)} %get-tuple-element.39) | copy-start | bytes 12582916
  100.2 2.2 %copy-start.3 = (f32[256,512]{1,0:T(8,128)S(1)}, f32[256,512]{1,0:T(8,128)}, u32[]{:S(2)}) copy-start(f32[256,512]{1,0:T(8,128)} %copy-done.2) | copy-start | bytes 1572868
  100.2 2.2 %copy-start.4 = (f32[4,2048]{1,0:T(4,128)S(1)}, f32[4,2048]{1,0:T(4,128)}, u32[]{:S(2)}) copy-start(f32[4,2048]{1,0:T(4,128)} %taps.5) | copy-start | bytes 98308
  100.2 2.2 %copy-start.5 = (bf16[1,3,2048]{2,1,0:T(4,128)(2,1)S(1)}, bf16[1,3,2048]{2,1,0:T(4,128)(2,1)}, u32[]{:S(2)}) copy-start(bf16[1,3,2048]{2,1,0:T(4,128)(2,1)} %state.5) | copy-start | bytes 36868
  100.2 2.2 %copy-start.6 = (f32[2048]{0:T(1024)S(1)}, f32[2048]{0:T(1024)}, u32[]{:S(2)}) copy-start(f32[2048]{0:T(1024)} %param.15) | copy-start | bytes 24580
  100.2 2.1 %copy-start.7 = (s32[3]{0:T(128)S(1)}, s32[3]{0:T(128)}, u32[]{:S(2)}) copy-start(s32[3]{0:T(128)} %pad_add_fusion.where) | copy-start | bytes 40
  100.3 14.2 %collective-permute-start.20 = (bf16[256,1024]{1,0:T(8,128)(2,1)S(1)}, bf16[256,1024]{1,0:T(8,128)(2,1)S(1)}, u32[]{:S(2)}, u32[]{:S(2)}) collective-permute-start(bf16[256,1024]{1,0:T(8,128)(2,1)S(1)} %pad_maximum_fusion.5), channel_id=1, source_target_pairs={{0,1},{1,0},{2,3},{3,2},{4,5},{5,4},{6,7},{7,6},{8,9},{9,8},{10,11... | collective-permute-start | bytes 1572872 | tf_op jit(solution)/shard_map/ppermute | solution.py:27
  101.9 13.9 %collective-permute-start.22 = (bf16[256,1024]{1,0:T(8,128)(2,1)S(1)}, bf16[256,1024]{1,0:T(8,128)(2,1)S(1)}, u32[]{:S(2)}, u32[]{:S(2)}) collective-permute-start(bf16[256,1024]{1,0:T(8,128)(2,1)S(1)} %bitcast.40), channel_id=1, source_target_pairs={{0,2},{1,3},{2,0},{3,1},{4,6},{5,7},{6,4},{7,5},{8,10},{9,11},{10,... | collective-permute-start | bytes 1572872 | tf_op jit(solution)/shard_map/ppermute | solution.py:27
  102.1 31.4 %collective-permute-start.18 = (bf16[256,1024]{1,0:T(8,128)(2,1)S(1)}, bf16[256,1024]{1,0:T(8,128)(2,1)S(1)}, u32[]{:S(2)}, u32[]{:S(2)}) collective-permute-start(bf16[256,1024]{1,0:T(8,128)(2,1)S(1)} %get-tuple-element.46), channel_id=1, source_target_pairs={{0,16},{4,20},{8,24},{12,28},{16,0},{20,4},{24,8},{28,12},{1,17},{... | collective-permute-start | bytes 1572872 | tf_op jit(solution)/shard_map/ppermute | solution.py:22
  116.2 17.3 %collective-permute-start.21 = (bf16[128,1024]{1,0:T(8,128)(2,1)S(1)}, bf16[128,1024]{1,0:T(8,128)(2,1)S(1)}, u32[]{:S(2)}, u32[]{:S(2)}) collective-permute-start(bf16[128,1024]{1,0:T(8,128)(2,1)S(1)} %get-tuple-element.63), channel_id=1, source_target_pairs={{0,2},{1,3},{2,0},{3,1},{4,6},{5,7},{6,4},{7,5},{8,10},{9,11},{10,... | collective-permute-start | bytes 786440 | tf_op jit(solution)/shard_map/ppermute | solution.py:27
  116.5 17.0 %collective-permute-start.23 = (bf16[128,1024]{1,0:T(8,128)(2,1)S(1)}, bf16[128,1024]{1,0:T(8,128)(2,1)S(1)}, u32[]{:S(2)}, u32[]{:S(2)}) collective-permute-start(bf16[128,1024]{1,0:T(8,128)(2,1)S(1)} %get-tuple-element.58), channel_id=1, source_target_pairs={{0,1},{1,0},{2,3},{3,2},{4,5},{5,4},{6,7},{7,6},{8,9},{9,8},{10,11... | collective-permute-start | bytes 786440 | tf_op jit(solution)/shard_map/ppermute | solution.py:27
  117.1 27.7 %collective-permute-start.17 = (bf16[256,512]{1,0:T(8,128)(2,1)S(1)}, bf16[256,512]{1,0:T(8,128)(2,1)S(1)}, u32[]{:S(2)}, u32[]{:S(2)}) collective-permute-start(bf16[256,512]{1,0:T(8,128)(2,1)S(1)} %get-tuple-element.43), channel_id=1, source_target_pairs={{0,16},{4,20},{8,24},{12,28},{16,0},{20,4},{24,8},{28,12},{1,17},{... | collective-permute-start | bytes 786440 | tf_op jit(solution)/shard_map/ppermute | solution.py:22
  134.3 12.4 %collective-permute-start.24 = (bf16[128,512]{1,0:T(8,128)(2,1)S(1)}, bf16[128,512]{1,0:T(8,128)(2,1)S(1)}, u32[]{:S(2)}, u32[]{:S(2)}) collective-permute-start(bf16[128,512]{1,0:T(8,128)(2,1)S(1)} %get-tuple-element.55), channel_id=1, source_target_pairs={{0,8},{4,12},{8,0},{12,4},{16,24},{20,28},{24,16},{28,20},{1,9},{5... | collective-permute-start | bytes 393224 | tf_op jit(solution)/shard_map/ppermute | solution.py:22
  134.3 13.3 %collective-permute-start.25 = (bf16[128,512]{1,0:T(8,128)(2,1)S(1)}, bf16[128,512]{1,0:T(8,128)(2,1)S(1)}, u32[]{:S(2)}, u32[]{:S(2)}) collective-permute-start(bf16[128,512]{1,0:T(8,128)(2,1)S(1)} %get-tuple-element.56), channel_id=1, source_target_pairs={{0,16},{4,20},{8,24},{12,28},{16,0},{20,4},{24,8},{28,12},{1,17},{... | collective-permute-start | bytes 393224 | tf_op jit(solution)/shard_map/ppermute | solution.py:22
  136.3 11.4 %collective-permute-start.26 = (bf16[128,512]{1,0:T(8,128)(2,1)S(1)}, bf16[128,512]{1,0:T(8,128)(2,1)S(1)}, u32[]{:S(2)}, u32[]{:S(2)}) collective-permute-start(bf16[128,512]{1,0:T(8,128)(2,1)S(1)} %get-tuple-element.57), channel_id=1, source_target_pairs={{0,24},{4,28},{8,16},{12,20},{16,8},{20,12},{24,0},{28,4},{1,25},{... | collective-permute-start | bytes 393224 | tf_op jit(solution)/shard_map/ppermute | solution.py:22

commit v5 on v4

--- a/solution.py
+++ b/solution.py
@@ -14,7 +14,7 @@
 VMEM = 24 << 20
 VMEM_ALL = 56 << 20
 SMEM_SPEC = pl.BlockSpec(memory_space=pltpu.SMEM)
-CHUNKS = (1, 1, 2)
+CHUNKS = (3, 1, 4)
 
 
 def xor_send(value, mask):

time: 149 us -> 151 us (1.013)
  waiting for transfers between devices: 55 us -> 51.5 us
  other arithmetic: 4.99 us -> 7.04 us
  starting transfers between devices: 27.3 us -> 28.9 us
    ppermute x10, waiting for transfers between devices: 18.7 us -> 12.3 us  [owner_send(): return lax.ppermute(value, 'expert', pairs)]
    ppermute x17, waiting for transfers between devices: 36.3 us -> 39.2 us  [xor_send(): return lax.ppermute(value, 'dp', pairs)]
    ppermute x10, starting transfers between devices: 12.1 us -> 14.2 us  [owner_send(): return lax.ppermute(value, 'expert', pairs)]
  transfers between devices with their start and end apart: 27 -> 27, of which waited for: 9 -> 9; matrix products, arithmetic and copies ran while one was open for 3% -> 5% of each run, Pallas kernels for 35% -> 35%
where the time goes in v5:
time: 151 us; the launch traced here: 150 us
  Pallas kernels  55.1 us (36%)
  waiting for transfers between devices  51.5 us (34%)
  starting transfers between devices  28.9 us (19%)
  other arithmetic  7.04 us (5%)
  local copies, waits for them, and re-layouts  6.58 us (4%)
    ppermute x17, waiting for transfers between devices, xor_send(): return lax.ppermute(value, 'dp', pairs)  39.2 us
    pallas_call x1, Pallas kernels, hidden_units(): pl.pallas_call(functools.partial(hidden_kernel, quarter), grid_spec=pltpu...  22.1 us
    ppermute x17, starting transfers between devices, xor_send(): return lax.ppermute(value, 'dp', pairs)  14.7 us
    pallas_call x1, Pallas kernels, down_units(): pl.pallas_call(functools.partial(down_kernel, steps), grid_spec=pltpu.Pre...  14.3 us
    ppermute x10, starting transfers between devices, owner_send(): return lax.ppermute(value, 'expert', pairs)  14.2 us
    ppermute x10, waiting for transfers between devices, owner_send(): return lax.ppermute(value, 'expert', pairs)  12.3 us
    pallas_call x3, Pallas kernels, half_product(): pl.pallas_call(functools.partial(half_product_kernel, len(weights), depth...  11.6 us
    pallas_call x3, Pallas kernels, conv(): pl.pallas_call(functools.partial(conv_kernel_body, pad, pieces), grid=(co...  6.42 us
  transfers between devices with their start and end apart: 27, of which 9 were waited for; matrix products, arithmetic and copies ran while one was open for 5% of the time, Pallas kernels for 35%

profile of v5, /device:TPU:0, one launch (start us, length us, event | category | flops | bytes accessed | tf_op | source)
XLA Modules:
  0.0 150.1 jit_solution(17154587729470427211)
XLA Ops:
  0.7 1.8 %dynamic-slice_bitcast_fusion = bf16[64,2048]{1,0:T(8,128)(2,1)} fusion(bf16[1,256,4096]{2,1,0:T(8,128)(2,1)} %window.5, s32[]{:T(128)S(6)} %select_n.17, s32[]{:T(128)S(6)} %select_n.18), kind=kLoop, calls=%fused_computation.21 | loop fusion | bytes 524296 | tf_op jit(solution)/shard_map/squeeze | solution.py:354
  2.5 1.1 constant_dynamic-slice_fusion
  3.6 3.0 %collective-permute-start.1 = (bf16[128,1024]{1,0:T(8,128)(2,1)S(1)}, bf16[128,1024]{1,0:T(8,128)(2,1)}, u32[]{:S(2)}, u32[]{:S(2)}) collective-permute-start(bf16[128,1024]{1,0:T(8,128)(2,1)S(1)} %get-tuple-element.67), channel_id=1, source_target_pairs={{0,1},{1,0},{2,3},{3,2},{4,5},{5,4},{6,7},{7,6},{8,9},{9,8},{10,11... | collective-permute-start | bytes 786440 | tf_op jit(solution)/shard_map/ppermute | solution.py:27
  6.6 0.7 convert_element_type.43
  7.4 1.6 %collective-permute-start.7 = (bf16[128,1152]{1,0:T(8,128)(2,1)S(1)}, bf16[128,1152]{1,0:T(8,128)(2,1)S(1)}, u32[]{:S(2)}, u32[]{:S(2)}) collective-permute-start(bf16[128,1152]{1,0:T(8,128)(2,1)S(1)} %pad_maximum_fusion.6), channel_id=1, source_target_pairs={{0,2},{1,3},{2,0},{3,1},{4,6},{5,7},{6,4},{7,5},{8,10},{9,11},{10,... | collective-permute-start | bytes 884744 | tf_op jit(solution)/shard_map/ppermute | solution.py:27
  9.1 1.6 %collective-permute-start.4 = (bf16[512,768]{1,0:T(8,128)(2,1)S(1)}, bf16[512,768]{1,0:T(8,128)(2,1)S(1)}, u32[]{:S(2)}, u32[]{:S(2)}) collective-permute-start(bf16[512,768]{1,0:T(8,128)(2,1)S(1)} %slice.68), channel_id=1, source_target_pairs={{0,8},{4,12},{8,0},{12,4},{16,24},{20,28},{24,16},{28,20},{1,9},{5... | collective-permute-start | bytes 2359304 | tf_op jit(solution)/shard_map/ppermute | solution.py:22
  10.8 2.2 %collective-permute-done.1 = bf16[128,1024]{1,0:T(8,128)(2,1)} collective-permute-done((bf16[128,1024]{1,0:T(8,128)(2,1)S(1)}, bf16[128,1024]{1,0:T(8,128)(2,1)}, u32[]{:S(2)}, u32[]{:S(2)}) %collective-permute-start.1) | collective-permute-done | bytes 262176 | tf_op jit(solution)/shard_map/ppermute | solution.py:27
  13.0 1.0 pad_maximum_fusion.3
  14.0 1.8 %collective-permute-start.2 = (bf16[256,1024]{1,0:T(8,128)(2,1)S(1)}, bf16[256,1024]{1,0:T(8,128)(2,1)S(1)}, u32[]{:S(2)}, u32[]{:S(2)}) collective-permute-start(bf16[256,1024]{1,0:T(8,128)(2,1)S(1)} %pad_maximum_fusion.3), channel_id=1, source_target_pairs={{0,2},{1,3},{2,0},{3,1},{4,6},{5,7},{6,4},{7,5},{8,10},{9,11},{10,... | collective-permute-start | bytes 1572872 | tf_op jit(solution)/shard_map/ppermute | solution.py:27
  15.8 0.2 collective-permute-done.7
  16.1 1.4 collective-permute-start.8
  17.4 2.6 %collective-permute-start = (bf16[64,2048]{1,0:T(8,128)(2,1)S(1)}, bf16[64,2048]{1,0:T(8,128)(2,1)S(1)}, u32[]{:S(2)}, u32[]{:S(2)}) collective-permute-start(bf16[64,2048]{1,0:T(8,128)(2,1)S(1)} %copy-done.13), channel_id=1, source_target_pairs={{0,16},{4,20},{8,24},{12,28},{16,0},{20,4},{24,8},{28,12},{1,17},{... | collective-permute-start | bytes 786440 | tf_op jit(solution)/shard_map/ppermute | solution.py:22
  20.1 12.5 %collective-permute-done.refs_0_ = bf16[64,2048]{1,0:T(8,128)(2,1)S(1)} collective-permute-done((bf16[64,2048]{1,0:T(8,128)(2,1)S(1)}, bf16[64,2048]{1,0:T(8,128)(2,1)S(1)}, u32[]{:S(2)}, u32[]{:S(2)}) %collective-permute-start) | collective-permute-done | bytes 262176 | tf_op jit(solution)/shard_map/ppermute | solution.py:22
  32.6 0.5 collective-permute-start.3
  33.2 2.1 %pad_maximum_fusion.1.refs_0_ = bf16[512,1024]{1,0:T(8,128)(2,1)} fusion(bf16[256,1024]{1,0:T(8,128)(2,1)S(1)} %collective-permute-done.2, bf16[128,1024]{1,0:T(8,128)(2,1)} %collective-permute-done.1, bf16[128,1024]{1,0:T(8,128)(2,1)} %copy-done.12), kind=kLoop, calls=%fused_computation.2 | loop fusion | flops 3145728 | bytes 2097152 | tf_op jit(solution)/shard_map/concatenate | solution.py:395
  35.2 3.5 %collective-permute-start.5 = (bf16[512,256]{1,0:T(8,128)(2,1)S(1)}, bf16[512,256]{1,0:T(8,128)(2,1)}, u32[]{:S(2)}, u32[]{:S(2)}) collective-permute-start(bf16[512,256]{1,0:T(8,128)(2,1)S(1)} %slice.69), channel_id=1, source_target_pairs={{0,8},{4,12},{8,0},{12,4},{16,24},{20,28},{24,16},{28,20},{1,9},{5... | collective-permute-start | bytes 786440 | tf_op jit(solution)/shard_map/ppermute | solution.py:22
  38.9 1.3 slice.87
  40.2 3.2 %collective-permute-done.5.refs_5_ = bf16[512,256]{1,0:T(8,128)(2,1)} collective-permute-done((bf16[512,256]{1,0:T(8,128)(2,1)S(1)}, bf16[512,256]{1,0:T(8,128)(2,1)}, u32[]{:S(2)}, u32[]{:S(2)}) %collective-permute-start.5) | collective-permute-done | bytes 262176 | tf_op jit(solution)/shard_map/ppermute | solution.py:22
  43.4 1.1 slice.73
  44.5 1.8 %collective-permute-start.15 = (bf16[512,1024]{1,0:T(8,128)(2,1)}, bf16[512,1024]{1,0:T(8,128)(2,1)}, u32[]{:S(2)}, u32[]{:S(2)}) collective-permute-start(bf16[512,1024]{1,0:T(8,128)(2,1)} %slice.73), channel_id=1, source_target_pairs={{0,8},{4,12},{8,0},{12,4},{16,24},{20,28},{24,16},{28,20},{1,9},{5... | collective-permute-start | bytes 3145736 | tf_op jit(solution)/shard_map/ppermute | solution.py:22
  46.4 0.7 pad_add_fusion.where
  47.1 0.6 collective-permute-start.12
  47.6 0.5 collective-permute-start.11
  48.2 22.1 %hidden_units.1 = (bf16[512,1536]{1,0:T(8,128)(2,1)}, f32[512,128]{1,0:T(8,128)}) custom-call(s32[3]{0:T(128)} %pad_add_fusion.where, bf16[512,1024]{1,0:T(8,128)(2,1)} %pad_maximum_fusion.1.refs_0_, bf16[512,1152]{1,0:T(8,128)(2,1)} %copy-done.8, bf16[512,1024]{1,0:T(8,128)(2,1)} %collective-permute-done.9.refs_2_, ...), custom_call_target="tpu_custom_call" | custom-call | flops 12884901888 | bytes 33554432 | tf_op jit(solution)/shard_map/hidden_units/pallas_call | solution.py:214
  70.4 4.2 %half_product.3 = (f32[256,768]{1,0:T(8,128)S(1)}, bf16[256,768]{1,0:T(8,128)(2,1)S(1)}) custom-call(s32[2]{0:T(128)S(1)} %pad_add_fusion.1.where, bf16[1,256,4096]{2,1,0:T(8,128)(2,1)S(1)} %copy-done.1, bf16[64,2048]{1,0:T(8,128)(2,1)S(1)} %collective-permute-done.refs_0_, bf16[64,2048]{1,0:T(8,128)(2,1)S(1)} %collective-permute-done.3.refs_1_, ...), custom_call_target="tpu_custom_call" | custom-call | flops 1610612736 | bytes 6422528 | tf_op jit(solution)/shard_map/half_product/pallas_call | solution.py:84
  74.6 0.9 copy-done.2
  75.6 14.3 %down_units.1 = (bf16[512,2048]{1,0:T(8,128)(2,1)}, f32[512,2048]{1,0:T(8,128)}) custom-call(s32[3]{0:T(128)} %pad_add_fusion.where, bf16[512,1536]{1,0:T(8,128)(2,1)} %get-tuple-element.37.hidden, f32[512,128]{1,0:T(8,128)} %get-tuple-element.38.scale, bf16[1,1536,4096]{2,1,0:T(8,128)(2,1)} %down.1), custom_call_target="tpu_custom_call" | custom-call | flops 6442450944 | bytes 18350080 | tf_op jit(solution)/shard_map/down_units/pallas_call | solution.py:260
  89.8 6.1 %collective-permute-done.14.back = bf16[256,768]{1,0:T(8,128)(2,1)S(1)} collective-permute-done((bf16[256,768]{1,0:T(8,128)(2,1)S(1)}, bf16[256,768]{1,0:T(8,128)(2,1)S(1)}, u32[]{:S(2)}, u32[]{:S(2)}) %collective-permute-start.14) | collective-permute-done | bytes 393248 | tf_op jit(solution)/shard_map/ppermute | solution.py:22
  95.9 2.4 %half_product.4 = (f32[256,256]{1,0:T(8,128)S(1)}, bf16[256,256]{1,0:T(8,128)(2,1)S(1)}) custom-call(s32[2]{0:T(128)S(1)} %pad_add_fusion.1.where, bf16[1,256,4096]{2,1,0:T(8,128)(2,1)S(1)} %copy-done.1, bf16[64,2048]{1,0:T(8,128)(2,1)S(1)} %collective-permute-done.refs_0_, bf16[64,2048]{1,0:T(8,128)(2,1)S(1)} %collective-permute-done.3.refs_1_, ...), custom_call_target="tpu_custom_call" | custom-call | flops 536870912 | bytes 3538944 | tf_op jit(solution)/shard_map/half_product/pallas_call | solution.py:84
  98.5 5.0 %half_product.5 = (f32[256,1024]{1,0:T(8,128)S(1)}, bf16[256,1024]{1,0:T(8,128)(2,1)S(1)}) custom-call(s32[2]{0:T(128)S(1)} %pad_add_fusion.1.where, bf16[1,256,4096]{2,1,0:T(8,128)(2,1)S(1)} %copy-done.1, bf16[64,2048]{1,0:T(8,128)(2,1)S(1)} %collective-permute-done.refs_0_, bf16[64,2048]{1,0:T(8,128)(2,1)S(1)} %collective-permute-done.3.refs_1_, ...), custom_call_target="tpu_custom_call" | custom-call | flops 2147483648 | bytes 7864320 | tf_op jit(solution)/shard_map/half_product/pallas_call | solution.py:84
  103.5 0.9 convert_add_fusion
  104.3 0.3 convert.9
  104.8 1.6 %collective-permute-start.20 = (bf16[256,1024]{1,0:T(8,128)(2,1)S(1)}, bf16[256,1024]{1,0:T(8,128)(2,1)S(1)}, u32[]{:S(2)}, u32[]{:S(2)}) collective-permute-start(bf16[256,1024]{1,0:T(8,128)(2,1)S(1)} %pad_maximum_fusion.5), channel_id=1, source_target_pairs={{0,1},{1,0},{2,3},{3,2},{4,5},{5,4},{6,7},{7,6},{8,9},{9,8},{10,11... | collective-permute-start | bytes 1572872 | tf_op jit(solution)/shard_map/ppermute | solution.py:27
  106.4 1.6 %collective-permute-start.22 = (bf16[256,1024]{1,0:T(8,128)(2,1)S(1)}, bf16[256,1024]{1,0:T(8,128)(2,1)S(1)}, u32[]{:S(2)}, u32[]{:S(2)}) collective-permute-start(bf16[256,1024]{1,0:T(8,128)(2,1)S(1)} %bitcast.40), channel_id=1, source_target_pairs={{0,2},{1,3},{2,0},{3,1},{4,6},{5,7},{6,4},{7,5},{8,10},{9,11},{10,... | collective-permute-start | bytes 1572872 | tf_op jit(solution)/shard_map/ppermute | solution.py:27
  108.0 2.4 %conv.3.refs_0_ = bf16[1,256,2048]{2,1,0:T(8,128)(2,1)} custom-call(s32[3]{0:T(128)S(1)} %copy-done.7, f32[256,768]{1,0:T(8,128)S(1)} %copy-done.3, bf16[256,768]{1,0:T(8,128)(2,1)S(1)} %collective-permute-done.14.back, bf16[1,3,2048]{2,1,0:T(4,128)(2,1)S(1)} %copy-done.5, f32[4,2048]{1,0:T(4,128)S(1)} %copy-done.4, f32[1,2048]{1,0:T(1,128)S(1)} %bitcast.35), custom_call_target="tpu_custom_call" | custom-call | flops 2359296 | bytes 1572864 | tf_op jit(solution)/shard_map/conv/pallas_call | solution.py:147
  110.5 8.6 %collective-permute-done.20 = bf16[256,1024]{1,0:T(8,128)(2,1)S(1)} collective-permute-done((bf16[256,1024]{1,0:T(8,128)(2,1)S(1)}, bf16[256,1024]{1,0:T(8,128)(2,1)S(1)}, u32[]{:S(2)}, u32[]{:S(2)}) %collective-permute-start.20) | collective-permute-done | bytes 524320 | tf_op jit(solution)/shard_map/ppermute | solution.py:27
  119.1 1.3 collective-permute-done.22
  120.4 0.4 fusion.1
  120.8 1.6 %collective-permute-start.21 = (bf16[128,1024]{1,0:T(8,128)(2,1)S(1)}, bf16[128,1024]{1,0:T(8,128)(2,1)S(1)}, u32[]{:S(2)}, u32[]{:S(2)}) collective-permute-start(bf16[128,1024]{1,0:T(8,128)(2,1)S(1)} %get-tuple-element.63), channel_id=1, source_target_pairs={{0,2},{1,3},{2,0},{3,1},{4,6},{5,7},{6,4},{7,5},{8,10},{9,11},{10,... | collective-permute-start | bytes 786440 | tf_op jit(solution)/shard_map/ppermute | solution.py:27
  122.4 0.5 collective-permute-start.23
  122.9 12.7 %collective-permute-done.18.back = bf16[256,1024]{1,0:T(8,128)(2,1)S(1)} collective-permute-done((bf16[256,1024]{1,0:T(8,128)(2,1)S(1)}, bf16[256,1024]{1,0:T(8,128)(2,1)S(1)}, u32[]{:S(2)}, u32[]{:S(2)}) %collective-permute-start.18) | collective-permute-done | bytes 524320 | tf_op jit(solution)/shard_map/ppermute | solution.py:22
  135.6 0.7 collect.1
  136.4 2.8 %collective-permute-start.25 = (bf16[128,512]{1,0:T(8,128)(2,1)S(1)}, bf16[128,512]{1,0:T(8,128)(2,1)S(1)}, u32[]{:S(2)}, u32[]{:S(2)}) collective-permute-start(bf16[128,512]{1,0:T(8,128)(2,1)S(1)} %get-tuple-element.56), channel_id=1, source_target_pairs={{0,16},{4,20},{8,24},{12,28},{16,0},{20,4},{24,8},{28,12},{1,17},{... | collective-permute-start | bytes 393224 | tf_op jit(solution)/shard_map/ppermute | solution.py:22
  139.2 1.6 %collective-permute-start.26 = (bf16[128,512]{1,0:T(8,128)(2,1)S(1)}, bf16[128,512]{1,0:T(8,128)(2,1)S(1)}, u32[]{:S(2)}, u32[]{:S(2)}) collective-permute-start(bf16[128,512]{1,0:T(8,128)(2,1)S(1)} %get-tuple-element.57), channel_id=1, source_target_pairs={{0,24},{4,28},{8,16},{12,20},{16,8},{20,12},{24,0},{28,4},{1,25},{... | collective-permute-start | bytes 393224 | tf_op jit(solution)/shard_map/ppermute | solution.py:22
  140.8 2.5 %conv.4.refs_0_ = bf16[1,256,2048]{2,1,0:T(8,128)(2,1)} custom-call(s32[3]{0:T(128)S(1)} %copy-done.7, f32[256,1024]{1,0:T(8,128)S(1)} %get-tuple-element.45.own, bf16[256,1024]{1,0:T(8,128)(2,1)S(1)} %collective-permute-done.18.back, bf16[1,3,2048]{2,1,0:T(4,128)(2,1)S(1)} %copy-done.5, f32[4,2048]{1,0:T(4,128)S(1)} %copy-done.4, ...), custom_call_target="tpu_custom_call", output_to_operand_aliasing={{}: (6, {})} | custom-call | flops 3145728 | bytes 2097152 | tf_op jit(solution)/shard_map/conv/pallas_call | solution.py:147
  143.3 1.5 conv.5
  144.8 4.6 %collective-permute-done.25 = bf16[128,512]{1,0:T(8,128)(2,1)S(1)} collective-permute-done((bf16[128,512]{1,0:T(8,128)(2,1)S(1)}, bf16[128,512]{1,0:T(8,128)(2,1)S(1)}, u32[]{:S(2)}, u32[]{:S(2)}) %collective-permute-start.25) | collective-permute-done | bytes 131104 | tf_op jit(solution)/shard_map/ppermute | solution.py:22
  149.4 0.7 add_convert_fusion
  (70 shorter events, 1.1 us)
Async XLA Ops:
  0.6 8.4 %copy-start = (bf16[512,2048]{1,0:T(8,128)(2,1)S(1)}, bf16[512,2048]{1,0:T(8,128)(2,1)}, u32[]{:S(2)}) copy-start(bf16[512,2048]{1,0:T(8,128)(2,1)} %refs_3_.5) | copy-start | bytes 6291460
  3.5 12.5 %copy-start.9 = (bf16[128,1024]{1,0:T(8,128)(2,1)}, bf16[128,1024]{1,0:T(8,128)(2,1)S(1)}, u32[]{:S(2)}) copy-start(bf16[128,1024]{1,0:T(8,128)(2,1)S(1)} %get-tuple-element.66) | copy-start | bytes 786436
  3.6 16.5 %copy-start.12 = (bf16[128,1024]{1,0:T(8,128)(2,1)}, bf16[128,1024]{1,0:T(8,128)(2,1)S(1)}, u32[]{:S(2)}) copy-start(bf16[128,1024]{1,0:T(8,128)(2,1)S(1)} %get-tuple-element.67) | copy-start | bytes 786436
  3.6 9.4 %collective-permute-start.1 = (bf16[128,1024]{1,0:T(8,128)(2,1)S(1)}, bf16[128,1024]{1,0:T(8,128)(2,1)}, u32[]{:S(2)}, u32[]{:S(2)}) collective-permute-start(bf16[128,1024]{1,0:T(8,128)(2,1)S(1)} %get-tuple-element.67), channel_id=1, source_target_pairs={{0,1},{1,0},{2,3},{3,2},{4,5},{5,4},{6,7},{7,6},{8,9},{9,8},{10,11... | collective-permute-start | bytes 786440 | tf_op jit(solution)/shard_map/ppermute | solution.py:27
  7.4 10.0 %copy-start.13 = (bf16[64,2048]{1,0:T(8,128)(2,1)S(1)}, bf16[64,2048]{1,0:T(8,128)(2,1)}, u32[]{:S(2)}) copy-start(bf16[64,2048]{1,0:T(8,128)(2,1)} %dynamic-slice_bitcast_fusion) | copy-start | bytes 786436
  7.4 8.5 %collective-permute-start.7 = (bf16[128,1152]{1,0:T(8,128)(2,1)S(1)}, bf16[128,1152]{1,0:T(8,128)(2,1)S(1)}, u32[]{:S(2)}, u32[]{:S(2)}) collective-permute-start(bf16[128,1152]{1,0:T(8,128)(2,1)S(1)} %pad_maximum_fusion.6), channel_id=1, source_target_pairs={{0,2},{1,3},{2,0},{3,1},{4,6},{5,7},{6,4},{7,5},{8,10},{9,11},{10,... | collective-permute-start | bytes 884744 | tf_op jit(solution)/shard_map/ppermute | solution.py:27
  9.1 26.1 %collective-permute-start.4 = (bf16[512,768]{1,0:T(8,128)(2,1)S(1)}, bf16[512,768]{1,0:T(8,128)(2,1)S(1)}, u32[]{:S(2)}, u32[]{:S(2)}) collective-permute-start(bf16[512,768]{1,0:T(8,128)(2,1)S(1)} %slice.68), channel_id=1, source_target_pairs={{0,8},{4,12},{8,0},{12,4},{16,24},{20,28},{24,16},{28,20},{1,9},{5... | collective-permute-start | bytes 2359304 | tf_op jit(solution)/shard_map/ppermute | solution.py:22
  14.0 19.2 %collective-permute-start.2 = (bf16[256,1024]{1,0:T(8,128)(2,1)S(1)}, bf16[256,1024]{1,0:T(8,128)(2,1)S(1)}, u32[]{:S(2)}, u32[]{:S(2)}) collective-permute-start(bf16[256,1024]{1,0:T(8,128)(2,1)S(1)} %pad_maximum_fusion.3), channel_id=1, source_target_pairs={{0,2},{1,3},{2,0},{3,1},{4,6},{5,7},{6,4},{7,5},{8,10},{9,11},{10,... | collective-permute-start | bytes 1572872 | tf_op jit(solution)/shard_map/ppermute | solution.py:27
  16.1 22.7 %collective-permute-start.8 = (bf16[256,1152]{1,0:T(8,128)(2,1)S(1)}, bf16[256,1152]{1,0:T(8,128)(2,1)S(1)}, u32[]{:S(2)}, u32[]{:S(2)}) collective-permute-start(bf16[256,1152]{1,0:T(8,128)(2,1)S(1)} %pad_maximum_fusion.2), channel_id=1, source_target_pairs={{0,1},{1,0},{2,3},{3,2},{4,5},{5,4},{6,7},{7,6},{8,9},{9,8},{10,11... | collective-permute-start | bytes 1769480 | tf_op jit(solution)/shard_map/ppermute | solution.py:27
  17.4 21.4 %copy-start.10 = (bf16[128,1024]{1,0:T(8,128)(2,1)S(1)}, bf16[128,1024]{1,0:T(8,128)(2,1)}, u32[]{:S(2)}) copy-start(bf16[128,1024]{1,0:T(8,128)(2,1)} %copy-done.9) | copy-start | bytes 786436
  17.4 15.2 %collective-permute-start = (bf16[64,2048]{1,0:T(8,128)(2,1)S(1)}, bf16[64,2048]{1,0:T(8,128)(2,1)S(1)}, u32[]{:S(2)}, u32[]{:S(2)}) collective-permute-start(bf16[64,2048]{1,0:T(8,128)(2,1)S(1)} %copy-done.13), channel_id=1, source_target_pairs={{0,16},{4,20},{8,24},{12,28},{16,0},{20,4},{24,8},{28,12},{1,17},{... | collective-permute-start | bytes 786440 | tf_op jit(solution)/shard_map/ppermute | solution.py:22
  20.0 27.6 %collective-permute-start.6 = (bf16[512,2048]{1,0:T(8,128)(2,1)S(1)}, bf16[512,2048]{1,0:T(8,128)(2,1)}, u32[]{:S(2)}, u32[]{:S(2)}) collective-permute-start(bf16[512,2048]{1,0:T(8,128)(2,1)S(1)} %copy-done), channel_id=1, source_target_pairs={{0,4},{4,0},{8,12},{12,8},{16,20},{20,16},{24,28},{28,24},{1,5},{5... | collective-permute-start | bytes 6291464 | tf_op jit(solution)/shard_map/ppermute | solution.py:22
  32.6 7.6 %collective-permute-start.3 = (bf16[64,2048]{1,0:T(8,128)(2,1)S(1)}, bf16[64,2048]{1,0:T(8,128)(2,1)S(1)}, u32[]{:S(2)}, u32[]{:S(2)}) collective-permute-start(bf16[64,2048]{1,0:T(8,128)(2,1)S(1)} %collective-permute-done.refs_0_), channel_id=1, source_target_pairs={{0,1},{1,0},{2,3},{3,2},{4,5},{5,4},{6,7},{7,6},{8,9},{9,8},{10,11... | collective-permute-start | bytes 786440 | tf_op jit(solution)/shard_map/ppermute | solution.py:27
  35.2 8.1 %collective-permute-start.5 = (bf16[512,256]{1,0:T(8,128)(2,1)S(1)}, bf16[512,256]{1,0:T(8,128)(2,1)}, u32[]{:S(2)}, u32[]{:S(2)}) collective-permute-start(bf16[512,256]{1,0:T(8,128)(2,1)S(1)} %slice.69), channel_id=1, source_target_pairs={{0,8},{4,12},{8,0},{12,4},{16,24},{20,28},{24,16},{28,20},{1,9},{5... | collective-permute-start | bytes 786440 | tf_op jit(solution)/shard_map/ppermute | solution.py:22
  38.9 5.6 %copy-start.8 = (bf16[512,1152]{1,0:T(8,128)(2,1)}, bf16[512,1152]{1,0:T(8,128)(2,1)S(1)}, u32[]{:S(2)}) copy-start(bf16[512,1152]{1,0:T(8,128)(2,1)S(1)} %pad_maximum_fusion.refs_1_) | copy-start | bytes 3538948
  40.2 7.4 %collective-permute-start.10 = (bf16[512,1024]{1,0:T(8,128)(2,1)}, bf16[512,1024]{1,0:T(8,128)(2,1)}, u32[]{:S(2)}, u32[]{:S(2)}) collective-permute-start(bf16[512,1024]{1,0:T(8,128)(2,1)} %slice.87), channel_id=1, source_target_pairs={{0,4},{4,0},{8,12},{12,8},{16,20},{20,16},{24,28},{28,24},{1,5},{5... | collective-permute-start | bytes 3145736 | tf_op jit(solution)/shard_map/ppermute | solution.py:22
  43.4 4.8 %collective-permute-start.9 = (bf16[512,1024]{1,0:T(8,128)(2,1)}, bf16[512,1024]{1,0:T(8,128)(2,1)}, u32[]{:S(2)}, u32[]{:S(2)}) collective-permute-start(bf16[512,1024]{1,0:T(8,128)(2,1)} %pad_maximum_fusion.1.refs_0_), channel_id=1, source_target_pairs={{0,4},{4,0},{8,12},{12,8},{16,20},{20,16},{24,28},{28,24},{1,5},{5... | collective-permute-start | bytes 3145736 | tf_op jit(solution)/shard_map/ppermute | solution.py:22
  44.5 31.0 %collective-permute-start.15 = (bf16[512,1024]{1,0:T(8,128)(2,1)}, bf16[512,1024]{1,0:T(8,128)(2,1)}, u32[]{:S(2)}, u32[]{:S(2)}) collective-permute-start(bf16[512,1024]{1,0:T(8,128)(2,1)} %slice.73), channel_id=1, source_target_pairs={{0,8},{4,12},{8,0},{12,4},{16,24},{20,28},{24,16},{28,20},{1,9},{5... | collective-permute-start | bytes 3145736 | tf_op jit(solution)/shard_map/ppermute | solution.py:22
  47.1 23.3 %collective-permute-start.12 = (bf16[128,2048]{1,0:T(8,128)(2,1)S(1)}, bf16[128,2048]{1,0:T(8,128)(2,1)S(1)}, u32[]{:S(2)}, u32[]{:S(2)}) collective-permute-start(bf16[128,2048]{1,0:T(8,128)(2,1)S(1)} %pad_maximum_fusion.4), channel_id=1, source_target_pairs={{0,2},{1,3},{2,0},{3,1},{4,6},{5,7},{6,4},{7,5},{8,10},{9,11},{10,... | collective-permute-start | bytes 1572872 | tf_op jit(solution)/shard_map/ppermute | solution.py:27
  47.6 22.7 %collective-permute-start.13 = (bf16[512,768]{1,0:T(8,128)(2,1)S(1)}, bf16[512,768]{1,0:T(8,128)(2,1)S(1)}, u32[]{:S(2)}, u32[]{:S(2)}) collective-permute-start(bf16[512,768]{1,0:T(8,128)(2,1)S(1)} %collective-permute-done.4.refs_5_), channel_id=1, source_target_pairs={{0,4},{4,0},{8,12},{12,8},{16,20},{20,16},{24,28},{28,24},{1,5},{5... | collective-permute-start | bytes 2359304 | tf_op jit(solution)/shard_map/ppermute | solution.py:22
  47.6 22.7 %collective-permute-start.11 = (bf16[512,256]{1,0:T(8,128)(2,1)}, bf16[512,256]{1,0:T(8,128)(2,1)S(1)}, u32[]{:S(2)}, u32[]{:S(2)}) collective-permute-start(bf16[512,256]{1,0:T(8,128)(2,1)} %collective-permute-done.5.refs_5_), channel_id=1, source_target_pairs={{0,4},{4,0},{8,12},{12,8},{16,20},{20,16},{24,28},{28,24},{1,5},{5... | collective-permute-start | bytes 786440 | tf_op jit(solution)/shard_map/ppermute | solution.py:22
  48.2 22.2 %copy-start.1 = (bf16[1,256,4096]{2,1,0:T(8,128)(2,1)S(1)}, bf16[1,256,4096]{2,1,0:T(8,128)(2,1)}, u32[]{:S(2)}) copy-start(bf16[1,256,4096]{2,1,0:T(8,128)(2,1)} %window.5) | copy-start | bytes 6291460
  74.6 0.9 copy-start.2
  75.5 20.4 %collective-permute-start.16 = (bf16[512,1024]{1,0:T(8,128)(2,1)}, bf16[512,1024]{1,0:T(8,128)(2,1)S(1)}, u32[]{:S(2)}, u32[]{:S(2)}) collective-permute-start(bf16[512,1024]{1,0:T(8,128)(2,1)} %collective-permute-done.15.refs_5_), channel_id=1, source_target_pairs={{0,4},{4,0},{8,12},{12,8},{16,20},{20,16},{24,28},{28,24},{1,5},{5... | collective-permute-start | bytes 3145736 | tf_op jit(solution)/shard_map/ppermute | solution.py:22
  75.5 20.4 %collective-permute-start.14 = (bf16[256,768]{1,0:T(8,128)(2,1)S(1)}, bf16[256,768]{1,0:T(8,128)(2,1)S(1)}, u32[]{:S(2)}, u32[]{:S(2)}) collective-permute-start(bf16[256,768]{1,0:T(8,128)(2,1)S(1)} %get-tuple-element.36), channel_id=1, source_target_pairs={{0,16},{4,20},{8,24},{12,28},{16,0},{20,4},{24,8},{28,12},{1,17},{... | collective-permute-start | bytes 1179656 | tf_op jit(solution)/shard_map/ppermute | solution.py:22
  95.9 2.4 %copy-start.14 = (bf16[512,2048]{1,0:T(8,128)(2,1)S(1)}, bf16[512,2048]{1,0:T(8,128)(2,1)}, u32[]{:S(2)}) copy-start(bf16[512,2048]{1,0:T(8,128)(2,1)} %get-tuple-element.50) | copy-start | bytes 6291460
  98.3 5.1 %collective-permute-start.19 = (bf16[512,2048]{1,0:T(8,128)(2,1)S(1)}, bf16[512,2048]{1,0:T(8,128)(2,1)S(1)}, u32[]{:S(2)}, u32[]{:S(2)}) collective-permute-start(bf16[512,2048]{1,0:T(8,128)(2,1)S(1)} %copy-done.14), channel_id=1, source_target_pairs={{0,4},{4,0},{8,12},{12,8},{16,20},{20,16},{24,28},{28,24},{1,5},{5... | collective-permute-start | bytes 6291464 | tf_op jit(solution)/shard_map/ppermute | solution.py:22
  98.5 5.0 %copy-start.11 = (f32[512,2048]{1,0:T(8,128)S(1)}, f32[512,2048]{1,0:T(8,128)}, u32[]{:S(2)}) copy-start(f32[512,2048]{1,0:T(8,128)} %get-tuple-element.39) | copy-start | bytes 12582916
  104.7 3.3 %copy-start.3 = (f32[256,768]{1,0:T(8,128)S(1)}, f32[256,768]{1,0:T(8,128)}, u32[]{:S(2)}) copy-start(f32[256,768]{1,0:T(8,128)} %copy-done.2) | copy-start | bytes 2359300
  104.7 3.3 %copy-start.4 = (f32[4,2048]{1,0:T(4,128)S(1)}, f32[4,2048]{1,0:T(4,128)}, u32[]{:S(2)}) copy-start(f32[4,2048]{1,0:T(4,128)} %taps.5) | copy-start | bytes 98308
  104.7 3.3 %copy-start.5 = (bf16[1,3,2048]{2,1,0:T(4,128)(2,1)S(1)}, bf16[1,3,2048]{2,1,0:T(4,128)(2,1)}, u32[]{:S(2)}) copy-start(bf16[1,3,2048]{2,1,0:T(4,128)(2,1)} %state.5) | copy-start | bytes 36868
  104.7 3.3 %copy-start.6 = (f32[2048]{0:T(1024)S(1)}, f32[2048]{0:T(1024)}, u32[]{:S(2)}) copy-start(f32[2048]{0:T(1024)} %param.15) | copy-start | bytes 24580
  104.7 3.3 %copy-start.7 = (s32[3]{0:T(128)S(1)}, s32[3]{0:T(128)}, u32[]{:S(2)}) copy-start(s32[3]{0:T(128)} %pad_add_fusion.where) | copy-start | bytes 40
  104.8 14.2 %collective-permute-start.20 = (bf16[256,1024]{1,0:T(8,128)(2,1)S(1)}, bf16[256,1024]{1,0:T(8,128)(2,1)S(1)}, u32[]{:S(2)}, u32[]{:S(2)}) collective-permute-start(bf16[256,1024]{1,0:T(8,128)(2,1)S(1)} %pad_maximum_fusion.5), channel_id=1, source_target_pairs={{0,1},{1,0},{2,3},{3,2},{4,5},{5,4},{6,7},{7,6},{8,9},{9,8},{10,11... | collective-permute-start | bytes 1572872 | tf_op jit(solution)/shard_map/ppermute | solution.py:27
  106.4 14.0 %collective-permute-start.22 = (bf16[256,1024]{1,0:T(8,128)(2,1)S(1)}, bf16[256,1024]{1,0:T(8,128)(2,1)S(1)}, u32[]{:S(2)}, u32[]{:S(2)}) collective-permute-start(bf16[256,1024]{1,0:T(8,128)(2,1)S(1)} %bitcast.40), channel_id=1, source_target_pairs={{0,2},{1,3},{2,0},{3,1},{4,6},{5,7},{6,4},{7,5},{8,10},{9,11},{10,... | collective-permute-start | bytes 1572872 | tf_op jit(solution)/shard_map/ppermute | solution.py:27
  108.0 27.6 %collective-permute-start.18 = (bf16[256,1024]{1,0:T(8,128)(2,1)S(1)}, bf16[256,1024]{1,0:T(8,128)(2,1)S(1)}, u32[]{:S(2)}, u32[]{:S(2)}) collective-permute-start(bf16[256,1024]{1,0:T(8,128)(2,1)S(1)} %get-tuple-element.46), channel_id=1, source_target_pairs={{0,16},{4,20},{8,24},{12,28},{16,0},{20,4},{24,8},{28,12},{1,17},{... | collective-permute-start | bytes 1572872 | tf_op jit(solution)/shard_map/ppermute | solution.py:22
  120.8 14.9 %collective-permute-start.21 = (bf16[128,1024]{1,0:T(8,128)(2,1)S(1)}, bf16[128,1024]{1,0:T(8,128)(2,1)S(1)}, u32[]{:S(2)}, u32[]{:S(2)}) collective-permute-start(bf16[128,1024]{1,0:T(8,128)(2,1)S(1)} %get-tuple-element.63), channel_id=1, source_target_pairs={{0,2},{1,3},{2,0},{3,1},{4,6},{5,7},{6,4},{7,5},{8,10},{9,11},{10,... | collective-permute-start | bytes 786440 | tf_op jit(solution)/shard_map/ppermute | solution.py:27
  122.4 13.3 %collective-permute-start.23 = (bf16[128,1024]{1,0:T(8,128)(2,1)S(1)}, bf16[128,1024]{1,0:T(8,128)(2,1)S(1)}, u32[]{:S(2)}, u32[]{:S(2)}) collective-permute-start(bf16[128,1024]{1,0:T(8,128)(2,1)S(1)} %get-tuple-element.58), channel_id=1, source_target_pairs={{0,1},{1,0},{2,3},{3,2},{4,5},{5,4},{6,7},{7,6},{8,9},{9,8},{10,11... | collective-permute-start | bytes 786440 | tf_op jit(solution)/shard_map/ppermute | solution.py:27
  122.9 20.4 %collective-permute-start.17 = (bf16[256,256]{1,0:T(8,128)(2,1)S(1)}, bf16[256,256]{1,0:T(8,128)(2,1)S(1)}, u32[]{:S(2)}, u32[]{:S(2)}) collective-permute-start(bf16[256,256]{1,0:T(8,128)(2,1)S(1)} %get-tuple-element.43), channel_id=1, source_target_pairs={{0,16},{4,20},{8,24},{12,28},{16,0},{20,4},{24,8},{28,12},{1,17},{... | collective-permute-start | bytes 393224 | tf_op jit(solution)/shard_map/ppermute | solution.py:22
  136.4 8.4 %collective-permute-start.24 = (bf16[128,512]{1,0:T(8,128)(2,1)S(1)}, bf16[128,512]{1,0:T(8,128)(2,1)S(1)}, u32[]{:S(2)}, u32[]{:S(2)}) collective-permute-start(bf16[128,512]{1,0:T(8,128)(2,1)S(1)} %get-tuple-element.55), channel_id=1, source_target_pairs={{0,8},{4,12},{8,0},{12,4},{16,24},{20,28},{24,16},{28,20},{1,9},{5... | collective-permute-start | bytes 393224 | tf_op jit(solution)/shard_map/ppermute | solution.py:22
  136.4 13.0 %collective-permute-start.25 = (bf16[128,512]{1,0:T(8,128)(2,1)S(1)}, bf16[128,512]{1,0:T(8,128)(2,1)S(1)}, u32[]{:S(2)}, u32[]{:S(2)}) collective-permute-start(bf16[128,512]{1,0:T(8,128)(2,1)S(1)} %get-tuple-element.56), channel_id=1, source_target_pairs={{0,16},{4,20},{8,24},{12,28},{16,0},{20,4},{24,8},{28,12},{1,17},{... | collective-permute-start | bytes 393224 | tf_op jit(solution)/shard_map/ppermute | solution.py:22
  139.2 10.2 %collective-permute-start.26 = (bf16[128,512]{1,0:T(8,128)(2,1)S(1)}, bf16[128,512]{1,0:T(8,128)(2,1)S(1)}, u32[]{:S(2)}, u32[]{:S(2)}) collective-permute-start(bf16[128,512]{1,0:T(8,128)(2,1)S(1)} %get-tuple-element.57), channel_id=1, source_target_pairs={{0,24},{4,28},{8,16},{12,20},{16,8},{20,12},{24,0},{28,4},{1,25},{... | collective-permute-start | bytes 393224 | tf_op jit(solution)/shard_map/ppermute | solution.py:22
